TPU v7x, 8 devices: a whole 2x2x1 slice. The times are simulated.
8 devices in a mesh: data: 1 (over z), tp: 8 (over y, x, core).
Axes of the slice: x: 2, y: 2, z: 1, core: 2. Of those that a mesh axis runs over, the one named last changes fastest.
Arguments:
- X: bfloat16 [2048, 4096], P(('data', 'tp'))
- gamma: float32 [4096], replicated
- W1: bfloat16 [4096, 14336], P(None, 'tp')
- W2: bfloat16 [14336, 4096], P('tp')
- dY: bfloat16 [2048, 4096], P(('data', 'tp'))
Outputs:
- output 1: bfloat16 [2048, 4096], P(('data', 'tp'))
- output 2: bfloat16 [2048, 4096], P(('data', 'tp'))
- output 3: float32 [4096, 14336], P('data', 'tp')
- output 4: float32 [14336, 4096], P(('data', 'tp'))
- output 5: float32 [4096], P('data')
All inputs are finite; a program needn't handle non-finite values.
Results may differ from a plain program's by a relative error of at most 0.001.
Values are sent between devices in bfloat16 or wider.
A program may use at most 1 GiB of HBM per device.

v0:
```python
import jax
import jax.numpy as jnp
from jax import lax
from jax.sharding import PartitionSpec as P

EPS = 1e-6


def _gelu(a):
    return jax.nn.gelu(a, approximate=True)


def _ln(x):
    mu = jnp.mean(x, axis=-1, keepdims=True)
    xc = x - mu
    var = jnp.mean(xc * xc, axis=-1, keepdims=True)
    rstd = lax.rsqrt(var + EPS)
    return xc * rstd, rstd


def _tn(a, b):
    return lax.dot_general(a, b, (((0,), (0,)), ((), ())), preferred_element_type=jnp.float32)


def _nt(a, b):
    return lax.dot_general(a, b, (((1,), (1,)), ((), ())), preferred_element_type=jnp.float32)


def solution(mesh):
    rows = P(("data", "tp"), None)

    def body(X, gamma, W1, W2, dY):
        x = X.astype(jnp.float32)
        xhatv, rstd = _ln(x)
        Xn = lax.all_gather((xhatv * gamma).astype(jnp.bfloat16), "tp", axis=0, tiled=True)
        A = jnp.dot(Xn, W1, preferred_element_type=jnp.float32)
        H = _gelu(A).astype(jnp.bfloat16)
        Yp = jnp.dot(H, W2, preferred_element_type=jnp.float32)
        Y = (x + lax.psum_scatter(Yp, "tp", scatter_dimension=0, tiled=True)).astype(jnp.bfloat16)
        g = lax.all_gather(dY, "tp", axis=0, tiled=True)
        dW2 = _tn(H, g)
        dH = _nt(g, W2)
        dA = jax.vjp(_gelu, A)[1](dH)[0].astype(jnp.bfloat16)
        dW1 = _tn(Xn, dA)
        dXn = lax.psum_scatter(_nt(dA, W1), "tp", scatter_dimension=0, tiled=True)
        dgamma = lax.psum(jnp.sum(dXn * xhatv, axis=0), "tp")
        dxhat = dXn * gamma
        dx = rstd * (dxhat - jnp.mean(dxhat, axis=-1, keepdims=True) - xhatv * jnp.mean(dxhat * xhatv, axis=-1, keepdims=True))
        dX = (dY.astype(jnp.float32) + dx).astype(jnp.bfloat16)
        return Y, dX, dW1, dW2, dgamma

    return jax.shard_map(body, mesh=mesh,
                         in_specs=(rows, P(None), P(None, "tp"), P("tp", None), rows),
                         out_specs=(rows, rows, P("data", "tp"), rows, P("data")),
                         check_vma=False)
```

profile of v0, /device:TPU:0, one launch (start us, length us, event | category | flops | bytes accessed | tf_op | source)
XLA Modules:
  0.0 681.9 jit_solution(17909456976730208321)
XLA Ops:
  7.2 0.0 all-gather.5.cloned.1.call-start
  7.2 0.7 all-gather.5.cloned.1.call-update
  7.9 0.0 all-gather.3.cloned.1.call-start
  7.9 2.0 convert_reduce_fusion
  9.9 0.0 copy-start.2
  9.9 2.3 fusion.20
  12.2 0.0 copy-done.2
  12.2 0.0 copy-start.4
  12.2 0.6 copy-done.4
  12.8 3.8 fusion.13
  16.6 0.0 all-gather.3.cloned.1.call-update
  16.6 0.0 reduce-scatter.5.cloned.1.call-start
  16.6 80.1 %all-gather.5.cloned.1.call-done = bf16[2048,4096]{1,0:T(8,128)(2,1)} async-done(((bf16[256,4096]{1,0:T(8,128)(2,1)}), bf16[2048,4096]{1,0:T(8,128)(2,1)}) %all-gather.5.cloned.1.call-update) | async-done | bytes 16777232 | tf_op jit(solution)/shard_map/all_gather | solution.py:40
  96.7 39.4 %fusion.24 = f32[2048,1792]{1,0:T(8,128)} fusion(bf16[2048,4096]{1,0:T(8,128)(2,1)} %all-gather.5.cloned.1.call-done, bf16[1792,4096]{1,0:T(8,128)(2,1)} %param.8), kind=kOutput, calls=%fused_computation.35 | convolution fusion | flops 30064771072 | bytes 46137344 | tf_op jit(solution)/shard_map/dot_general | solution.py:26
  136.1 47.1 %all-gather.3.cloned.1.call-done = bf16[2048,4096]{1,0:T(8,128)(2,1)} async-done(((bf16[256,4096]{1,0:T(8,128)(2,1)}), bf16[2048,4096]{1,0:T(8,128)(2,1)}) %all-gather.3.cloned.1.call-update) | async-done | bytes 16777232 | tf_op jit(solution)/shard_map/all_gather | solution.py:35
  183.2 47.9 %fusion.6 = (bf16[2048,1792]{1,0:T(8,128)(2,1)S(1)}, f32[2048,1792]{1,0:T(8,128)}) fusion(f32[2048,1792]{1,0:T(8,128)} %fusion.24, bf16[2048,4096]{1,0:T(8,128)(2,1)} %all-gather.3.cloned.1.call-done, bf16[4096,1792]{1,0:T(8,128)(2,1)} %param.7), kind=kOutput, calls=%fused_computation.8 | convolution fusion | flops 30138171392 | bytes 68157440 | tf_op jit(solution)/shard_map/dot_general | solution.py:36
  231.1 0.0 copy-start.6
  231.1 3.0 copy-done.6
  234.2 38.2 %fusion.25 = f32[2048,4096]{1,0:T(8,128)} fusion(bf16[2048,1792]{1,0:T(8,128)(2,1)S(1)} %get-tuple-element.10, bf16[4096,1792]{1,0:T(8,128)(2,1)} %param.7), kind=kOutput, calls=%fused_computation.36 | convolution fusion | flops 30064771072 | bytes 55574528 | tf_op jit(solution)/shard_map/dot_general | solution.py:26
  272.4 0.0 reduce-scatter.5.cloned.1.call-update
  272.4 0.0 reduce-scatter.3.cloned.1.call-start
  272.4 41.7 %fusion.23 = f32[2048,4096]{1,0:T(8,128)} fusion(bf16[1792,4096]{1,0:T(8,128)(2,1)} %param.8, f32[2048,1792]{1,0:T(8,128)} %get-tuple-element.11), kind=kOutput, calls=%fused_computation.34 | convolution fusion | flops 30097801216 | bytes 62914560 | tf_op jit(solution)/shard_map/dot_general | solution.py:38
  314.1 0.0 reduce-scatter.3.cloned.1.call-update
  314.1 39.4 %fusion.26 = f32[4096,1792]{1,0:T(8,128)} fusion(bf16[2048,4096]{1,0:T(8,128)(2,1)} %all-gather.3.cloned.1.call-done, bf16[2048,1792]{1,0:T(8,128)(2,1)} %copy-done.6), kind=kOutput, calls=%fused_computation.37 | convolution fusion | flops 30064771072 | bytes 53477376 | tf_op jit(solution)/shard_map/dot_general | solution.py:22
  353.5 0.0 copy-start
  353.5 0.0 copy-start.1
  353.5 0.0 copy-start.3
  353.5 0.0 copy-start.5
  353.5 51.7 %fusion.22 = f32[1792,4096]{1,0:T(8,128)} fusion(bf16[2048,4096]{1,0:T(8,128)(2,1)} %all-gather.5.cloned.1.call-done, f32[2048,1792]{1,0:T(8,128)} %get-tuple-element.11), kind=kOutput, calls=%fused_computation.33 | convolution fusion | flops 30097801216 | bytes 60817408 | tf_op jit(solution)/shard_map/dot_general | solution.py:22
  405.2 63.6 %reduce-scatter.5.cloned.1.call-done = f32[256,4096]{1,0:T(8,128)} async-done(((f32[2048,4096]{1,0:T(8,128)}), f32[256,4096]{1,0:T(8,128)}) %reduce-scatter.5.cloned.1.call-update) | async-done | bytes 4194320 | tf_op jit(solution)/shard_map/reduce_scatter | solution.py:45
  468.8 0.0 copy-done
  468.8 0.0 copy-done.1
  468.8 0.0 copy-done.3
  468.8 0.0 copy-done.5
  468.8 3.9 fusion.19
  472.7 22.3 %psum.7 = f32[4096]{0:T(1024)} all-reduce(f32[4096]{0:T(1024)S(1)} %get-tuple-element.5), channel_id=1, replica_groups=mesh['data'=1,'tp'=8] {'tp'}, use_global_device_ids=true, to_apply=%region_7.0 | all-reduce | flops 4096 | bytes 32768 | tf_op jit(solution)/shard_map/psum | solution.py:46
  495.0 173.4 %reduce-scatter.3.cloned.1.call-done = f32[256,4096]{1,0:T(8,128)} async-done(((f32[2048,4096]{1,0:T(8,128)}), f32[256,4096]{1,0:T(8,128)}) %reduce-scatter.3.cloned.1.call-update) | async-done | bytes 4194320 | tf_op jit(solution)/shard_map/reduce_scatter | solution.py:39
  668.4 6.5 fusion.18
  (3 shorter events, 0.0 us)
Async XLA Ops:
  7.2 89.6 %all-gather.5.cloned.1.call-start = ((), (), s32[]{:S(2)}) async-start(), calls=%async_computation.4 | async-start | bytes 18874368 | tf_op jit(solution)/shard_map/all_gather | solution.py:40
  7.9 175.3 %all-gather.3.cloned.1.call-start = ((), (), s32[]{:S(2)}) async-start(), calls=%async_computation.2 | async-start | bytes 18874368 | tf_op jit(solution)/shard_map/all_gather | solution.py:35
  9.9 2.3 copy-start.2
  12.2 0.6 copy-start.4
  16.6 452.2 %reduce-scatter.5.cloned.1.call-start = ((), (), s32[]{:S(2)}) async-start(), calls=%async_computation.5 | async-start | bytes 37748736 | tf_op jit(solution)/shard_map/reduce_scatter | solution.py:45
  231.1 3.0 copy-start.6
  272.4 396.0 %reduce-scatter.3.cloned.1.call-start = ((), (), s32[]{:S(2)}) async-start(), calls=%async_computation.3 | async-start | bytes 37748736 | tf_op jit(solution)/shard_map/reduce_scatter | solution.py:39
  353.5 115.3 %copy-start = (bf16[256,4096]{1,0:T(8,128)(2,1)S(1)}, bf16[256,4096]{1,0:T(8,128)(2,1)}, u32[]{:S(2)}) copy-start(bf16[256,4096]{1,0:T(8,128)(2,1)} %param.5) | copy-start | bytes 6291460
  353.5 115.3 %copy-start.1 = (f32[4096]{0:T(1024)S(1)}, f32[4096]{0:T(1024)}, u32[]{:S(2)}) copy-start(f32[4096]{0:T(1024)} %param.6) | copy-start | bytes 49156
  353.5 115.3 %copy-start.3 = (f32[256]{0:T(256)S(1)}, f32[256]{0:T(256)}, u32[]{:S(2)}) copy-start(f32[256]{0:T(256)} %copy-done.2) | copy-start | bytes 3076
  353.5 115.3 %copy-start.5 = (f32[256]{0:T(256)S(1)}, f32[256]{0:T(256)}, u32[]{:S(2)}) copy-start(f32[256]{0:T(256)} %copy-done.4) | copy-start | bytes 3076
Sparse Core Ops, SparseCore 0:
  9.8 86.8 all-gather.4
  99.1 84.0 all-gather.2
  272.5 196.2 reduce-scatter.4
  472.1 196.2 reduce-scatter.2
where the time goes:
time: 688 us; the launch traced here: 682 us
  waiting for transfers between devices  365 us (53%)
  matrix products  258 us (38%)
  blocking collectives  22.3 us (3%)
  other arithmetic  18.4 us (3%)
  between operations  14.2 us (2%)
    reduce_scatter x1, waiting for transfers between devices, body(): lax.psum_scatter(Yp, 'tp', scatter_dimension=0, tiled=True)  173 us
    dot_general x2, matrix products, _tn(): lax.dot_general(a, b, (((0,), (0,)), ((), ())), preferred_element_type=jn...  91 us
    all_gather x1, waiting for transfers between devices, body(): g = lax.all_gather(dY, 'tp', axis=0, tiled=True)  80.1 us
    dot_general x2, matrix products, _nt(): lax.dot_general(a, b, (((1,), (1,)), ((), ())), preferred_element_type=jn...  77.6 us
    reduce_scatter x1, waiting for transfers between devices, body(): dXn = lax.psum_scatter(_nt(dA, W1), 'tp', scatter_dimension=0, tiled=True)  63.6 us
    dot_general x1, matrix products, body(): A = jnp.dot(Xn, W1, preferred_element_type=jnp.float32)  47.9 us
    all_gather x1, waiting for transfers between devices, body(): lax.all_gather((xhatv * gamma).astype(jnp.bfloat16), 'tp', axis=0, tiled=...  47.1 us
    dot_general x1, matrix products, body(): Yp = jnp.dot(H, W2, preferred_element_type=jnp.float32)  41.7 us
  transfers between devices with their start and end apart: 4, of which 4 were waited for; matrix products, arithmetic and copies ran while one was open for 27% of the time, Pallas kernels for 0%

commit v1 on v0

v1 whole, which is shorter than its diff:
```python
import jax
import jax.numpy as jnp
from jax import lax
from jax.experimental import pallas as pl
from jax.experimental.pallas import tpu as pltpu
from jax.sharding import PartitionSpec as P


EPS = 1e-6


CORE, XN, YN, DIAG = 1, 2, 4, 6
NN = (((1,), (0,)), ((), ()))
NT = (((1,), (1,)), ((), ()))
ANY = pl.BlockSpec(memory_space=pl.ANY)


C1, C2 = 0.7978845608028654, 0.7978845608028654 * 0.044715


def _gelu(a):
    s = a * a
    q = 0.5 + 0.5 * jnp.tanh(a * (C1 + C2 * s))
    h = a * q
    return h, q + (h - h * q) * (2 * C1 + (6 * C2) * s)


def _ln(x):
    mu = jnp.mean(x, axis=-1, keepdims=True)
    xc = x - mu
    var = jnp.mean(xc * xc, axis=-1, keepdims=True)
    rstd = lax.rsqrt(var + EPS)
    return xc * rstd, rstd


def _tn(a, b):
    return lax.dot_general(a, b, (((0,), (0,)), ((), ())), preferred_element_type=jnp.float32)


def _dot(a, b, dims):
    return lax.dot_general(a, b, dims, preferred_element_type=jnp.float32)


def _swap(v, k):
    return lax.ppermute(v, "tp", [(i, i ^ k) for i in range(8)])


def _cost(m, k, n, extra=0):
    return pl.CostEstimate(flops=2 * m * k * n, bytes_accessed=2 * k * n + 2 * m * k + extra, transcendentals=0)


def _params():
    return pltpu.CompilerParams(dimension_semantics=("arbitrary",), vmem_limit_bytes=60 << 20)


def _fill(pieces, cat):
    if cat is None:
        return pieces[0][...]

    @pl.when(pl.program_id(0) == 0)
    def _():
        at = 0
        for p in pieces:
            cat[at:at + p.shape[0]] = p[...]
            at += p.shape[0]

    return cat[...]


def _up(pieces, weights, dims, slopes=None, after=(), tile=256):
    m, D = sum(p.shape[0] for p in pieces), pieces[0].shape[1]
    nt = dims == NT
    F = weights[0].shape[0 if nt else 1]
    nw, npc, ns = len(weights), len(pieces), len(slopes or ())

    def body(*refs):
        ps, ws, ss = refs[:npc], refs[npc:npc + nw], refs[npc + nw:npc + nw + ns]
        outs = refs[npc + nw + ns + len(after):]
        a = _fill(ps, refs[-1] if npc > 1 else None)
        for i in range(nw):
            r = _dot(a, ws[i][...], dims)
            if slopes:
                outs[i][...] = (ss[i][...] * r).astype(jnp.bfloat16)
            else:
                h, slope = _gelu(r)
                outs[2 * i][...] = h.astype(jnp.bfloat16)
                outs[2 * i + 1][...] = slope

    w_spec = pl.BlockSpec((tile, D), lambda j: (j, 0)) if nt else pl.BlockSpec((D, tile), lambda j: (0, j))
    o_spec = pl.BlockSpec((m, tile), lambda j: (0, j))
    types = [jnp.bfloat16] * nw if slopes else [jnp.bfloat16, jnp.float32] * nw
    return pl.pallas_call(
        body, grid=(F // tile,),
        in_specs=[pl.BlockSpec(p.shape, lambda j: (0, 0)) for p in pieces] + [w_spec] * nw
        + [o_spec] * ns + [ANY] * len(after),
        out_specs=[o_spec] * len(types),
        out_shape=[jax.ShapeDtypeStruct((m, F), t) for t in types],
        scratch_shapes=[pltpu.VMEM((m, D), jnp.bfloat16)] if npc > 1 else [],
        compiler_params=_params(), cost_estimate=_cost(m, D, F * nw),
        name="up_dA" if slopes else "up_A",
    )(*pieces, *weights, *(slopes or ()), *after)


def _down(parts, weights, dims, split=1, after=(), tile=512):
    F = parts[0][0].shape[1]
    m, nb = sum(p.shape[0] for p in parts[0]), len(parts[0])
    ms = [p.shape[0] // split for p in parts[0] for _ in range(split)]
    nt = dims == NT
    D = weights[0].shape[0 if nt else 1]
    n = len(parts)
    half, steps = D // 2, D // tile
    nin = n * nb

    def body(*refs):
        ws, outs = refs[nin:nin + n], refs[nin + n + len(after):]
        cats = outs[2 * len(ms):] or [None] * n
        r = None
        for i in range(n):
            d = _dot(_fill(refs[i * nb:(i + 1) * nb], cats[i]), ws[i][...], dims)
            r = d if r is None else r + d

        for h, on in enumerate((pl.program_id(0) < steps // 2, pl.program_id(0) >= steps // 2)):
            @pl.when(on)
            def _():
                at = 0
                for b, rows in enumerate(ms):
                    outs[2 * b + h][...] = r[at:at + rows]
                    at += rows

    w_spec = pl.BlockSpec((tile, F), lambda j: (j, 0)) if nt else pl.BlockSpec((F, tile), lambda j: (0, j))
    lo = lambda j: (0, jnp.minimum(j, steps // 2 - 1))
    hi = lambda j: (0, jnp.maximum(j - steps // 2, 0))
    blocks = [p for part in parts for p in part]
    out = pl.pallas_call(
        body, grid=(steps,),
        in_specs=[pl.BlockSpec(p.shape, lambda j: (0, 0)) for p in blocks] + [w_spec] * n + [ANY] * len(after),
        out_specs=[pl.BlockSpec((r, tile), f) for r in ms for f in (lo, hi)],
        out_shape=[jax.ShapeDtypeStruct((r, half), jnp.float32) for r in ms for _ in range(2)],
        scratch_shapes=[pltpu.VMEM((m, F), jnp.bfloat16)] * n if nb > 1 else [],
        compiler_params=_params(), cost_estimate=_cost(m, F * n, D, 4 * m * D),
        name="down",
    )(*blocks, *weights, *after)
    return [out[2 * b:2 * b + 2] for b in range(len(ms))]


def _grad(left, right, tile, after=()):
    m, N, M = sum(p.shape[0] for p in left), right[0].shape[1], left[0].shape[1]
    nl, nr = len(left), len(right)

    def body(*refs):
        ls, rs = refs[:nl], refs[nl:nl + nr]
        out, lcat, rcat = refs[-3:]
        at = 0
        for p in ls:
            lcat[at:at + p.shape[0]] = p[...]
            at += p.shape[0]
        _fill(rs, rcat)
        out[...] = _tn(lcat[...], rcat[...])

    return pl.pallas_call(
        body, grid=(M // tile,),
        in_specs=[pl.BlockSpec((p.shape[0], tile), lambda j: (0, j)) for p in left]
        + [pl.BlockSpec(p.shape, lambda j: (0, 0)) for p in right] + [ANY] * len(after),
        out_specs=pl.BlockSpec((tile, N), lambda j: (j, 0)),
        out_shape=jax.ShapeDtypeStruct((M, N), jnp.float32),
        scratch_shapes=[pltpu.VMEM((m, tile), jnp.bfloat16), pltpu.VMEM((m, N), jnp.bfloat16)],
        compiler_params=_params(), cost_estimate=_cost(M, m, N, 4 * M * N),
    )(*left, *right, *after)


def _norm(X, gamma, tile=64):
    def body(x_ref, g_ref, out):
        out[...] = (_ln(x_ref[...].astype(jnp.float32))[0] * g_ref[...]).astype(jnp.bfloat16)

    n, D = X.shape
    spec = pl.BlockSpec((tile, D), lambda j: (j, 0))
    return pl.pallas_call(
        body, grid=(n // tile,), in_specs=[spec, pl.BlockSpec((1, D), lambda j: (0, 0))], out_specs=spec,
        out_shape=jax.ShapeDtypeStruct(X.shape, X.dtype), compiler_params=_params(),
        cost_estimate=pl.CostEstimate(flops=10 * n * D, bytes_accessed=4 * n * D, transcendentals=0), name="norm",
    )(X, gamma[None])


def _finish(base, last, row, whole, n, tile=64):
    def body(*refs):
        out = refs[-1]
        half = out.shape[1] // 2
        for h in range(2):
            out[:, h * half:(h + 1) * half] = (refs[h][...] + refs[2 + h][...]).astype(out.dtype)

    rows, half = last[0].shape
    at = lambda j: (j + row // tile, 0)
    spec = pl.BlockSpec((tile, half), at)
    return pl.pallas_call(
        body, grid=(rows // tile,),
        in_specs=[spec] * 2 + [pl.BlockSpec((tile, half), lambda j: (j, 0))] * 2 + [ANY] * (whole is not None),
        out_specs=pl.BlockSpec((tile, 2 * half), at),
        out_shape=jax.ShapeDtypeStruct((n, 2 * half), jnp.bfloat16),
        input_output_aliases={4: 0} if whole is not None else {}, compiler_params=_params(),
        cost_estimate=pl.CostEstimate(flops=2 * rows * half, bytes_accessed=20 * rows * half, transcendentals=0),
        name="finish",
    )(*base, *last, *([] if whole is None else [whole]))


def _tie(vals, after):
    return lax.optimization_barrier((tuple(vals), tuple(after)))[0]


def _near(v):
    return _swap(v, XN), _swap(v, YN)


def _far(gx, gy):
    h = gx.shape[0] // 2
    sent = gy[:h], gx[h:]
    return _swap(sent[0], XN), _swap(sent[1], YN), sent


def solution(mesh):
    rows = P(("data", "tp"), None)

    def block(X, gamma, W1, W2, dY):
        n, D = X.shape
        W1p = _swap(W1, CORE)
        W2p = _swap(W2, CORE)
        x0 = _norm(X, gamma)
        xx, xy = _near(x0)
        gx, gy = _near(dY)
        Ws1, Ws2 = [W1, W1p], [W2, W2p]

        H0, s0 = _up([x0], [W1], NN)
        H0p, s0p = _up([x0], [W1p], NN, after=(H0,))
        (A0,) = _up([dY], [W2], NT, slopes=(s0,), after=(H0p,))
        (A0p,) = _up([dY], [W2p], NT, slopes=(s0p,), after=(A0,))
        xx, xy = _tie((xx, xy), (A0p,))
        xa, xb, sent = _far(xx, xy)
        Hn, sn, Hnp, snp = _up([xx, xy], Ws1, NN, after=(A0p,) + sent)
        Yx, Yy = _down([[Hn], [Hnp]], Ws2, NN, split=2)
        sa = _swap(Yx[0], XN)
        sb = _swap(Yy[1], YN)
        gx, gy = _tie((gx, gy), (Yx[0],))
        ga, gb, sent = _far(gx, gy)
        An, Anp = _up([gx, gy], Ws2, NT, slopes=(sn, snp), after=(Yx[0],) + sent)
        Zx, Zy = _down([[An], [Anp]], Ws1, NT, split=2)
        ra = _swap(Zx[0], XN)
        rb = _swap(Zy[1], YN)
        Hd, sd, Hdp, sdp = _up([xa, xb], Ws1, NN, after=(Zx[0],))
        Ad, Adp = _up([ga, gb], Ws2, NT, slopes=(sd, sdp))
        Z0, Zd = _down([[A0, Ad], [A0p, Adp]], Ws1, NT)
        fa = _swap(Zd[0], XN)
        fb = _swap(Zd[1], YN)
        Y0, Yd = _down([[H0, Hd], [H0p, Hdp]], Ws2, NN, after=(Zd[0],))
        ya = _swap(Yd[0], XN)
        yb = _swap(Yd[1], YN)
        pair = lambda own, sent: own + [_swap(v, CORE) for v in _tie(sent, (Ad,))]
        dW1 = _grad(pair([x0, xx, xy, xa, xb], [x0, xx, xy, xa, xb]),
                      pair([A0, An, Ad], [A0p, Anp, Adp]), 512, after=(Yd[0],))
        Zx1, Zy0 = _tie((Zx[1], Zy[0]), (dW1,))
        far_a, far_b = Zy0 + fa, Zx1 + fb
        za = _swap(far_a, YN)
        zb = _swap(far_b, XN)
        dW2 = _grad(pair([H0, Hn, Hd], [H0p, Hnp, Hdp]),
                      pair([dY, gx, gy, ga, gb], [dY, gx, gy, ga, gb]), 256, after=(far_a, far_b))
        Yx1, Yy0, Y00, Y01, X = _tie((Yx[1], Yy[0], Y0[0], Y0[1], X), (dW2,))
        far_a, far_b = Yy0 + ya, Yx1 + yb
        q = n - n // 4
        va = _swap(far_a[:q], YN)
        vb = _swap(far_b[:q], XN)
        x = X.astype(jnp.float32)
        base = x[:, :D // 2] + (Y00 + sa), x[:, D // 2:] + (Y01 + sb)
        xhatv, rstd = _ln(x)
        Z00, Z01 = _tie(Z0, base)
        dXn = jnp.concatenate([Z00 + ra + za, Z01 + rb + zb], axis=1)
        dg = jnp.sum(dXn * xhatv, axis=0)
        dg = dg + _swap(dg, CORE)
        dgamma = (dg + _swap(dg, XN)) + (_swap(dg, YN) + _swap(dg, DIAG))
        wa = _swap(far_a[q:], YN)
        wb = _swap(far_b[q:], XN)
        dxhat = dXn * gamma
        dx = rstd * (dxhat - jnp.mean(dxhat, axis=-1, keepdims=True) - xhatv * jnp.mean(dxhat * xhatv, axis=-1, keepdims=True))
        dX = (dY.astype(jnp.float32) + dx).astype(jnp.bfloat16)
        va, vb = _tie((va, vb), (dX,))
        Y = _finish(base, (va, vb), 0, None, n)
        Y = _finish(base, (wa, wb), q, Y, n)
        return Y, dX, dW1, dW2, dgamma

    return jax.shard_map(block, mesh=mesh,
                         in_specs=(rows, P(None), P(None, "tp"), P("tp", None), rows),
                         out_specs=(rows, rows, P("data", "tp"), rows, P("data")),
                         check_vma=False)
```

time: 688 us -> 574 us (0.83)
  Pallas kernels: 0 us -> 316 us
  matrix products: 258 us -> 0 us
  waiting for transfers between devices: 365 us -> 176 us
  starting transfers between devices: 0.16 us -> 36.7 us
  blocking collectives: 22.3 us -> 0 us
  between operations: 14.2 us -> 0.98 us
  local copies, waits for them, and re-layouts: 3.63 us -> 16.4 us
  other arithmetic: 18.4 us -> 27.3 us
    pallas_call x0 -> x17, Pallas kernels: none -> 316 us  [the longest x8 130 us: _up(): pl.pallas_call(body, grid=(F // tile,), in_specs=[pl.BlockSpec(p.shape, l...]
    dot_general x6 -> x0, matrix products: 258 us -> none  [the longest x2 91 us: _tn(): lax.dot_general(a, b, (((0,), (0,)), ((), ())), preferred_element_type=jn...]
    reduce_scatter x2 -> x0, waiting for transfers between devices: 237 us -> none  [the longest x1 173 us: body(): lax.psum_scatter(Yp, 'tp', scatter_dimension=0, tiled=True)]
    ppermute x0 -> x44, waiting for transfers between devices: none -> 176 us  [_swap(): return lax.ppermute(v, 'tp', [(i, i ^ k) for i in range(8)])]
    all_gather x2 -> x0, waiting for transfers between devices: 127 us -> none  [the longest x1 80.1 us: body(): g = lax.all_gather(dY, 'tp', axis=0, tiled=True)]
    ppermute x0 -> x44, starting transfers between devices: none -> 36.7 us  [_swap(): return lax.ppermute(v, 'tp', [(i, i ^ k) for i in range(8)])]
    psum x1 -> x0, blocking collectives: 22.3 us -> none  [body(): dgamma = lax.psum(jnp.sum(dXn * xhatv, axis=0), 'tp')]
    add x0 -> x9, other arithmetic: none -> 20.5 us  [the longest x2 7.22 us: block(): far_a, far_b = (Zy0 + fa, Zx1 + fb)]
  transfers between devices with their start and end apart: 4 -> 44, of which waited for: 4 -> 12; matrix products, arithmetic and copies ran while one was open for 27% -> 7% of each run, Pallas kernels for 0% -> 52%
where the time goes in v1:
time: 574 us; the launch traced here: 573 us
  Pallas kernels  316 us (55%)
  waiting for transfers between devices  176 us (31%)
  starting transfers between devices  36.7 us (6%)
  other arithmetic  27.3 us (5%)
  local copies, waits for them, and re-layouts  16.4 us (3%)
    ppermute x44, waiting for transfers between devices, _swap(): return lax.ppermute(v, 'tp', [(i, i ^ k) for i in range(8)])  176 us
    pallas_call x8, Pallas kernels, _up(): pl.pallas_call(body, grid=(F // tile,), in_specs=[pl.BlockSpec(p.shape, l...  130 us
    pallas_call x4, Pallas kernels, _down(): pl.pallas_call(body, grid=(steps,), in_specs=[pl.BlockSpec(p.shape, lambd...  92.4 us
    pallas_call x2, Pallas kernels, _grad(): pl.pallas_call(body, grid=(M // tile,), in_specs=[pl.BlockSpec((p.shape[0...  82 us
    ppermute x44, starting transfers between devices, _swap(): return lax.ppermute(v, 'tp', [(i, i ^ k) for i in range(8)])  36.7 us
  transfers between devices with their start and end apart: 44, of which 12 were waited for; matrix products, arithmetic and copies ran while one was open for 7% of the time, Pallas kernels for 52%

profile of v1, /device:TPU:0, one launch (start us, length us, event | category | flops | bytes accessed | tf_op | source)
XLA Modules:
  0.0 573.3 jit_solution(16985774096140434665)
XLA Ops:
  0.6 0.9 collective-permute-start.3
  1.5 4.7 norm.1.refs_0_
  6.3 2.9 collective-permute-start
  9.2 1.5 collective-permute-start.1
  11.3 11.5 %up_A.4 = (bf16[256,1792]{1,0:T(8,128)(2,1)}, f32[256,1792]{1,0:T(8,128)}) custom-call(bf16[256,4096]{1,0:T(8,128)(2,1)} %norm.1.refs_0_, bf16[4096,1792]{1,0:T(8,128)(2,1)} %refs_4_.2), custom_call_target="tpu_custom_call" | custom-call | flops 3758096384 | bytes 16777216 | tf_op jit(solution)/shard_map/up_A/pallas_call | solution.py:92
  22.7 0.9 collective-permute-done.3.refs_1_.refs_3_.refs_5_
  23.6 2.9 collective-permute-start.7
  26.5 11.5 %up_A.5 = (bf16[256,1792]{1,0:T(8,128)(2,1)}, f32[256,1792]{1,0:T(8,128)}) custom-call(bf16[256,4096]{1,0:T(8,128)(2,1)} %norm.1.refs_0_, bf16[4096,1792]{1,0:T(8,128)(2,1)} %collective-permute-done.3.refs_1_.refs_3_.refs_5_, bf16[256,1792]{1,0:T(8,128)(2,1)} %get-tuple-element.68.refs_2_.refs_0_), custom_call_target="tpu_custom_call" | custom-call | flops 3758096384 | bytes 16777216 | tf_op jit(solution)/shard_map/up_A/pallas_call | solution.py:92
  38.0 11.7 %up_dA.4.refs_3_.refs_0_.refs_10_ = bf16[256,1792]{1,0:T(8,128)(2,1)} custom-call(bf16[256,4096]{1,0:T(8,128)(2,1)} %refs_6_.1, bf16[1792,4096]{1,0:T(8,128)(2,1)} %refs_4_.3, f32[256,1792]{1,0:T(8,128)} %get-tuple-element.70.refs_2_, bf16[256,1792]{1,0:T(8,128)(2,1)} %get-tuple-element.95.refs_3_.refs_2_), custom_call_target="tpu_custom_call" | custom-call | flops 3758096384 | bytes 16777216 | tf_op jit(solution)/shard_map/up_dA/pallas_call | solution.py:92
  49.7 11.7 %up_dA.5.refs_4_.refs_2_ = bf16[256,1792]{1,0:T(8,128)(2,1)} custom-call(bf16[256,4096]{1,0:T(8,128)(2,1)} %refs_6_.1, bf16[1792,4096]{1,0:T(8,128)(2,1)} %collective-permute-done.2.refs_1_.refs_3_.refs_5_, f32[256,1792]{1,0:T(8,128)} %get-tuple-element.69.refs_2_, bf16[256,1792]{1,0:T(8,128)(2,1)} %up_dA.4.refs_3_.refs_0_.refs_10_), custom_call_target="tpu_custom_call" | custom-call | flops 3758096384 | bytes 16777216 | tf_op jit(solution)/shard_map/up_dA/pallas_call | solution.py:92
  61.4 2.3 slice.30.refs_5_
  63.7 2.3 slice.31.refs_6_
  66.0 1.5 collective-permute-start.4
  68.0 24.2 %up_A.6 = (bf16[512,1792]{1,0:T(8,128)(2,1)}, f32[512,1792]{1,0:T(8,128)}, bf16[512,1792]{1,0:T(8,128)(2,1)}, f32[512,1792]{1,0:T(8,128)}) custom-call(bf16[256,4096]{1,0:T(8,128)(2,1)} %collective-permute-done.refs_0_.refs_1_, bf16[256,4096]{1,0:T(8,128)(2,1)} %collective-permute-done.1.refs_1_.refs_2_, bf16[4096,1792]{1,0:T(8,128)(2,1)} %refs_4_.2, ...), custom_call_target="tpu_custom_call" | custom-call | flops 15032385536 | bytes 33554432 | tf_op jit(solution)/shard_map/up_A/pallas_call | solution.py:92
  92.2 22.7 %down.4 = (f32[256,2048]{1,0:T(8,128)}, f32[256,2048]{1,0:T(8,128)}, f32[256,2048]{1,0:T(8,128)}, f32[256,2048]{1,0:T(8,128)}) custom-call(bf16[512,1792]{1,0:T(8,128)(2,1)} %get-tuple-element.74.refs_0_.refs_1_, bf16[512,1792]{1,0:T(8,128)(2,1)} %get-tuple-element.96.refs_1_, bf16[1792,4096]{1,0:T(8,128)(2,1)} %refs_4_.3, ...), custom_call_target="tpu_custom_call" | custom-call | flops 15032385536 | bytes 41418752 | tf_op jit(solution)/shard_map/down/pallas_call | solution.py:134
  114.9 2.3 slice.32.refs_7_
  117.2 1.3 slice.33.refs_8_
  118.6 2.0 collective-permute-start.9
  120.6 23.6 %up_dA.6 = (bf16[512,1792]{1,0:T(8,128)(2,1)}, bf16[512,1792]{1,0:T(8,128)(2,1)}) custom-call(bf16[256,4096]{1,0:T(8,128)(2,1)} %collective-permute-done.6.refs_0_.refs_7_, bf16[256,4096]{1,0:T(8,128)(2,1)} %collective-permute-done.7.refs_1_.refs_8_, bf16[1792,4096]{1,0:T(8,128)(2,1)} %refs_4_.3, ...), custom_call_target="tpu_custom_call" | custom-call | flops 15032385536 | bytes 33554432 | tf_op jit(solution)/shard_map/up_dA/pallas_call | solution.py:92
  144.2 22.7 %down.5 = (f32[256,2048]{1,0:T(8,128)}, f32[256,2048]{1,0:T(8,128)}, f32[256,2048]{1,0:T(8,128)}, f32[256,2048]{1,0:T(8,128)}) custom-call(bf16[512,1792]{1,0:T(8,128)(2,1)} %get-tuple-element.83.refs_0_.refs_11_, bf16[512,1792]{1,0:T(8,128)(2,1)} %get-tuple-element.111.refs_1_, bf16[4096,1792]{1,0:T(8,128)(2,1)} %refs_4_.2, ...), custom_call_target="tpu_custom_call" | custom-call | flops 15032385536 | bytes 41418752 | tf_op jit(solution)/shard_map/down/pallas_call | solution.py:134
  166.9 17.9 %up_A.7 = (bf16[256,1792]{1,0:T(8,128)(2,1)}, f32[256,1792]{1,0:T(8,128)}, bf16[256,1792]{1,0:T(8,128)(2,1)}, f32[256,1792]{1,0:T(8,128)}) custom-call(bf16[128,4096]{1,0:T(8,128)(2,1)} %collective-permute-done.4.refs_0_.refs_3_, bf16[128,4096]{1,0:T(8,128)(2,1)} %collective-permute-done.5.refs_1_.refs_4_, bf16[4096,1792]{1,0:T(8,128)(2,1)} %refs_4_.2, ...), custom_call_target="tpu_custom_call" | custom-call | flops 7516192768 | bytes 31457280 | tf_op jit(solution)/shard_map/up_A/pallas_call | solution.py:92
  184.8 0.9 copy-done.15
  186.2 17.8 %up_dA.7 = (bf16[256,1792]{1,0:T(8,128)(2,1)}, bf16[256,1792]{1,0:T(8,128)(2,1)}) custom-call(bf16[128,4096]{1,0:T(8,128)(2,1)} %copy-done.15, bf16[128,4096]{1,0:T(8,128)(2,1)} %copy-done.16, bf16[1792,4096]{1,0:T(8,128)(2,1)} %refs_4_.3, bf16[1792,4096]{1,0:T(8,128)(2,1)} %collective-permute-done.2.refs_1_.refs_3_.refs_5_, ...), custom_call_target="tpu_custom_call" | custom-call | flops 7516192768 | bytes 31457280 | tf_op jit(solution)/shard_map/up_dA/pallas_call | solution.py:92
  205.1 1.4 collective-permute-done.23.refs_13_
  206.7 1.2 collective-permute-done.25.refs_15_
  208.0 1.2 collective-permute-done.10.refs_3_
  209.3 0.8 copy-done.26
  210.5 0.9 copy-done.27
  211.6 23.4 %down.6 = (f32[256,2048]{1,0:T(8,128)}, f32[256,2048]{1,0:T(8,128)}, f32[256,2048]{1,0:T(8,128)}, f32[256,2048]{1,0:T(8,128)}) custom-call(bf16[256,1792]{1,0:T(8,128)(2,1)} %up_dA.4.refs_3_.refs_0_.refs_10_, bf16[256,1792]{1,0:T(8,128)(2,1)} %get-tuple-element.90.refs_1_.refs_12_, bf16[256,1792]{1,0:T(8,128)(2,1)} %up_dA.5.refs_4_.refs_2_, ...), custom_call_target="tpu_custom_call" | custom-call | flops 15032385536 | bytes 41418752 | tf_op jit(solution)/shard_map/down/pallas_call | solution.py:134
  236.4 1.5 collective-permute-start.26
  237.9 23.6 %down.7 = (f32[256,2048]{1,0:T(8,128)}, f32[256,2048]{1,0:T(8,128)}, f32[256,2048]{1,0:T(8,128)}, f32[256,2048]{1,0:T(8,128)}) custom-call(bf16[256,1792]{1,0:T(8,128)(2,1)} %get-tuple-element.68.refs_2_.refs_0_, bf16[256,1792]{1,0:T(8,128)(2,1)} %get-tuple-element.86.refs_1_.refs_2_, bf16[256,1792]{1,0:T(8,128)(2,1)} %get-tuple-element.95.refs_3_.refs_2_, ...), custom_call_target="tpu_custom_call" | custom-call | flops 15032385536 | bytes 41418752 | tf_op jit(solution)/shard_map/down/pallas_call | solution.py:134
  262.1 21.8 %collective-permute-done.27 = f32[256,2048]{1,0:T(8,128)} collective-permute-done((f32[256,2048]{1,0:T(8,128)}, f32[256,2048]{1,0:T(8,128)}, u32[]{:S(2)}, u32[]{:S(2)}) %collective-permute-start.27) | collective-permute-done | bytes 2097184 | tf_op jit(solution)/shard_map/ppermute | solution.py:45
  284.1 1.6 collective-permute-start.32
  285.7 39.9 %shard_map.92 = f32[4096,1792]{1,0:T(8,128)} custom-call(bf16[256,4096]{1,0:T(8,128)(2,1)} %norm.1.refs_0_, bf16[256,4096]{1,0:T(8,128)(2,1)} %collective-permute-done.refs_0_.refs_1_, bf16[256,4096]{1,0:T(8,128)(2,1)} %collective-permute-done.1.refs_1_.refs_2_, bf16[128,4096]{1,0:T(8,128)(2,1)} %collective-permute-done.4.refs_0_.refs_3_, ...), custom_call_target="tpu_custom_call" | custom-call | flops 30064771072 | bytes 53477376 | tf_op jit(solution)/shard_map/pallas_call | solution.py:160
  325.6 4.0 add.63.refs_17_
  329.6 3.2 add.62.refs_16_
  332.8 1.5 collective-permute-start.28
  335.3 1.5 collective-permute-start.30
  336.8 1.5 collective-permute-start.37
  338.4 42.1 %shard_map.93 = f32[1792,4096]{1,0:T(8,128)} custom-call(bf16[256,1792]{1,0:T(8,128)(2,1)} %get-tuple-element.68.refs_2_.refs_0_, bf16[512,1792]{1,0:T(8,128)(2,1)} %get-tuple-element.74.refs_0_.refs_1_, bf16[256,1792]{1,0:T(8,128)(2,1)} %get-tuple-element.86.refs_1_.refs_2_, bf16[256,1792]{1,0:T(8,128)(2,1)} %copy-done.26, ...), custom_call_target="tpu_custom_call" | custom-call | flops 30064771072 | bytes 53477376 | tf_op jit(solution)/shard_map/pallas_call | solution.py:160
  380.5 1.8 add.69
  382.5 0.8 slice.43
  383.3 86.2 %collective-permute-done.30 = f32[256,2048]{1,0:T(8,128)} collective-permute-done((f32[256,2048]{1,0:T(8,128)}, f32[256,2048]{1,0:T(8,128)}, u32[]{:S(2)}, u32[]{:S(2)}) %collective-permute-start.30) | collective-permute-done | bytes 2097184 | tf_op jit(solution)/shard_map/ppermute | solution.py:45
  469.5 1.6 collective-permute-start.38
  471.1 1.9 add.68
  473.0 1.3 slice.44
  474.2 0.8 slice.42
  475.6 1.1 copy-done.7
  476.7 1.5 collective-permute-start.39
  478.2 5.5 slice_add_fusion
  483.7 1.3 collective-permute-start.35
  487.4 2.8 add_add_fusion.1
  490.3 27.9 %collective-permute-done.38 = f32[256,2048]{1,0:T(8,128)S(1)} collective-permute-done((f32[256,2048]{1,0:T(8,128)}, f32[256,2048]{1,0:T(8,128)S(1)}, u32[]{:S(2)}, u32[]{:S(2)}) %collective-permute-start.38) | collective-permute-done | bytes 2097184 | tf_op jit(solution)/shard_map/ppermute | solution.py:45
  518.2 1.6 collective-permute-start.31
  519.8 5.4 collective-permute-done.39
  525.8 2.3 multiply_reduce_fusion
  528.1 1.2 collective-permute-done.40
  529.3 1.5 collective-permute-start.41
  530.8 28.2 %collective-permute-done.35.refs_3_ = f32[192,2048]{1,0:T(8,128)S(1)} collective-permute-done((f32[192,2048]{1,0:T(8,128)S(1)}, f32[192,2048]{1,0:T(8,128)S(1)}, u32[]{:S(2)}, u32[]{:S(2)}) %collective-permute-start.35) | collective-permute-done | bytes 1572896 | tf_op jit(solution)/shard_map/ppermute | solution.py:45
  559.4 2.5 collective-permute-start.43
  561.9 3.0 add_convert_fusion
  564.9 4.5 finish.2.refs_4_
  569.5 0.8 copy-done.20
  570.3 2.4 finish.3
  (126 shorter events, 11.5 us)
Async XLA Ops:
  0.6 23.0 %collective-permute-start.3 = (bf16[4096,1792]{1,0:T(8,128)(2,1)}, bf16[4096,1792]{1,0:T(8,128)(2,1)}, u32[]{:S(2)}, u32[]{:S(2)}) collective-permute-start(bf16[4096,1792]{1,0:T(8,128)(2,1)} %refs_4_.2), channel_id=1, source_target_pairs={{0,1},{1,0},{2,3},{3,2},{4,5},{5,4},{6,7},{7,6}} | collective-permute-start | bytes 44040200 | tf_op jit(solution)/shard_map/ppermute | solution.py:45
  1.5 48.2 %collective-permute-start.2 = (bf16[1792,4096]{1,0:T(8,128)(2,1)}, bf16[1792,4096]{1,0:T(8,128)(2,1)}, u32[]{:S(2)}, u32[]{:S(2)}) collective-permute-start(bf16[1792,4096]{1,0:T(8,128)(2,1)} %refs_4_.3), channel_id=1, source_target_pairs={{0,1},{1,0},{2,3},{3,2},{4,5},{5,4},{6,7},{7,6}} | collective-permute-start | bytes 44040200 | tf_op jit(solution)/shard_map/ppermute | solution.py:45
  1.5 9.2 %copy-start.1 = (bf16[256,4096]{1,0:T(8,128)(2,1)S(1)}, bf16[256,4096]{1,0:T(8,128)(2,1)}, u32[]{:S(2)}) copy-start(bf16[256,4096]{1,0:T(8,128)(2,1)} %refs_6_.1) | copy-start | bytes 6291460
  6.3 55.2 %collective-permute-start = (bf16[256,4096]{1,0:T(8,128)(2,1)}, bf16[256,4096]{1,0:T(8,128)(2,1)}, u32[]{:S(2)}, u32[]{:S(2)}) collective-permute-start(bf16[256,4096]{1,0:T(8,128)(2,1)} %norm.1.refs_0_), channel_id=1, source_target_pairs={{0,2},{1,3},{2,0},{3,1},{4,6},{5,7},{6,4},{7,5}} | collective-permute-start | bytes 6291464 | tf_op jit(solution)/shard_map/ppermute | solution.py:45
  9.2 52.2 %collective-permute-start.1 = (bf16[256,4096]{1,0:T(8,128)(2,1)}, bf16[256,4096]{1,0:T(8,128)(2,1)}, u32[]{:S(2)}, u32[]{:S(2)}) collective-permute-start(bf16[256,4096]{1,0:T(8,128)(2,1)} %norm.1.refs_0_), channel_id=1, source_target_pairs={{0,4},{1,5},{2,6},{3,7},{4,0},{5,1},{6,2},{7,3}} | collective-permute-start | bytes 6291464 | tf_op jit(solution)/shard_map/ppermute | solution.py:45
  10.7 104.1 %collective-permute-start.6 = (bf16[256,4096]{1,0:T(8,128)(2,1)S(1)}, bf16[256,4096]{1,0:T(8,128)(2,1)}, u32[]{:S(2)}, u32[]{:S(2)}) collective-permute-start(bf16[256,4096]{1,0:T(8,128)(2,1)S(1)} %copy-done.1), channel_id=1, source_target_pairs={{0,2},{1,3},{2,0},{3,1},{4,6},{5,7},{6,4},{7,5}} | collective-permute-start | bytes 6291464 | tf_op jit(solution)/shard_map/ppermute | solution.py:45
  23.6 91.3 %collective-permute-start.7 = (bf16[256,4096]{1,0:T(8,128)(2,1)S(1)}, bf16[256,4096]{1,0:T(8,128)(2,1)}, u32[]{:S(2)}, u32[]{:S(2)}) collective-permute-start(bf16[256,4096]{1,0:T(8,128)(2,1)S(1)} %copy-done.1), channel_id=1, source_target_pairs={{0,4},{1,5},{2,6},{3,7},{4,0},{5,1},{6,2},{7,3}} | collective-permute-start | bytes 6291464 | tf_op jit(solution)/shard_map/ppermute | solution.py:45
  66.0 100.9 %collective-permute-start.4 = (bf16[128,4096]{1,0:T(8,128)(2,1)}, bf16[128,4096]{1,0:T(8,128)(2,1)}, u32[]{:S(2)}, u32[]{:S(2)}) collective-permute-start(bf16[128,4096]{1,0:T(8,128)(2,1)} %slice.30.refs_5_), channel_id=1, source_target_pairs={{0,2},{1,3},{2,0},{3,1},{4,6},{5,7},{6,4},{7,5}} | collective-permute-start | bytes 3145736 | tf_op jit(solution)/shard_map/ppermute | solution.py:45
  67.5 99.4 %collective-permute-start.5 = (bf16[128,4096]{1,0:T(8,128)(2,1)}, bf16[128,4096]{1,0:T(8,128)(2,1)}, u32[]{:S(2)}, u32[]{:S(2)}) collective-permute-start(bf16[128,4096]{1,0:T(8,128)(2,1)} %slice.31.refs_6_), channel_id=1, source_target_pairs={{0,4},{1,5},{2,6},{3,7},{4,0},{5,1},{6,2},{7,3}} | collective-permute-start | bytes 3145736 | tf_op jit(solution)/shard_map/ppermute | solution.py:45
  118.5 66.3 %collective-permute-start.8 = (bf16[128,4096]{1,0:T(8,128)(2,1)}, bf16[128,4096]{1,0:T(8,128)(2,1)S(1)}, u32[]{:S(2)}, u32[]{:S(2)}) collective-permute-start(bf16[128,4096]{1,0:T(8,128)(2,1)} %slice.32.refs_7_), channel_id=1, source_target_pairs={{0,2},{1,3},{2,0},{3,1},{4,6},{5,7},{6,4},{7,5}} | collective-permute-start | bytes 3145736 | tf_op jit(solution)/shard_map/ppermute | solution.py:45
  118.6 66.3 %collective-permute-start.9 = (bf16[128,4096]{1,0:T(8,128)(2,1)S(1)}, bf16[128,4096]{1,0:T(8,128)(2,1)S(1)}, u32[]{:S(2)}, u32[]{:S(2)}) collective-permute-start(bf16[128,4096]{1,0:T(8,128)(2,1)S(1)} %slice.33.refs_8_), channel_id=1, source_target_pairs={{0,4},{1,5},{2,6},{3,7},{4,0},{5,1},{6,2},{7,3}} | collective-permute-start | bytes 3145736 | tf_op jit(solution)/shard_map/ppermute | solution.py:45
  186.2 17.8 %copy-start.19 = (bf16[256,1792]{1,0:T(8,128)(2,1)S(1)}, bf16[256,1792]{1,0:T(8,128)(2,1)}, u32[]{:S(2)}) copy-start(bf16[256,1792]{1,0:T(8,128)(2,1)} %up_dA.5.refs_4_.refs_2_) | copy-start | bytes 2752516
  186.2 18.4 %copy-start.18 = (bf16[256,1792]{1,0:T(8,128)(2,1)S(1)}, bf16[256,1792]{1,0:T(8,128)(2,1)}, u32[]{:S(2)}) copy-start(bf16[256,1792]{1,0:T(8,128)(2,1)} %get-tuple-element.95.refs_3_.refs_2_) | copy-start | bytes 2752516
  204.1 2.5 collective-permute-start.23
  204.1 3.8 collective-permute-start.25
  204.6 4.6 collective-permute-start.10
  204.6 5.9 %collective-permute-start.12 = (bf16[256,1792]{1,0:T(8,128)(2,1)}, bf16[256,1792]{1,0:T(8,128)(2,1)S(1)}, u32[]{:S(2)}, u32[]{:S(2)}) collective-permute-start(bf16[256,1792]{1,0:T(8,128)(2,1)} %get-tuple-element.97.refs_3_), channel_id=1, source_target_pairs={{0,1},{1,0},{2,3},{3,2},{4,5},{5,4},{6,7},{7,6}} | collective-permute-start | bytes 2752520 | tf_op jit(solution)/shard_map/ppermute | solution.py:45
  205.1 31.3 %collective-permute-start.24 = (bf16[512,1792]{1,0:T(8,128)(2,1)}, bf16[512,1792]{1,0:T(8,128)(2,1)S(1)}, u32[]{:S(2)}, u32[]{:S(2)}) collective-permute-start(bf16[512,1792]{1,0:T(8,128)(2,1)} %get-tuple-element.111.refs_1_), channel_id=1, source_target_pairs={{0,1},{1,0},{2,3},{3,2},{4,5},{5,4},{6,7},{7,6}} | collective-permute-start | bytes 5505032 | tf_op jit(solution)/shard_map/ppermute | solution.py:45
  206.5 3.9 copy-start.28
  206.5 28.4 %collective-permute-start.21 = (bf16[128,4096]{1,0:T(8,128)(2,1)}, bf16[128,4096]{1,0:T(8,128)(2,1)}, u32[]{:S(2)}, u32[]{:S(2)}) collective-permute-start(bf16[128,4096]{1,0:T(8,128)(2,1)} %collective-permute-done.4.refs_0_.refs_3_), channel_id=1, source_target_pairs={{0,1},{1,0},{2,3},{3,2},{4,5},{5,4},{6,7},{7,6}} | collective-permute-start | bytes 3145736 | tf_op jit(solution)/shard_map/ppermute | solution.py:45
  207.9 2.6 copy-start.29
  207.9 27.5 %collective-permute-start.22 = (bf16[128,4096]{1,0:T(8,128)(2,1)}, bf16[128,4096]{1,0:T(8,128)(2,1)}, u32[]{:S(2)}, u32[]{:S(2)}) collective-permute-start(bf16[128,4096]{1,0:T(8,128)(2,1)} %collective-permute-done.5.refs_1_.refs_4_), channel_id=1, source_target_pairs={{0,1},{1,0},{2,3},{3,2},{4,5},{5,4},{6,7},{7,6}} | collective-permute-start | bytes 3145736 | tf_op jit(solution)/shard_map/ppermute | solution.py:45
  209.2 26.4 %collective-permute-start.16 = (bf16[128,4096]{1,0:T(8,128)(2,1)}, bf16[128,4096]{1,0:T(8,128)(2,1)S(1)}, u32[]{:S(2)}, u32[]{:S(2)}) collective-permute-start(bf16[128,4096]{1,0:T(8,128)(2,1)} %copy-done.15), channel_id=1, source_target_pairs={{0,1},{1,0},{2,3},{3,2},{4,5},{5,4},{6,7},{7,6}} | collective-permute-start | bytes 3145736 | tf_op jit(solution)/shard_map/ppermute | solution.py:45
  211.4 24.5 %collective-permute-start.17 = (bf16[128,4096]{1,0:T(8,128)(2,1)}, bf16[128,4096]{1,0:T(8,128)(2,1)S(1)}, u32[]{:S(2)}, u32[]{:S(2)}) collective-permute-start(bf16[128,4096]{1,0:T(8,128)(2,1)} %copy-done.16), channel_id=1, source_target_pairs={{0,1},{1,0},{2,3},{3,2},{4,5},{5,4},{6,7},{7,6}} | collective-permute-start | bytes 3145736 | tf_op jit(solution)/shard_map/ppermute | solution.py:45
  235.0 26.6 %collective-permute-start.18 = (bf16[256,4096]{1,0:T(8,128)(2,1)}, bf16[256,4096]{1,0:T(8,128)(2,1)}, u32[]{:S(2)}, u32[]{:S(2)}) collective-permute-start(bf16[256,4096]{1,0:T(8,128)(2,1)} %norm.1.refs_0_), channel_id=1, source_target_pairs={{0,1},{1,0},{2,3},{3,2},{4,5},{5,4},{6,7},{7,6}} | collective-permute-start | bytes 6291464 | tf_op jit(solution)/shard_map/ppermute | solution.py:45
  235.4 26.2 %collective-permute-start.19 = (bf16[256,4096]{1,0:T(8,128)(2,1)}, bf16[256,4096]{1,0:T(8,128)(2,1)}, u32[]{:S(2)}, u32[]{:S(2)}) collective-permute-start(bf16[256,4096]{1,0:T(8,128)(2,1)} %collective-permute-done.refs_0_.refs_1_), channel_id=1, source_target_pairs={{0,1},{1,0},{2,3},{3,2},{4,5},{5,4},{6,7},{7,6}} | collective-permute-start | bytes 6291464 | tf_op jit(solution)/shard_map/ppermute | solution.py:45
  235.5 2.4 copy-start.24
  235.5 26.6 %collective-permute-start.20 = (bf16[256,4096]{1,0:T(8,128)(2,1)}, bf16[256,4096]{1,0:T(8,128)(2,1)}, u32[]{:S(2)}, u32[]{:S(2)}) collective-permute-start(bf16[256,4096]{1,0:T(8,128)(2,1)} %collective-permute-done.1.refs_1_.refs_2_), channel_id=1, source_target_pairs={{0,1},{1,0},{2,3},{3,2},{4,5},{5,4},{6,7},{7,6}} | collective-permute-start | bytes 6291464 | tf_op jit(solution)/shard_map/ppermute | solution.py:45
  235.9 48.0 %collective-permute-start.27 = (f32[256,2048]{1,0:T(8,128)}, f32[256,2048]{1,0:T(8,128)}, u32[]{:S(2)}, u32[]{:S(2)}) collective-permute-start(f32[256,2048]{1,0:T(8,128)} %get-tuple-element.116), channel_id=1, source_target_pairs={{0,4},{1,5},{2,6},{3,7},{4,0},{5,1},{6,2},{7,3}} | collective-permute-start | bytes 6291464 | tf_op jit(solution)/shard_map/ppermute | solution.py:45
  236.4 47.7 %collective-permute-start.26 = (f32[256,2048]{1,0:T(8,128)}, f32[256,2048]{1,0:T(8,128)}, u32[]{:S(2)}, u32[]{:S(2)}) collective-permute-start(f32[256,2048]{1,0:T(8,128)} %get-tuple-element.92.refs_6_), channel_id=1, source_target_pairs={{0,2},{1,3},{2,0},{3,1},{4,6},{5,7},{6,4},{7,5}} | collective-permute-start | bytes 6291464 | tf_op jit(solution)/shard_map/ppermute | solution.py:45
  237.9 23.6 %copy-start.2 = (bf16[256,4096]{1,0:T(8,128)(2,1)S(1)}, bf16[256,4096]{1,0:T(8,128)(2,1)}, u32[]{:S(2)}) copy-start(bf16[256,4096]{1,0:T(8,128)(2,1)} %refs_6_.1) | copy-start | bytes 6291460
  237.9 46.0 %copy-start.22 = (bf16[512,1792]{1,0:T(8,128)(2,1)S(1)}, bf16[512,1792]{1,0:T(8,128)(2,1)}, u32[]{:S(2)}) copy-start(bf16[512,1792]{1,0:T(8,128)(2,1)} %get-tuple-element.96.refs_1_) | copy-start | bytes 5505028
  261.6 72.7 %collective-permute-start.13 = (bf16[256,4096]{1,0:T(8,128)(2,1)S(1)}, bf16[256,4096]{1,0:T(8,128)(2,1)}, u32[]{:S(2)}, u32[]{:S(2)}) collective-permute-start(bf16[256,4096]{1,0:T(8,128)(2,1)S(1)} %copy-done.2), channel_id=1, source_target_pairs={{0,1},{1,0},{2,3},{3,2},{4,5},{5,4},{6,7},{7,6}} | collective-permute-start | bytes 6291464 | tf_op jit(solution)/shard_map/ppermute | solution.py:45
  261.6 73.2 %collective-permute-start.14 = (bf16[256,4096]{1,0:T(8,128)(2,1)}, bf16[256,4096]{1,0:T(8,128)(2,1)}, u32[]{:S(2)}, u32[]{:S(2)}) collective-permute-start(bf16[256,4096]{1,0:T(8,128)(2,1)} %collective-permute-done.6.refs_0_.refs_7_), channel_id=1, source_target_pairs={{0,1},{1,0},{2,3},{3,2},{4,5},{5,4},{6,7},{7,6}} | collective-permute-start | bytes 6291464 | tf_op jit(solution)/shard_map/ppermute | solution.py:45
  262.1 73.2 %collective-permute-start.15 = (bf16[256,4096]{1,0:T(8,128)(2,1)}, bf16[256,4096]{1,0:T(8,128)(2,1)}, u32[]{:S(2)}, u32[]{:S(2)}) collective-permute-start(bf16[256,4096]{1,0:T(8,128)(2,1)} %collective-permute-done.7.refs_1_.refs_8_), channel_id=1, source_target_pairs={{0,1},{1,0},{2,3},{3,2},{4,5},{5,4},{6,7},{7,6}} | collective-permute-start | bytes 6291464 | tf_op jit(solution)/shard_map/ppermute | solution.py:45
  283.9 48.9 %collective-permute-start.11 = (bf16[512,1792]{1,0:T(8,128)(2,1)S(1)}, bf16[512,1792]{1,0:T(8,128)(2,1)}, u32[]{:S(2)}, u32[]{:S(2)}) collective-permute-start(bf16[512,1792]{1,0:T(8,128)(2,1)S(1)} %copy-done.22), channel_id=1, source_target_pairs={{0,1},{1,0},{2,3},{3,2},{4,5},{5,4},{6,7},{7,6}} | collective-permute-start | bytes 5505032 | tf_op jit(solution)/shard_map/ppermute | solution.py:45
  284.1 52.8 %collective-permute-start.32 = (f32[256,2048]{1,0:T(8,128)}, f32[256,2048]{1,0:T(8,128)}, u32[]{:S(2)}, u32[]{:S(2)}) collective-permute-start(f32[256,2048]{1,0:T(8,128)} %get-tuple-element.123), channel_id=1, source_target_pairs={{0,4},{1,5},{2,6},{3,7},{4,0},{5,1},{6,2},{7,3}} | collective-permute-start | bytes 6291464 | tf_op jit(solution)/shard_map/ppermute | solution.py:45
  325.6 4.0 copy-start.6
  332.8 142.8 %collective-permute-start.28 = (f32[256,2048]{1,0:T(8,128)}, f32[256,2048]{1,0:T(8,128)}, u32[]{:S(2)}, u32[]{:S(2)}) collective-permute-start(f32[256,2048]{1,0:T(8,128)} %get-tuple-element.78.refs_6_), channel_id=1, source_target_pairs={{0,2},{1,3},{2,0},{3,1},{4,6},{5,7},{6,4},{7,5}} | collective-permute-start | bytes 6291464 | tf_op jit(solution)/shard_map/ppermute | solution.py:45
  334.3 151.8 %collective-permute-start.36 = (f32[256,2048]{1,0:T(8,128)}, f32[256,2048]{1,0:T(8,128)}, u32[]{:S(2)}, u32[]{:S(2)}) collective-permute-start(f32[256,2048]{1,0:T(8,128)} %get-tuple-element.85.refs_4_), channel_id=1, source_target_pairs={{0,2},{1,3},{2,0},{3,1},{4,6},{5,7},{6,4},{7,5}} | collective-permute-start | bytes 6291464 | tf_op jit(solution)/shard_map/ppermute | solution.py:45
  334.8 45.6 %copy-start.5 = (f32[256,2048]{1,0:T(8,128)S(1)}, f32[256,2048]{1,0:T(8,128)}, u32[]{:S(2)}) copy-start(f32[256,2048]{1,0:T(8,128)} %get-tuple-element.122) | copy-start | bytes 6291460
  334.8 143.3 %collective-permute-start.29 = (f32[256,2048]{1,0:T(8,128)}, f32[256,2048]{1,0:T(8,128)}, u32[]{:S(2)}, u32[]{:S(2)}) collective-permute-start(f32[256,2048]{1,0:T(8,128)} %get-tuple-element.120), channel_id=1, source_target_pairs={{0,4},{1,5},{2,6},{3,7},{4,0},{5,1},{6,2},{7,3}} | collective-permute-start | bytes 6291464 | tf_op jit(solution)/shard_map/ppermute | solution.py:45
  335.3 134.2 %collective-permute-start.30 = (f32[256,2048]{1,0:T(8,128)}, f32[256,2048]{1,0:T(8,128)}, u32[]{:S(2)}, u32[]{:S(2)}) collective-permute-start(f32[256,2048]{1,0:T(8,128)} %get-tuple-element.113.refs_16_), channel_id=1, source_target_pairs={{0,2},{1,3},{2,0},{3,1},{4,6},{5,7},{6,4},{7,5}} | collective-permute-start | bytes 6291464 | tf_op jit(solution)/shard_map/ppermute | solution.py:45
  336.8 149.8 %collective-permute-start.37 = (f32[256,2048]{1,0:T(8,128)}, f32[256,2048]{1,0:T(8,128)}, u32[]{:S(2)}, u32[]{:S(2)}) collective-permute-start(f32[256,2048]{1,0:T(8,128)} %add.62.refs_16_), channel_id=1, source_target_pairs={{0,4},{1,5},{2,6},{3,7},{4,0},{5,1},{6,2},{7,3}} | collective-permute-start | bytes 6291464 | tf_op jit(solution)/shard_map/ppermute | solution.py:45
  382.3 88.7 %copy-start.4 = (f32[256,2048]{1,0:T(8,128)S(1)}, f32[256,2048]{1,0:T(8,128)}, u32[]{:S(2)}) copy-start(f32[256,2048]{1,0:T(8,128)} %get-tuple-element.121) | copy-start | bytes 6291460
  469.5 48.7 %collective-permute-start.38 = (f32[256,2048]{1,0:T(8,128)}, f32[256,2048]{1,0:T(8,128)S(1)}, u32[]{:S(2)}, u32[]{:S(2)}) collective-permute-start(f32[256,2048]{1,0:T(8,128)} %get-tuple-element.128), channel_id=1, source_target_pairs={{0,4},{1,5},{2,6},{3,7},{4,0},{5,1},{6,2},{7,3}} | collective-permute-start | bytes 6291464 | tf_op jit(solution)/shard_map/ppermute | solution.py:45
  475.1 3.1 copy-start.10
  475.1 3.1 copy-start.11
  476.7 48.5 %collective-permute-start.39 = (f32[256,2048]{1,0:T(8,128)S(1)}, f32[256,2048]{1,0:T(8,128)S(1)}, u32[]{:S(2)}, u32[]{:S(2)}) collective-permute-start(f32[256,2048]{1,0:T(8,128)S(1)} %copy-done.7), channel_id=1, source_target_pairs={{0,2},{1,3},{2,0},{3,1},{4,6},{5,7},{6,4},{7,5}} | collective-permute-start | bytes 6291464 | tf_op jit(solution)/shard_map/ppermute | solution.py:45
  483.7 2.4 copy-start.14
  483.7 3.7 copy-start.9
  483.7 75.2 %collective-permute-start.35 = (f32[192,2048]{1,0:T(8,128)S(1)}, f32[192,2048]{1,0:T(8,128)S(1)}, u32[]{:S(2)}, u32[]{:S(2)}) collective-permute-start(f32[192,2048]{1,0:T(8,128)S(1)} %slice.45), channel_id=1, source_target_pairs={{0,2},{1,3},{2,0},{3,1},{4,6},{5,7},{6,4},{7,5}} | collective-permute-start | bytes 4718600 | tf_op jit(solution)/shard_map/ppermute | solution.py:45
  486.1 39.1 %copy-start.8 = (f32[256,2048]{1,0:T(8,128)S(1)}, f32[256,2048]{1,0:T(8,128)}, u32[]{:S(2)}) copy-start(f32[256,2048]{1,0:T(8,128)} %get-tuple-element.127) | copy-start | bytes 6291460
  486.1 73.3 %collective-permute-start.34 = (f32[192,2048]{1,0:T(8,128)S(1)}, f32[192,2048]{1,0:T(8,128)S(1)}, u32[]{:S(2)}, u32[]{:S(2)}) collective-permute-start(f32[192,2048]{1,0:T(8,128)S(1)} %copy-done.14), channel_id=1, source_target_pairs={{0,4},{1,5},{2,6},{3,7},{4,0},{5,1},{6,2},{7,3}} | collective-permute-start | bytes 4718600 | tf_op jit(solution)/shard_map/ppermute | solution.py:45
  486.6 82.8 %collective-permute-start.33 = (f32[64,2048]{1,0:T(8,128)}, f32[64,2048]{1,0:T(8,128)S(1)}, u32[]{:S(2)}, u32[]{:S(2)}) collective-permute-start(f32[64,2048]{1,0:T(8,128)} %slice.43), channel_id=1, source_target_pairs={{0,2},{1,3},{2,0},{3,1},{4,6},{5,7},{6,4},{7,5}} | collective-permute-start | bytes 1572872 | tf_op jit(solution)/shard_map/ppermute | solution.py:45
  490.2 35.5 %copy-start.21 = (f32[4096]{0:T(1024)S(1)}, f32[4096]{0:T(1024)}, u32[]{:S(2)}) copy-start(f32[4096]{0:T(1024)} %param.6) | copy-start | bytes 49156
  518.2 51.3 %collective-permute-start.31 = (f32[64,2048]{1,0:T(8,128)}, f32[64,2048]{1,0:T(8,128)}, u32[]{:S(2)}, u32[]{:S(2)}) collective-permute-start(f32[64,2048]{1,0:T(8,128)} %slice.42), channel_id=1, source_target_pairs={{0,4},{1,5},{2,6},{3,7},{4,0},{5,1},{6,2},{7,3}} | collective-permute-start | bytes 1572872 | tf_op jit(solution)/shard_map/ppermute | solution.py:45
  525.8 36.1 %copy-start.3 = (bf16[256,4096]{1,0:T(8,128)(2,1)S(1)}, bf16[256,4096]{1,0:T(8,128)(2,1)}, u32[]{:S(2)}) copy-start(bf16[256,4096]{1,0:T(8,128)(2,1)} %refs_6_.1) | copy-start | bytes 6291460
  528.1 1.2 collective-permute-start.40
  529.3 43.4 %collective-permute-start.41 = (f32[4096]{0:T(1024)S(1)}, f32[4096]{0:T(1024)S(1)}, u32[]{:S(2)}, u32[]{:S(2)}) collective-permute-start(f32[4096]{0:T(1024)S(1)} %add.77), channel_id=1, source_target_pairs={{0,2},{1,3},{2,0},{3,1},{4,6},{5,7},{6,4},{7,5}} | collective-permute-start | bytes 49160 | tf_op jit(solution)/shard_map/ppermute | solution.py:45
  558.9 6.0 %copy-start.12 = (f32[192,2048]{1,0:T(8,128)}, f32[192,2048]{1,0:T(8,128)S(1)}, u32[]{:S(2)}) copy-start(f32[192,2048]{1,0:T(8,128)S(1)} %collective-permute-done.35.refs_3_) | copy-start | bytes 4718596
  558.9 13.8 %collective-permute-start.42 = (f32[4096]{0:T(1024)S(1)}, f32[4096]{0:T(1024)S(1)}, u32[]{:S(2)}, u32[]{:S(2)}) collective-permute-start(f32[4096]{0:T(1024)S(1)} %add.77), channel_id=1, source_target_pairs={{0,4},{1,5},{2,6},{3,7},{4,0},{5,1},{6,2},{7,3}} | collective-permute-start | bytes 49160 | tf_op jit(solution)/shard_map/ppermute | solution.py:45
  559.4 5.5 copy-start.13
  559.4 13.3 %collective-permute-start.43 = (f32[4096]{0:T(1024)S(1)}, f32[4096]{0:T(1024)S(1)}, u32[]{:S(2)}, u32[]{:S(2)}) collective-permute-start(f32[4096]{0:T(1024)S(1)} %add.77), channel_id=1, source_target_pairs={{0,6},{1,7},{2,4},{3,5},{4,2},{5,3},{6,0},{7,1}} | collective-permute-start | bytes 49160 | tf_op jit(solution)/shard_map/ppermute | solution.py:45
  (10 other events, 14.4 us)

commit v2 on v1

--- a/solution.py
+++ b/solution.py
@@ -67,16 +67,36 @@
     return cat[...]
 
 
-def _up(pieces, weights, dims, slopes=None, after=(), tile=256):
+def _norm(pieces, gamma, out, chunk=32):
+    at = 0
+    for p in pieces:
+        def rows(i, _, p=p, at=at):
+            r = pl.multiple_of(i * chunk, chunk)
+            xhatv, _ = _ln(p[pl.ds(r, chunk)].astype(jnp.float32))
+            out[pl.ds(at + r, chunk)] = (xhatv * gamma[...]).astype(out.dtype)
+            return 0
+
+        lax.fori_loop(0, p.shape[0] // chunk, rows, 0)
+        at += p.shape[0]
+
+
+def _up(pieces, weights, dims, slopes=None, gamma=None, after=(), tile=256):
     m, D = sum(p.shape[0] for p in pieces), pieces[0].shape[1]
     nt = dims == NT
     F = weights[0].shape[0 if nt else 1]
-    nw, npc, ns = len(weights), len(pieces), len(slopes or ())
+    nw, npc, ns, nx = len(weights), len(pieces), len(slopes or ()), int(gamma is not None)
 
     def body(*refs):
         ps, ws, ss = refs[:npc], refs[npc:npc + nw], refs[npc + nw:npc + nw + ns]
-        outs = refs[npc + nw + ns + len(after):]
-        a = _fill(ps, refs[-1] if npc > 1 else None)
+        outs = refs[npc + nw + ns + nx + len(after):]
+        if nx:
+            @pl.when(pl.program_id(0) == 0)
+            def _():
+                _norm(ps, refs[npc + nw + ns], outs[-1])
+
+            a = outs[-1][...]
+        else:
+            a = _fill(ps, refs[-1] if npc > 1 else None)
         for i in range(nw):
             r = _dot(a, ws[i][...], dims)
             if slopes:
@@ -92,13 +112,13 @@
     return pl.pallas_call(
         body, grid=(F // tile,),
         in_specs=[pl.BlockSpec(p.shape, lambda j: (0, 0)) for p in pieces] + [w_spec] * nw
-        + [o_spec] * ns + [ANY] * len(after),
-        out_specs=[o_spec] * len(types),
-        out_shape=[jax.ShapeDtypeStruct((m, F), t) for t in types],
-        scratch_shapes=[pltpu.VMEM((m, D), jnp.bfloat16)] if npc > 1 else [],
+        + [o_spec] * ns + [pl.BlockSpec((1, D), lambda j: (0, 0))] * nx + [ANY] * len(after),
+        out_specs=[o_spec] * len(types) + [pl.BlockSpec((m, D), lambda j: (0, 0))] * nx,
+        out_shape=[jax.ShapeDtypeStruct((m, F), t) for t in types] + [jax.ShapeDtypeStruct((m, D), jnp.bfloat16)] * nx,
+        scratch_shapes=[pltpu.VMEM((m, D), jnp.bfloat16)] if npc > 1 and not nx else [],
         compiler_params=_params(), cost_estimate=_cost(m, D, F * nw),
         name="up_dA" if slopes else "up_A",
-    )(*pieces, *weights, *(slopes or ()), *after)
+    )(*pieces, *weights, *(slopes or ()), *([gamma[None]] if nx else []), *after)
 
 
 def _down(parts, weights, dims, split=1, after=(), tile=512):
@@ -168,20 +188,7 @@
     )(*left, *right, *after)
 
 
-def _norm(X, gamma, tile=64):
-    def body(x_ref, g_ref, out):
-        out[...] = (_ln(x_ref[...].astype(jnp.float32))[0] * g_ref[...]).astype(jnp.bfloat16)
-
-    n, D = X.shape
-    spec = pl.BlockSpec((tile, D), lambda j: (j, 0))
-    return pl.pallas_call(
-        body, grid=(n // tile,), in_specs=[spec, pl.BlockSpec((1, D), lambda j: (0, 0))], out_specs=spec,
-        out_shape=jax.ShapeDtypeStruct(X.shape, X.dtype), compiler_params=_params(),
-        cost_estimate=pl.CostEstimate(flops=10 * n * D, bytes_accessed=4 * n * D, transcendentals=0), name="norm",
-    )(X, gamma[None])
-
-
-def _finish(base, last, row, whole, n, tile=64):
+def _finish(base, last, row, whole, n, tile):
     def body(*refs):
         out = refs[-1]
         half = out.shape[1] // 2
@@ -210,67 +217,60 @@
     return _swap(v, XN), _swap(v, YN)
 
 
-def _far(gx, gy):
-    h = gx.shape[0] // 2
-    sent = gy[:h], gx[h:]
-    return _swap(sent[0], XN), _swap(sent[1], YN), sent
-
-
 def solution(mesh):
     rows = P(("data", "tp"), None)
 
     def block(X, gamma, W1, W2, dY):
         n, D = X.shape
+        xx, xy = _near(X)
+        gx, gy = _near(dY)
         W1p = _swap(W1, CORE)
         W2p = _swap(W2, CORE)
-        x0 = _norm(X, gamma)
-        xx, xy = _near(x0)
-        gx, gy = _near(dY)
         Ws1, Ws2 = [W1, W1p], [W2, W2p]
 
-        H0, s0 = _up([x0], [W1], NN)
-        H0p, s0p = _up([x0], [W1p], NN, after=(H0,))
-        (A0,) = _up([dY], [W2], NT, slopes=(s0,), after=(H0p,))
-        (A0p,) = _up([dY], [W2p], NT, slopes=(s0p,), after=(A0,))
-        xx, xy = _tie((xx, xy), (A0p,))
-        xa, xb, sent = _far(xx, xy)
-        Hn, sn, Hnp, snp = _up([xx, xy], Ws1, NN, after=(A0p,) + sent)
-        Yx, Yy = _down([[Hn], [Hnp]], Ws2, NN, split=2)
+        H0, s0, X0 = _up([X], [W1], NN, gamma=gamma)
+        (A0,) = _up([dY], [W2], NT, slopes=(s0,))
+        H0p, s0p, _ = _up([X], [W1p], NN, gamma=gamma, after=(A0,))
+        xx, xy = _tie((xx, xy), (H0p,))
+        xd = _swap(xy, XN)
+        Hn, sn, Hnp, snp, Xn = _up([xx, xy], Ws1, NN, gamma=gamma, after=(H0p,))
+        (A0p,) = _up([dY], [W2p], NT, slopes=(s0p,), after=(Hn,))
+        gx, gy = _tie((gx, gy), (A0p,))
+        gd = _swap(gx, YN)
+        Yx, Yy = _down([[Hn], [Hnp]], Ws2, NN, split=2, after=(A0p,))
         sa = _swap(Yx[0], XN)
         sb = _swap(Yy[1], YN)
-        gx, gy = _tie((gx, gy), (Yx[0],))
-        ga, gb, sent = _far(gx, gy)
-        An, Anp = _up([gx, gy], Ws2, NT, slopes=(sn, snp), after=(Yx[0],) + sent)
+        An, Anp = _up([gx, gy], Ws2, NT, slopes=(sn, snp), after=(Yx[0],))
         Zx, Zy = _down([[An], [Anp]], Ws1, NT, split=2)
         ra = _swap(Zx[0], XN)
         rb = _swap(Zy[1], YN)
-        Hd, sd, Hdp, sdp = _up([xa, xb], Ws1, NN, after=(Zx[0],))
-        Ad, Adp = _up([ga, gb], Ws2, NT, slopes=(sd, sdp))
-        Z0, Zd = _down([[A0, Ad], [A0p, Adp]], Ws1, NT)
+        Hd, sd, Hdp, sdp, Xd = _up([xd], Ws1, NN, gamma=gamma, after=(Zx[0],))
+        Ad, Adp = _up([gd], Ws2, NT, slopes=(sd, sdp))
+        (Zd,) = _down([[Ad], [Adp]], Ws1, NT)
         fa = _swap(Zd[0], XN)
         fb = _swap(Zd[1], YN)
         Y0, Yd = _down([[H0, Hd], [H0p, Hdp]], Ws2, NN, after=(Zd[0],))
         ya = _swap(Yd[0], XN)
         yb = _swap(Yd[1], YN)
         pair = lambda own, sent: own + [_swap(v, CORE) for v in _tie(sent, (Ad,))]
-        dW1 = _grad(pair([x0, xx, xy, xa, xb], [x0, xx, xy, xa, xb]),
+        dW1 = _grad(pair([X0, Xn, Xd], [X0, Xn, Xd]),
                       pair([A0, An, Ad], [A0p, Anp, Adp]), 512, after=(Yd[0],))
         Zx1, Zy0 = _tie((Zx[1], Zy[0]), (dW1,))
         far_a, far_b = Zy0 + fa, Zx1 + fb
         za = _swap(far_a, YN)
         zb = _swap(far_b, XN)
         dW2 = _grad(pair([H0, Hn, Hd], [H0p, Hnp, Hdp]),
-                      pair([dY, gx, gy, ga, gb], [dY, gx, gy, ga, gb]), 256, after=(far_a, far_b))
+                      pair([dY, gx, gy, gd], [dY, gx, gy, gd]), 256, after=(far_a, far_b))
         Yx1, Yy0, Y00, Y01, X = _tie((Yx[1], Yy[0], Y0[0], Y0[1], X), (dW2,))
         far_a, far_b = Yy0 + ya, Yx1 + yb
-        q = n - n // 4
+        q = n - n // 8
         va = _swap(far_a[:q], YN)
         vb = _swap(far_b[:q], XN)
         x = X.astype(jnp.float32)
         base = x[:, :D // 2] + (Y00 + sa), x[:, D // 2:] + (Y01 + sb)
         xhatv, rstd = _ln(x)
-        Z00, Z01 = _tie(Z0, base)
-        dXn = jnp.concatenate([Z00 + ra + za, Z01 + rb + zb], axis=1)
+        (Z0,) = _down([[A0], [A0p]], Ws1, NT, after=base)
+        dXn = jnp.concatenate([Z0[0] + ra + za, Z0[1] + rb + zb], axis=1)
         dg = jnp.sum(dXn * xhatv, axis=0)
         dg = dg + _swap(dg, CORE)
         dgamma = (dg + _swap(dg, XN)) + (_swap(dg, YN) + _swap(dg, DIAG))
@@ -280,8 +280,8 @@
         dx = rstd * (dxhat - jnp.mean(dxhat, axis=-1, keepdims=True) - xhatv * jnp.mean(dxhat * xhatv, axis=-1, keepdims=True))
         dX = (dY.astype(jnp.float32) + dx).astype(jnp.bfloat16)
         va, vb = _tie((va, vb), (dX,))
-        Y = _finish(base, (va, vb), 0, None, n)
-        Y = _finish(base, (wa, wb), q, Y, n)
+        Y = _finish(base, (va, vb), 0, None, n, q // 2)
+        Y = _finish(base, (wa, wb), q, Y, n, n - q)
         return Y, dX, dW1, dW2, dgamma
 
     return jax.shard_map(block, mesh=mesh,

time: 574 us -> 575 us (level)
  Pallas kernels: 316 us -> 334 us
  local copies, waits for them, and re-layouts: 16.4 us -> 7.63 us
  starting transfers between devices: 36.7 us -> 29.1 us
    pallas_call x8, Pallas kernels: 130 us -> 143 us  [_up(): pl.pallas_call(body, grid=(F // tile,), in_specs=[pl.BlockSpec(p.shape, l...]
    pallas_call x4 -> x5, Pallas kernels: 92.4 us -> 102 us  [_down(): pl.pallas_call(body, grid=(steps,), in_specs=[pl.BlockSpec(p.shape, lambd...]
    slice x4 -> x0, local copies, waits for them, and re-layouts: 8.2 us -> none  [_far(): sent = (gy[:h], gx[h:])]
    ppermute x44 -> x39, starting transfers between devices: 36.7 us -> 29.1 us  [_swap(): return lax.ppermute(v, 'tp', [(i, i ^ k) for i in range(8)])]
    ppermute x44 -> x39, waiting for transfers between devices: 176 us -> 173 us  [_swap(): return lax.ppermute(v, 'tp', [(i, i ^ k) for i in range(8)])]
  transfers between devices with their start and end apart: 44 -> 39, of which waited for: 12 -> 13; matrix products, arithmetic and copies ran while one was open for 7% -> 6% of each run, Pallas kernels for 52% -> 55%
where the time goes in v2:
time: 575 us
  Pallas kernels  334 us (58%)
  waiting for transfers between devices  173 us (30%)
  other arithmetic  30.1 us (5%)
  starting transfers between devices  29.1 us (5%)
  local copies, waits for them, and re-layouts  7.63 us (1%)
    ppermute x39, waiting for transfers between devices, _swap(): return lax.ppermute(v, 'tp', [(i, i ^ k) for i in range(8)])  173 us
    pallas_call x8, Pallas kernels, _up(): pl.pallas_call(body, grid=(F // tile,), in_specs=[pl.BlockSpec(p.shape, l...  143 us
    pallas_call x5, Pallas kernels, _down(): pl.pallas_call(body, grid=(steps,), in_specs=[pl.BlockSpec(p.shape, lambd...  102 us
    pallas_call x2, Pallas kernels, _grad(): pl.pallas_call(body, grid=(M // tile,), in_specs=[pl.BlockSpec((p.shape[0...  82 us
    ppermute x39, starting transfers between devices, _swap(): return lax.ppermute(v, 'tp', [(i, i ^ k) for i in range(8)])  29.1 us
  transfers between devices with their start and end apart: 39, of which 13 were waited for; matrix products, arithmetic and copies ran while one was open for 6% of the time, Pallas kernels for 55%

profile of v2, /device:TPU:0, one launch (start us, length us, event | category | flops | bytes accessed | tf_op | source)
XLA Modules:
  0.0 574.7 jit_solution(2610721369020051676)
XLA Ops:
  0.6 0.9 collective-permute-start.2
  1.5 2.9 collective-permute-start
  4.5 1.5 collective-permute-start.1
  6.5 14.1 %up_A.4 = (bf16[256,1792]{1,0:T(8,128)(2,1)}, f32[256,1792]{1,0:T(8,128)}, bf16[256,4096]{1,0:T(8,128)(2,1)}) custom-call(bf16[256,4096]{1,0:T(8,128)(2,1)} %refs_0_.6, bf16[4096,1792]{1,0:T(8,128)(2,1)} %refs_2_.11, f32[1,4096]{1,0:T(1,128)} %bitcast.1), custom_call_target="tpu_custom_call" | custom-call | flops 3758096384 | bytes 16777216 | tf_op jit(solution)/shard_map/up_A/pallas_call | solution.py:112
  20.6 11.9 %up_dA.4.refs_3_.refs_6_.refs_0_ = bf16[256,1792]{1,0:T(8,128)(2,1)} custom-call(bf16[256,4096]{1,0:T(8,128)(2,1)} %refs_6_.1, bf16[1792,4096]{1,0:T(8,128)(2,1)} %refs_4_.1, f32[256,1792]{1,0:T(8,128)} %get-tuple-element.66.refs_2_), custom_call_target="tpu_custom_call" | custom-call | flops 3758096384 | bytes 16777216 | tf_op jit(solution)/shard_map/up_dA/pallas_call | solution.py:112
  32.5 14.1 %up_A.5 = (bf16[256,1792]{1,0:T(8,128)(2,1)}, f32[256,1792]{1,0:T(8,128)}, bf16[256,4096]{1,0:T(8,128)(2,1)}) custom-call(bf16[256,4096]{1,0:T(8,128)(2,1)} %refs_0_.6, bf16[4096,1792]{1,0:T(8,128)(2,1)} %collective-permute-done.2.refs_1_.refs_3_.refs_2_, f32[1,4096]{1,0:T(1,128)} %bitcast.2, bf16[256,1792]{1,0:T(8,128)(2,1)} %up_dA.4.refs_3_.refs_6_.refs_0_), custom_call_target="tpu_custom_call" | custom-call | flops 3758096384 | bytes 16777216 | tf_op jit(solution)/shard_map/up_A/pallas_call | solution.py:112
  46.6 4.7 collective-permute-done.refs_0_
  51.3 2.0 collective-permute-done.1.refs_1_
  53.4 29.7 %up_A.6 = (bf16[512,1792]{1,0:T(8,128)(2,1)}, f32[512,1792]{1,0:T(8,128)}, bf16[512,1792]{1,0:T(8,128)(2,1)}, f32[512,1792]{1,0:T(8,128)}, bf16[512,4096]{1,0:T(8,128)(2,1)}) custom-call(bf16[256,4096]{1,0:T(8,128)(2,1)} %collective-permute-done.refs_0_, bf16[256,4096]{1,0:T(8,128)(2,1)} %collective-permute-done.1.refs_1_, bf16[4096,1792]{1,0:T(8,128)(2,1)} %refs_2_.11, ...), custom_call_target="tpu_custom_call" | custom-call | flops 15032385536 | bytes 33554432 | tf_op jit(solution)/shard_map/up_A/pallas_call | solution.py:112
  83.0 11.7 %up_dA.5.refs_4_.refs_1_ = bf16[256,1792]{1,0:T(8,128)(2,1)} custom-call(bf16[256,4096]{1,0:T(8,128)(2,1)} %refs_6_.1, bf16[1792,4096]{1,0:T(8,128)(2,1)} %collective-permute-done.3.refs_1_.refs_3_.refs_2_.refs_5_, f32[256,1792]{1,0:T(8,128)} %get-tuple-element.72.refs_2_, bf16[512,1792]{1,0:T(8,128)(2,1)} %get-tuple-element.70.refs_3_.refs_0_.refs_1_), custom_call_target="tpu_custom_call" | custom-call | flops 3758096384 | bytes 16777216 | tf_op jit(solution)/shard_map/up_dA/pallas_call | solution.py:112
  94.8 1.4 collective-permute-done.5.refs_0_.refs_7_
  96.2 0.8 collective-permute-done.6.refs_1_.refs_8_
  97.0 1.5 collective-permute-start.7
  98.5 22.6 %down.5 = (f32[256,2048]{1,0:T(8,128)}, f32[256,2048]{1,0:T(8,128)}, f32[256,2048]{1,0:T(8,128)}, f32[256,2048]{1,0:T(8,128)}) custom-call(bf16[512,1792]{1,0:T(8,128)(2,1)} %get-tuple-element.70.refs_3_.refs_0_.refs_1_, bf16[512,1792]{1,0:T(8,128)(2,1)} %get-tuple-element.94.refs_1_, bf16[1792,4096]{1,0:T(8,128)(2,1)} %refs_4_.1, ...), custom_call_target="tpu_custom_call" | custom-call | flops 15032385536 | bytes 41418752 | tf_op jit(solution)/shard_map/down/pallas_call | solution.py:154
  121.2 23.6 %up_dA.6 = (bf16[512,1792]{1,0:T(8,128)(2,1)}, bf16[512,1792]{1,0:T(8,128)(2,1)}) custom-call(bf16[256,4096]{1,0:T(8,128)(2,1)} %collective-permute-done.5.refs_0_.refs_7_, bf16[256,4096]{1,0:T(8,128)(2,1)} %collective-permute-done.6.refs_1_.refs_8_, bf16[1792,4096]{1,0:T(8,128)(2,1)} %refs_4_.1, ...), custom_call_target="tpu_custom_call" | custom-call | flops 15032385536 | bytes 33554432 | tf_op jit(solution)/shard_map/up_dA/pallas_call | solution.py:112
  144.7 22.8 %down.6 = (f32[256,2048]{1,0:T(8,128)}, f32[256,2048]{1,0:T(8,128)}, f32[256,2048]{1,0:T(8,128)}, f32[256,2048]{1,0:T(8,128)}) custom-call(bf16[512,1792]{1,0:T(8,128)(2,1)} %get-tuple-element.81.refs_0_.refs_7_, bf16[512,1792]{1,0:T(8,128)(2,1)} %get-tuple-element.109.refs_1_, bf16[4096,1792]{1,0:T(8,128)(2,1)} %refs_2_.11, ...), custom_call_target="tpu_custom_call" | custom-call | flops 15032385536 | bytes 41418752 | tf_op jit(solution)/shard_map/down/pallas_call | solution.py:154
  167.5 20.4 %up_A.7 = (bf16[256,1792]{1,0:T(8,128)(2,1)}, f32[256,1792]{1,0:T(8,128)}, bf16[256,1792]{1,0:T(8,128)(2,1)}, f32[256,1792]{1,0:T(8,128)}, bf16[256,4096]{1,0:T(8,128)(2,1)}) custom-call(bf16[256,4096]{1,0:T(8,128)(2,1)} %collective-permute-done.4.refs_0_, bf16[4096,1792]{1,0:T(8,128)(2,1)} %refs_2_.11, ...), custom_call_target="tpu_custom_call" | custom-call | flops 7516192768 | bytes 31457280 | tf_op jit(solution)/shard_map/up_A/pallas_call | solution.py:112
  188.0 1.4 copy-done.7
  189.3 17.8 %up_dA.7 = (bf16[256,1792]{1,0:T(8,128)(2,1)}, bf16[256,1792]{1,0:T(8,128)(2,1)}) custom-call(bf16[256,4096]{1,0:T(8,128)(2,1)} %copy-done.7, bf16[1792,4096]{1,0:T(8,128)(2,1)} %refs_4_.1, bf16[1792,4096]{1,0:T(8,128)(2,1)} %collective-permute-done.3.refs_1_.refs_3_.refs_2_.refs_5_, f32[256,1792]{1,0:T(8,128)} %get-tuple-element.86.refs_3_, ...), custom_call_target="tpu_custom_call" | custom-call | flops 7516192768 | bytes 31457280 | tf_op jit(solution)/shard_map/up_dA/pallas_call | solution.py:112
  208.2 7.6 %collective-permute-done.18.refs_9_ = bf16[256,1792]{1,0:T(8,128)(2,1)S(1)} collective-permute-done((bf16[256,1792]{1,0:T(8,128)(2,1)S(1)}, bf16[256,1792]{1,0:T(8,128)(2,1)S(1)}, u32[]{:S(2)}, u32[]{:S(2)}) %collective-permute-start.18) | collective-permute-done | bytes 917536 | tf_op jit(solution)/shard_map/ppermute | solution.py:45
  215.8 0.9 copy-done.18
  216.9 16.8 %down.7 = (f32[256,2048]{1,0:T(8,128)}, f32[256,2048]{1,0:T(8,128)}) custom-call(bf16[256,1792]{1,0:T(8,128)(2,1)} %get-tuple-element.88.refs_0_.refs_8_, bf16[256,1792]{1,0:T(8,128)(2,1)} %get-tuple-element.110.refs_1_, bf16[4096,1792]{1,0:T(8,128)(2,1)} %refs_2_.11, bf16[4096,1792]{1,0:T(8,128)(2,1)} %collective-permute-done.2.refs_1_.refs_3_.refs_2_), custom_call_target="tpu_custom_call" | custom-call | flops 7516192768 | bytes 35389440 | tf_op jit(solution)/shard_map/down/pallas_call | solution.py:154
  234.6 1.4 collective-permute-start.21
  236.1 23.5 %down.8 = (f32[256,2048]{1,0:T(8,128)}, f32[256,2048]{1,0:T(8,128)}, f32[256,2048]{1,0:T(8,128)}, f32[256,2048]{1,0:T(8,128)}) custom-call(bf16[256,1792]{1,0:T(8,128)(2,1)} %get-tuple-element.75.refs_0_, bf16[256,1792]{1,0:T(8,128)(2,1)} %get-tuple-element.84.refs_1_.refs_2_, bf16[256,1792]{1,0:T(8,128)(2,1)} %get-tuple-element.93.refs_5_.refs_2_, ...), custom_call_target="tpu_custom_call" | custom-call | flops 15032385536 | bytes 41418752 | tf_op jit(solution)/shard_map/down/pallas_call | solution.py:154
  260.1 22.3 %collective-permute-done.22 = f32[256,2048]{1,0:T(8,128)} collective-permute-done((f32[256,2048]{1,0:T(8,128)}, f32[256,2048]{1,0:T(8,128)}, u32[]{:S(2)}, u32[]{:S(2)}) %collective-permute-start.22) | collective-permute-done | bytes 2097184 | tf_op jit(solution)/shard_map/ppermute | solution.py:45
  283.1 39.7 %shard_map.92 = f32[4096,1792]{1,0:T(8,128)} custom-call(bf16[256,4096]{1,0:T(8,128)(2,1)} %get-tuple-element.105.refs_0_, bf16[512,4096]{1,0:T(8,128)(2,1)} %get-tuple-element.106.refs_1_, bf16[256,4096]{1,0:T(8,128)(2,1)} %get-tuple-element.107.refs_2_, bf16[256,4096]{1,0:T(8,128)(2,1)} %collective-permute-done.15.refs_3_, ...), custom_call_target="tpu_custom_call" | custom-call | flops 30064771072 | bytes 53477376 | tf_op jit(solution)/shard_map/pallas_call | solution.py:180
  322.8 4.0 add.63.refs_15_
  326.8 3.2 add.62.refs_14_
  330.0 1.4 collective-permute-start.23
  332.1 1.7 collective-permute-start.24
  333.8 1.3 collective-permute-start.25
  335.6 42.3 %shard_map.93 = f32[1792,4096]{1,0:T(8,128)} custom-call(bf16[256,1792]{1,0:T(8,128)(2,1)} %get-tuple-element.75.refs_0_, bf16[512,1792]{1,0:T(8,128)(2,1)} %get-tuple-element.70.refs_3_.refs_0_.refs_1_, bf16[256,1792]{1,0:T(8,128)(2,1)} %get-tuple-element.84.refs_1_.refs_2_, bf16[256,1792]{1,0:T(8,128)(2,1)} %copy-done.17, ...), custom_call_target="tpu_custom_call" | custom-call | flops 30064771072 | bytes 53477376 | tf_op jit(solution)/shard_map/pallas_call | solution.py:180
  378.2 46.5 %collective-permute-done.27 = f32[256,2048]{1,0:T(8,128)} collective-permute-done((f32[256,2048]{1,0:T(8,128)}, f32[256,2048]{1,0:T(8,128)}, u32[]{:S(2)}, u32[]{:S(2)}) %collective-permute-start.27) | collective-permute-done | bytes 2097184 | tf_op jit(solution)/shard_map/ppermute | solution.py:45
  424.7 1.3 collective-permute-start.32
  426.5 1.1 copy-done.6
  427.6 1.9 add.69
  429.6 1.4 slice.29
  430.9 0.7 slice.27
  431.6 36.6 %collective-permute-done.25 = f32[256,2048]{1,0:T(8,128)} collective-permute-done((f32[256,2048]{1,0:T(8,128)}, f32[256,2048]{1,0:T(8,128)}, u32[]{:S(2)}, u32[]{:S(2)}) %collective-permute-start.25) | collective-permute-done | bytes 2097184 | tf_op jit(solution)/shard_map/ppermute | solution.py:45
  468.2 1.3 collective-permute-start.33
  469.5 1.9 add.68
  471.4 1.4 slice.28
  472.8 0.7 slice.26
  473.5 0.7 multiply_reduce_fusion.2
  474.2 1.3 collective-permute-start.34
  475.5 0.7 collective-permute-start.30
  476.3 5.6 slice_add_fusion
  481.9 16.8 %down.9 = (f32[256,2048]{1,0:T(8,128)}, f32[256,2048]{1,0:T(8,128)}) custom-call(bf16[256,1792]{1,0:T(8,128)(2,1)} %up_dA.4.refs_3_.refs_6_.refs_0_, bf16[256,1792]{1,0:T(8,128)(2,1)} %up_dA.5.refs_4_.refs_1_, bf16[4096,1792]{1,0:T(8,128)(2,1)} %refs_2_.11, bf16[4096,1792]{1,0:T(8,128)(2,1)} %collective-permute-done.2.refs_1_.refs_3_.refs_2_, ...), custom_call_target="tpu_custom_call" | custom-call | flops 7516192768 | bytes 35389440 | tf_op jit(solution)/shard_map/down/pallas_call | solution.py:154
  498.7 0.8 collective-permute-start.29
  499.4 1.3 collective-permute-start.28
  500.7 3.5 add_add_fusion.1
  504.2 13.2 %collective-permute-done.33 = f32[256,2048]{1,0:T(8,128)} collective-permute-done((f32[256,2048]{1,0:T(8,128)}, f32[256,2048]{1,0:T(8,128)}, u32[]{:S(2)}, u32[]{:S(2)}) %collective-permute-start.33) | collective-permute-done | bytes 2097184 | tf_op jit(solution)/shard_map/ppermute | solution.py:45
  517.5 0.9 collective-permute-start.26
  518.3 4.7 collective-permute-done.34
  523.1 2.7 add_add_fusion
  525.9 2.1 multiply_reduce_fusion
  528.0 1.2 collective-permute-done.35
  529.2 1.3 collective-permute-start.36
  530.4 31.9 %collective-permute-done.30.refs_3_ = f32[224,2048]{1,0:T(8,128)S(1)} collective-permute-done((f32[224,2048]{1,0:T(8,128)}, f32[224,2048]{1,0:T(8,128)S(1)}, u32[]{:S(2)}, u32[]{:S(2)}) %collective-permute-start.30) | collective-permute-done | bytes 1835040 | tf_op jit(solution)/shard_map/ppermute | solution.py:45
  562.3 0.8 collective-permute-start.37
  563.1 2.0 collective-permute-start.38
  565.0 2.9 add_convert_fusion
  567.9 4.2 finish.2.refs_4_
  572.1 1.9 finish.3
  (90 shorter events, 6.6 us)
Async XLA Ops:
  0.6 31.8 %collective-permute-start.2 = (bf16[4096,1792]{1,0:T(8,128)(2,1)}, bf16[4096,1792]{1,0:T(8,128)(2,1)}, u32[]{:S(2)}, u32[]{:S(2)}) collective-permute-start(bf16[4096,1792]{1,0:T(8,128)(2,1)} %refs_2_.11), channel_id=1, source_target_pairs={{0,1},{1,0},{2,3},{3,2},{4,5},{5,4},{6,7},{7,6}} | collective-permute-start | bytes 44040200 | tf_op jit(solution)/shard_map/ppermute | solution.py:45
  1.5 81.5 %collective-permute-start.3 = (bf16[1792,4096]{1,0:T(8,128)(2,1)}, bf16[1792,4096]{1,0:T(8,128)(2,1)}, u32[]{:S(2)}, u32[]{:S(2)}) collective-permute-start(bf16[1792,4096]{1,0:T(8,128)(2,1)} %refs_4_.1), channel_id=1, source_target_pairs={{0,1},{1,0},{2,3},{3,2},{4,5},{5,4},{6,7},{7,6}} | collective-permute-start | bytes 44040200 | tf_op jit(solution)/shard_map/ppermute | solution.py:45
  1.5 49.7 %collective-permute-start = (bf16[256,4096]{1,0:T(8,128)(2,1)}, bf16[256,4096]{1,0:T(8,128)(2,1)}, u32[]{:S(2)}, u32[]{:S(2)}) collective-permute-start(bf16[256,4096]{1,0:T(8,128)(2,1)} %refs_0_.6), channel_id=1, source_target_pairs={{0,2},{1,3},{2,0},{3,1},{4,6},{5,7},{6,4},{7,5}} | collective-permute-start | bytes 6291464 | tf_op jit(solution)/shard_map/ppermute | solution.py:45
  4.5 48.8 %collective-permute-start.1 = (bf16[256,4096]{1,0:T(8,128)(2,1)}, bf16[256,4096]{1,0:T(8,128)(2,1)}, u32[]{:S(2)}, u32[]{:S(2)}) collective-permute-start(bf16[256,4096]{1,0:T(8,128)(2,1)} %refs_0_.6), channel_id=1, source_target_pairs={{0,4},{1,5},{2,6},{3,7},{4,0},{5,1},{6,2},{7,3}} | collective-permute-start | bytes 6291464 | tf_op jit(solution)/shard_map/ppermute | solution.py:45
  6.0 90.2 %collective-permute-start.5 = (bf16[256,4096]{1,0:T(8,128)(2,1)}, bf16[256,4096]{1,0:T(8,128)(2,1)}, u32[]{:S(2)}, u32[]{:S(2)}) collective-permute-start(bf16[256,4096]{1,0:T(8,128)(2,1)} %refs_6_.1), channel_id=1, source_target_pairs={{0,2},{1,3},{2,0},{3,1},{4,6},{5,7},{6,4},{7,5}} | collective-permute-start | bytes 6291464 | tf_op jit(solution)/shard_map/ppermute | solution.py:45
  20.6 11.9 %copy-start.1 = (bf16[256,4096]{1,0:T(8,128)(2,1)S(1)}, bf16[256,4096]{1,0:T(8,128)(2,1)}, u32[]{:S(2)}) copy-start(bf16[256,4096]{1,0:T(8,128)(2,1)} %refs_6_.1) | copy-start | bytes 6291460
  32.4 64.6 %collective-permute-start.6 = (bf16[256,4096]{1,0:T(8,128)(2,1)S(1)}, bf16[256,4096]{1,0:T(8,128)(2,1)}, u32[]{:S(2)}, u32[]{:S(2)}) collective-permute-start(bf16[256,4096]{1,0:T(8,128)(2,1)S(1)} %copy-done.1), channel_id=1, source_target_pairs={{0,4},{1,5},{2,6},{3,7},{4,0},{5,1},{6,2},{7,3}} | collective-permute-start | bytes 6291464 | tf_op jit(solution)/shard_map/ppermute | solution.py:45
  53.3 114.2 %collective-permute-start.4 = (bf16[256,4096]{1,0:T(8,128)(2,1)}, bf16[256,4096]{1,0:T(8,128)(2,1)}, u32[]{:S(2)}, u32[]{:S(2)}) collective-permute-start(bf16[256,4096]{1,0:T(8,128)(2,1)} %collective-permute-done.1.refs_1_), channel_id=1, source_target_pairs={{0,2},{1,3},{2,0},{3,1},{4,6},{5,7},{6,4},{7,5}} | collective-permute-start | bytes 6291464 | tf_op jit(solution)/shard_map/ppermute | solution.py:45
  97.0 90.9 %collective-permute-start.7 = (bf16[256,4096]{1,0:T(8,128)(2,1)}, bf16[256,4096]{1,0:T(8,128)(2,1)S(1)}, u32[]{:S(2)}, u32[]{:S(2)}) collective-permute-start(bf16[256,4096]{1,0:T(8,128)(2,1)} %collective-permute-done.5.refs_0_.refs_7_), channel_id=1, source_target_pairs={{0,4},{1,5},{2,6},{3,7},{4,0},{5,1},{6,2},{7,3}} | collective-permute-start | bytes 6291464 | tf_op jit(solution)/shard_map/ppermute | solution.py:45
  187.9 1.4 copy-start.7
  189.3 17.8 %copy-start.4 = (bf16[256,1792]{1,0:T(8,128)(2,1)S(1)}, bf16[256,1792]{1,0:T(8,128)(2,1)}, u32[]{:S(2)}) copy-start(bf16[256,1792]{1,0:T(8,128)(2,1)} %up_dA.5.refs_4_.refs_1_) | copy-start | bytes 2752516
  207.1 75.9 %collective-permute-start.16 = (bf16[512,4096]{1,0:T(8,128)(2,1)}, bf16[512,4096]{1,0:T(8,128)(2,1)}, u32[]{:S(2)}, u32[]{:S(2)}) collective-permute-start(bf16[512,4096]{1,0:T(8,128)(2,1)} %get-tuple-element.106.refs_1_), channel_id=1, source_target_pairs={{0,1},{1,0},{2,3},{3,2},{4,5},{5,4},{6,7},{7,6}} | collective-permute-start | bytes 12582920 | tf_op jit(solution)/shard_map/ppermute | solution.py:45
  207.2 8.7 %collective-permute-start.18 = (bf16[256,1792]{1,0:T(8,128)(2,1)S(1)}, bf16[256,1792]{1,0:T(8,128)(2,1)S(1)}, u32[]{:S(2)}, u32[]{:S(2)}) collective-permute-start(bf16[256,1792]{1,0:T(8,128)(2,1)S(1)} %copy-done.4), channel_id=1, source_target_pairs={{0,1},{1,0},{2,3},{3,2},{4,5},{5,4},{6,7},{7,6}} | collective-permute-start | bytes 2752520 | tf_op jit(solution)/shard_map/ppermute | solution.py:45
  207.7 27.0 %collective-permute-start.19 = (bf16[512,1792]{1,0:T(8,128)(2,1)}, bf16[512,1792]{1,0:T(8,128)(2,1)S(1)}, u32[]{:S(2)}, u32[]{:S(2)}) collective-permute-start(bf16[512,1792]{1,0:T(8,128)(2,1)} %get-tuple-element.109.refs_1_), channel_id=1, source_target_pairs={{0,1},{1,0},{2,3},{3,2},{4,5},{5,4},{6,7},{7,6}} | collective-permute-start | bytes 5505032 | tf_op jit(solution)/shard_map/ppermute | solution.py:45
  207.7 26.0 %collective-permute-start.20 = (bf16[256,1792]{1,0:T(8,128)(2,1)}, bf16[256,1792]{1,0:T(8,128)(2,1)}, u32[]{:S(2)}, u32[]{:S(2)}) collective-permute-start(bf16[256,1792]{1,0:T(8,128)(2,1)} %get-tuple-element.110.refs_1_), channel_id=1, source_target_pairs={{0,1},{1,0},{2,3},{3,2},{4,5},{5,4},{6,7},{7,6}} | collective-permute-start | bytes 2752520 | tf_op jit(solution)/shard_map/ppermute | solution.py:45
  208.2 26.0 %collective-permute-start.10 = (bf16[256,1792]{1,0:T(8,128)(2,1)}, bf16[256,1792]{1,0:T(8,128)(2,1)S(1)}, u32[]{:S(2)}, u32[]{:S(2)}) collective-permute-start(bf16[256,1792]{1,0:T(8,128)(2,1)} %get-tuple-element.95.refs_3_), channel_id=1, source_target_pairs={{0,1},{1,0},{2,3},{3,2},{4,5},{5,4},{6,7},{7,6}} | collective-permute-start | bytes 2752520 | tf_op jit(solution)/shard_map/ppermute | solution.py:45
  215.8 0.9 copy-start.18
  216.7 17.5 %collective-permute-start.8 = (bf16[256,1792]{1,0:T(8,128)(2,1)}, bf16[256,1792]{1,0:T(8,128)(2,1)S(1)}, u32[]{:S(2)}, u32[]{:S(2)}) collective-permute-start(bf16[256,1792]{1,0:T(8,128)(2,1)} %get-tuple-element.93.refs_5_.refs_2_), channel_id=1, source_target_pairs={{0,1},{1,0},{2,3},{3,2},{4,5},{5,4},{6,7},{7,6}} | collective-permute-start | bytes 2752520 | tf_op jit(solution)/shard_map/ppermute | solution.py:45
  233.7 25.9 %collective-permute-start.15 = (bf16[256,4096]{1,0:T(8,128)(2,1)}, bf16[256,4096]{1,0:T(8,128)(2,1)}, u32[]{:S(2)}, u32[]{:S(2)}) collective-permute-start(bf16[256,4096]{1,0:T(8,128)(2,1)} %get-tuple-element.105.refs_0_), channel_id=1, source_target_pairs={{0,1},{1,0},{2,3},{3,2},{4,5},{5,4},{6,7},{7,6}} | collective-permute-start | bytes 6291464 | tf_op jit(solution)/shard_map/ppermute | solution.py:45
  234.1 1.9 copy-start.16
  234.1 25.6 %collective-permute-start.17 = (bf16[256,4096]{1,0:T(8,128)(2,1)}, bf16[256,4096]{1,0:T(8,128)(2,1)}, u32[]{:S(2)}, u32[]{:S(2)}) collective-permute-start(bf16[256,4096]{1,0:T(8,128)(2,1)} %get-tuple-element.107.refs_2_), channel_id=1, source_target_pairs={{0,1},{1,0},{2,3},{3,2},{4,5},{5,4},{6,7},{7,6}} | collective-permute-start | bytes 6291464 | tf_op jit(solution)/shard_map/ppermute | solution.py:45
  234.3 1.8 copy-start.17
  234.3 48.2 %collective-permute-start.22 = (f32[256,2048]{1,0:T(8,128)}, f32[256,2048]{1,0:T(8,128)}, u32[]{:S(2)}, u32[]{:S(2)}) collective-permute-start(f32[256,2048]{1,0:T(8,128)} %get-tuple-element.114), channel_id=1, source_target_pairs={{0,4},{1,5},{2,6},{3,7},{4,0},{5,1},{6,2},{7,3}} | collective-permute-start | bytes 6291464 | tf_op jit(solution)/shard_map/ppermute | solution.py:45
  234.6 1.4 copy-start.15
  234.6 47.9 %collective-permute-start.21 = (f32[256,2048]{1,0:T(8,128)}, f32[256,2048]{1,0:T(8,128)}, u32[]{:S(2)}, u32[]{:S(2)}) collective-permute-start(f32[256,2048]{1,0:T(8,128)} %get-tuple-element.90.refs_6_), channel_id=1, source_target_pairs={{0,2},{1,3},{2,0},{3,1},{4,6},{5,7},{6,4},{7,5}} | collective-permute-start | bytes 6291464 | tf_op jit(solution)/shard_map/ppermute | solution.py:45
  236.1 23.5 %copy-start.2 = (bf16[256,4096]{1,0:T(8,128)(2,1)S(1)}, bf16[256,4096]{1,0:T(8,128)(2,1)}, u32[]{:S(2)}) copy-start(bf16[256,4096]{1,0:T(8,128)(2,1)} %refs_6_.1) | copy-start | bytes 6291460
  236.1 46.9 %copy-start.14 = (bf16[512,1792]{1,0:T(8,128)(2,1)S(1)}, bf16[512,1792]{1,0:T(8,128)(2,1)}, u32[]{:S(2)}) copy-start(bf16[512,1792]{1,0:T(8,128)(2,1)} %get-tuple-element.94.refs_1_) | copy-start | bytes 5505028
  259.6 71.9 %collective-permute-start.11 = (bf16[256,4096]{1,0:T(8,128)(2,1)S(1)}, bf16[256,4096]{1,0:T(8,128)(2,1)}, u32[]{:S(2)}, u32[]{:S(2)}) collective-permute-start(bf16[256,4096]{1,0:T(8,128)(2,1)S(1)} %copy-done.2), channel_id=1, source_target_pairs={{0,1},{1,0},{2,3},{3,2},{4,5},{5,4},{6,7},{7,6}} | collective-permute-start | bytes 6291464 | tf_op jit(solution)/shard_map/ppermute | solution.py:45
  259.7 72.4 %collective-permute-start.12 = (bf16[256,4096]{1,0:T(8,128)(2,1)}, bf16[256,4096]{1,0:T(8,128)(2,1)}, u32[]{:S(2)}, u32[]{:S(2)}) collective-permute-start(bf16[256,4096]{1,0:T(8,128)(2,1)} %collective-permute-done.5.refs_0_.refs_7_), channel_id=1, source_target_pairs={{0,1},{1,0},{2,3},{3,2},{4,5},{5,4},{6,7},{7,6}} | collective-permute-start | bytes 6291464 | tf_op jit(solution)/shard_map/ppermute | solution.py:45
  282.5 51.3 %collective-permute-start.13 = (bf16[256,4096]{1,0:T(8,128)(2,1)}, bf16[256,4096]{1,0:T(8,128)(2,1)}, u32[]{:S(2)}, u32[]{:S(2)}) collective-permute-start(bf16[256,4096]{1,0:T(8,128)(2,1)} %collective-permute-done.6.refs_1_.refs_8_), channel_id=1, source_target_pairs={{0,1},{1,0},{2,3},{3,2},{4,5},{5,4},{6,7},{7,6}} | collective-permute-start | bytes 6291464 | tf_op jit(solution)/shard_map/ppermute | solution.py:45
  282.6 52.5 %collective-permute-start.14 = (bf16[256,4096]{1,0:T(8,128)(2,1)}, bf16[256,4096]{1,0:T(8,128)(2,1)}, u32[]{:S(2)}, u32[]{:S(2)}) collective-permute-start(bf16[256,4096]{1,0:T(8,128)(2,1)} %copy-done.7), channel_id=1, source_target_pairs={{0,1},{1,0},{2,3},{3,2},{4,5},{5,4},{6,7},{7,6}} | collective-permute-start | bytes 6291464 | tf_op jit(solution)/shard_map/ppermute | solution.py:45
  283.0 47.0 %collective-permute-start.9 = (bf16[512,1792]{1,0:T(8,128)(2,1)S(1)}, bf16[512,1792]{1,0:T(8,128)(2,1)}, u32[]{:S(2)}, u32[]{:S(2)}) collective-permute-start(bf16[512,1792]{1,0:T(8,128)(2,1)S(1)} %copy-done.14), channel_id=1, source_target_pairs={{0,1},{1,0},{2,3},{3,2},{4,5},{5,4},{6,7},{7,6}} | collective-permute-start | bytes 5505032 | tf_op jit(solution)/shard_map/ppermute | solution.py:45
  322.8 4.0 copy-start.8
  330.0 144.2 %collective-permute-start.23 = (f32[256,2048]{1,0:T(8,128)}, f32[256,2048]{1,0:T(8,128)}, u32[]{:S(2)}, u32[]{:S(2)}) collective-permute-start(f32[256,2048]{1,0:T(8,128)} %get-tuple-element.80.refs_6_), channel_id=1, source_target_pairs={{0,2},{1,3},{2,0},{3,1},{4,6},{5,7},{6,4},{7,5}} | collective-permute-start | bytes 6291464 | tf_op jit(solution)/shard_map/ppermute | solution.py:45
  331.5 167.2 %collective-permute-start.31 = (f32[256,2048]{1,0:T(8,128)}, f32[256,2048]{1,0:T(8,128)}, u32[]{:S(2)}, u32[]{:S(2)}) collective-permute-start(f32[256,2048]{1,0:T(8,128)} %get-tuple-element.83.refs_4_), channel_id=1, source_target_pairs={{0,2},{1,3},{2,0},{3,1},{4,6},{5,7},{6,4},{7,5}} | collective-permute-start | bytes 6291464 | tf_op jit(solution)/shard_map/ppermute | solution.py:45
  332.1 143.5 %collective-permute-start.24 = (f32[256,2048]{1,0:T(8,128)}, f32[256,2048]{1,0:T(8,128)}, u32[]{:S(2)}, u32[]{:S(2)}) collective-permute-start(f32[256,2048]{1,0:T(8,128)} %get-tuple-element.118), channel_id=1, source_target_pairs={{0,4},{1,5},{2,6},{3,7},{4,0},{5,1},{6,2},{7,3}} | collective-permute-start | bytes 6291464 | tf_op jit(solution)/shard_map/ppermute | solution.py:45
  333.8 134.5 %collective-permute-start.25 = (f32[256,2048]{1,0:T(8,128)}, f32[256,2048]{1,0:T(8,128)}, u32[]{:S(2)}, u32[]{:S(2)}) collective-permute-start(f32[256,2048]{1,0:T(8,128)} %get-tuple-element.111.refs_12_), channel_id=1, source_target_pairs={{0,2},{1,3},{2,0},{3,1},{4,6},{5,7},{6,4},{7,5}} | collective-permute-start | bytes 6291464 | tf_op jit(solution)/shard_map/ppermute | solution.py:45
  335.0 42.8 %copy-start = (bf16[256,4096]{1,0:T(8,128)(2,1)S(1)}, bf16[256,4096]{1,0:T(8,128)(2,1)}, u32[]{:S(2)}) copy-start(bf16[256,4096]{1,0:T(8,128)(2,1)} %refs_0_.6) | copy-start | bytes 6291460
  335.0 89.7 %collective-permute-start.27 = (f32[256,2048]{1,0:T(8,128)}, f32[256,2048]{1,0:T(8,128)}, u32[]{:S(2)}, u32[]{:S(2)}) collective-permute-start(f32[256,2048]{1,0:T(8,128)} %get-tuple-element.121), channel_id=1, source_target_pairs={{0,4},{1,5},{2,6},{3,7},{4,0},{5,1},{6,2},{7,3}} | collective-permute-start | bytes 6291464 | tf_op jit(solution)/shard_map/ppermute | solution.py:45
  424.7 74.7 %collective-permute-start.32 = (f32[256,2048]{1,0:T(8,128)}, f32[256,2048]{1,0:T(8,128)}, u32[]{:S(2)}, u32[]{:S(2)}) collective-permute-start(f32[256,2048]{1,0:T(8,128)} %add.62.refs_14_), channel_id=1, source_target_pairs={{0,4},{1,5},{2,6},{3,7},{4,0},{5,1},{6,2},{7,3}} | collective-permute-start | bytes 6291464 | tf_op jit(solution)/shard_map/ppermute | solution.py:45
  426.0 1.6 copy-start.6
  429.5 39.9 %copy-start.5 = (f32[256,2048]{1,0:T(8,128)S(1)}, f32[256,2048]{1,0:T(8,128)}, u32[]{:S(2)}) copy-start(f32[256,2048]{1,0:T(8,128)} %get-tuple-element.119) | copy-start | bytes 6291460
  468.2 49.3 %collective-permute-start.33 = (f32[256,2048]{1,0:T(8,128)}, f32[256,2048]{1,0:T(8,128)}, u32[]{:S(2)}, u32[]{:S(2)}) collective-permute-start(f32[256,2048]{1,0:T(8,128)} %get-tuple-element.124), channel_id=1, source_target_pairs={{0,4},{1,5},{2,6},{3,7},{4,0},{5,1},{6,2},{7,3}} | collective-permute-start | bytes 6291464 | tf_op jit(solution)/shard_map/ppermute | solution.py:45
  471.4 4.9 copy-start.11
  472.8 3.5 copy-start.10
  474.2 48.8 %collective-permute-start.34 = (f32[256,2048]{1,0:T(8,128)}, f32[256,2048]{1,0:T(8,128)}, u32[]{:S(2)}, u32[]{:S(2)}) collective-permute-start(f32[256,2048]{1,0:T(8,128)} %add.63.refs_15_), channel_id=1, source_target_pairs={{0,2},{1,3},{2,0},{3,1},{4,6},{5,7},{6,4},{7,5}} | collective-permute-start | bytes 6291464 | tf_op jit(solution)/shard_map/ppermute | solution.py:45
  475.5 86.8 %collective-permute-start.30 = (f32[224,2048]{1,0:T(8,128)}, f32[224,2048]{1,0:T(8,128)S(1)}, u32[]{:S(2)}, u32[]{:S(2)}) collective-permute-start(f32[224,2048]{1,0:T(8,128)} %slice.29), channel_id=1, source_target_pairs={{0,2},{1,3},{2,0},{3,1},{4,6},{5,7},{6,4},{7,5}} | collective-permute-start | bytes 5505032 | tf_op jit(solution)/shard_map/ppermute | solution.py:45
  498.7 64.4 %collective-permute-start.29 = (f32[224,2048]{1,0:T(8,128)}, f32[224,2048]{1,0:T(8,128)}, u32[]{:S(2)}, u32[]{:S(2)}) collective-permute-start(f32[224,2048]{1,0:T(8,128)} %slice.28), channel_id=1, source_target_pairs={{0,4},{1,5},{2,6},{3,7},{4,0},{5,1},{6,2},{7,3}} | collective-permute-start | bytes 5505032 | tf_op jit(solution)/shard_map/ppermute | solution.py:45
  499.4 72.7 %collective-permute-start.28 = (f32[32,2048]{1,0:T(8,128)}, f32[32,2048]{1,0:T(8,128)}, u32[]{:S(2)}, u32[]{:S(2)}) collective-permute-start(f32[32,2048]{1,0:T(8,128)} %slice.27), channel_id=1, source_target_pairs={{0,2},{1,3},{2,0},{3,1},{4,6},{5,7},{6,4},{7,5}} | collective-permute-start | bytes 786440 | tf_op jit(solution)/shard_map/ppermute | solution.py:45
  500.7 22.4 %copy-start.9 = (f32[256,2048]{1,0:T(8,128)S(1)}, f32[256,2048]{1,0:T(8,128)}, u32[]{:S(2)}) copy-start(f32[256,2048]{1,0:T(8,128)} %get-tuple-element.123) | copy-start | bytes 6291460
  517.5 54.7 %collective-permute-start.26 = (f32[32,2048]{1,0:T(8,128)}, f32[32,2048]{1,0:T(8,128)}, u32[]{:S(2)}, u32[]{:S(2)}) collective-permute-start(f32[32,2048]{1,0:T(8,128)} %slice.26), channel_id=1, source_target_pairs={{0,4},{1,5},{2,6},{3,7},{4,0},{5,1},{6,2},{7,3}} | collective-permute-start | bytes 786440 | tf_op jit(solution)/shard_map/ppermute | solution.py:45
  523.1 2.8 copy-start.13
  525.8 39.2 %copy-start.3 = (bf16[256,4096]{1,0:T(8,128)(2,1)S(1)}, bf16[256,4096]{1,0:T(8,128)(2,1)}, u32[]{:S(2)}) copy-start(bf16[256,4096]{1,0:T(8,128)(2,1)} %refs_6_.1) | copy-start | bytes 6291460
  528.0 1.2 collective-permute-start.35
  529.2 44.9 %collective-permute-start.36 = (f32[4096]{0:T(1024)S(1)}, f32[4096]{0:T(1024)S(1)}, u32[]{:S(2)}, u32[]{:S(2)}) collective-permute-start(f32[4096]{0:T(1024)S(1)} %add.77), channel_id=1, source_target_pairs={{0,2},{1,3},{2,0},{3,1},{4,6},{5,7},{6,4},{7,5}} | collective-permute-start | bytes 49160 | tf_op jit(solution)/shard_map/ppermute | solution.py:45
  562.3 5.6 copy-start.12
  562.3 11.8 %collective-permute-start.37 = (f32[4096]{0:T(1024)S(1)}, f32[4096]{0:T(1024)S(1)}, u32[]{:S(2)}, u32[]{:S(2)}) collective-permute-start(f32[4096]{0:T(1024)S(1)} %add.77), channel_id=1, source_target_pairs={{0,4},{1,5},{2,6},{3,7},{4,0},{5,1},{6,2},{7,3}} | collective-permute-start | bytes 49160 | tf_op jit(solution)/shard_map/ppermute | solution.py:45
  563.1 11.0 %collective-permute-start.38 = (f32[4096]{0:T(1024)S(1)}, f32[4096]{0:T(1024)S(1)}, u32[]{:S(2)}, u32[]{:S(2)}) collective-permute-start(f32[4096]{0:T(1024)S(1)} %add.77), channel_id=1, source_target_pairs={{0,6},{1,7},{2,4},{3,5},{4,2},{5,3},{6,0},{7,1}} | collective-permute-start | bytes 49160 | tf_op jit(solution)/shard_map/ppermute | solution.py:45

commit v3 on v2

--- a/solution.py
+++ b/solution.py
@@ -50,7 +50,7 @@
 
 
 def _params():
-    return pltpu.CompilerParams(dimension_semantics=("arbitrary",), vmem_limit_bytes=60 << 20)
+    return pltpu.CompilerParams(dimension_semantics=("arbitrary",), vmem_limit_bytes=67_000_000)
 
 
 def _fill(pieces, cat):
@@ -67,7 +67,7 @@
     return cat[...]
 
 
-def _norm(pieces, gamma, out, chunk=32):
+def _norm(pieces, gamma, out, chunk=16):
     at = 0
     for p in pieces:
         def rows(i, _, p=p, at=at):
@@ -76,7 +76,7 @@
             out[pl.ds(at + r, chunk)] = (xhatv * gamma[...]).astype(out.dtype)
             return 0
 
-        lax.fori_loop(0, p.shape[0] // chunk, rows, 0)
+        lax.fori_loop(0, p.shape[0] // chunk, rows, 0, unroll=4)
         at += p.shape[0]
 
 
@@ -121,46 +121,47 @@
     )(*pieces, *weights, *(slopes or ()), *([gamma[None]] if nx else []), *after)
 
 
-def _down(parts, weights, dims, split=1, after=(), tile=512):
+def _down(parts, weights, dims, split=1, halves=(0, 1), after=(), tile=512):
     F = parts[0][0].shape[1]
     m, nb = sum(p.shape[0] for p in parts[0]), len(parts[0])
     ms = [p.shape[0] // split for p in parts[0] for _ in range(split)]
     nt = dims == NT
     D = weights[0].shape[0 if nt else 1]
     n = len(parts)
-    half, steps = D // 2, D // tile
+    half, nh = D // 2, len(halves)
+    per = half // tile
+    steps, off = nh * per, halves[0] * per
     nin = n * nb
 
     def body(*refs):
         ws, outs = refs[nin:nin + n], refs[nin + n + len(after):]
-        cats = outs[2 * len(ms):] or [None] * n
+        cats = outs[nh * len(ms):] or [None] * n
         r = None
         for i in range(n):
             d = _dot(_fill(refs[i * nb:(i + 1) * nb], cats[i]), ws[i][...], dims)
             r = d if r is None else r + d
 
-        for h, on in enumerate((pl.program_id(0) < steps // 2, pl.program_id(0) >= steps // 2)):
-            @pl.when(on)
+        for h in range(nh):
+            @pl.when(pl.program_id(0) // per == h)
             def _():
                 at = 0
                 for b, rows in enumerate(ms):
-                    outs[2 * b + h][...] = r[at:at + rows]
+                    outs[nh * b + h][...] = r[at:at + rows]
                     at += rows
 
-    w_spec = pl.BlockSpec((tile, F), lambda j: (j, 0)) if nt else pl.BlockSpec((F, tile), lambda j: (0, j))
-    lo = lambda j: (0, jnp.minimum(j, steps // 2 - 1))
-    hi = lambda j: (0, jnp.maximum(j - steps // 2, 0))
+    w_spec = pl.BlockSpec((tile, F), lambda j: (j + off, 0)) if nt else pl.BlockSpec((F, tile), lambda j: (0, j + off))
+    places = [lambda j, h=h: (0, jnp.clip(j - h * per, 0, per - 1)) for h in range(nh)]
     blocks = [p for part in parts for p in part]
     out = pl.pallas_call(
         body, grid=(steps,),
         in_specs=[pl.BlockSpec(p.shape, lambda j: (0, 0)) for p in blocks] + [w_spec] * n + [ANY] * len(after),
-        out_specs=[pl.BlockSpec((r, tile), f) for r in ms for f in (lo, hi)],
-        out_shape=[jax.ShapeDtypeStruct((r, half), jnp.float32) for r in ms for _ in range(2)],
+        out_specs=[pl.BlockSpec((r, tile), f) for r in ms for f in places],
+        out_shape=[jax.ShapeDtypeStruct((r, half), jnp.float32) for r in ms for _ in halves],
         scratch_shapes=[pltpu.VMEM((m, F), jnp.bfloat16)] * n if nb > 1 else [],
-        compiler_params=_params(), cost_estimate=_cost(m, F * n, D, 4 * m * D),
+        compiler_params=_params(), cost_estimate=_cost(m, F * n, nh * half, 4 * m * nh * half),
         name="down",
     )(*blocks, *weights, *after)
-    return [out[2 * b:2 * b + 2] for b in range(len(ms))]
+    return [out[nh * b:nh * (b + 1)] for b in range(len(ms))]
 
 
 def _grad(left, right, tile, after=()):
@@ -188,25 +189,130 @@
     )(*left, *right, *after)
 
 
-def _finish(base, last, row, whole, n, tile):
-    def body(*refs):
-        out = refs[-1]
-        half = out.shape[1] // 2
+def _finish(base, last, row, whole, n, tile, dgs=()):
+    nw, ng = int(whole is not None), len(dgs)
+
+    def body(*refs):
+        gs, outs = refs[4:4 + ng], refs[4 + ng + nw:]
+        half = outs[0].shape[1] // 2
         for h in range(2):
-            out[:, h * half:(h + 1) * half] = (refs[h][...] + refs[2 + h][...]).astype(out.dtype)
+            outs[0][:, h * half:(h + 1) * half] = (refs[h][...] + refs[2 + h][...]).astype(outs[0].dtype)
+        if ng:
+            outs[1][...] = (gs[0][...] + gs[1][...]) + (gs[2][...] + gs[3][...])
 
     rows, half = last[0].shape
     at = lambda j: (j + row // tile, 0)
     spec = pl.BlockSpec((tile, half), at)
-    return pl.pallas_call(
+    one = pl.BlockSpec((1, 2 * half), lambda j: (0, 0))
+    out = pl.pallas_call(
         body, grid=(rows // tile,),
-        in_specs=[spec] * 2 + [pl.BlockSpec((tile, half), lambda j: (j, 0))] * 2 + [ANY] * (whole is not None),
-        out_specs=pl.BlockSpec((tile, 2 * half), at),
-        out_shape=jax.ShapeDtypeStruct((n, 2 * half), jnp.bfloat16),
-        input_output_aliases={4: 0} if whole is not None else {}, compiler_params=_params(),
+        in_specs=[spec] * 2 + [pl.BlockSpec((tile, half), lambda j: (j, 0))] * 2 + [one] * ng + [ANY] * nw,
+        out_specs=[pl.BlockSpec((tile, 2 * half), at)] + [one] * bool(ng),
+        out_shape=[jax.ShapeDtypeStruct((n, 2 * half), jnp.bfloat16)] + [jax.ShapeDtypeStruct((1, 2 * half), jnp.float32)] * bool(ng),
+        input_output_aliases={4 + ng: 0} if nw else {}, compiler_params=_params(),
         cost_estimate=pl.CostEstimate(flops=2 * rows * half, bytes_accessed=20 * rows * half, transcendentals=0),
         name="finish",
-    )(*base, *last, *([] if whole is None else [whole]))
+    )(*base, *last, *dgs, *([whole] if nw else []))
+    return out if ng else out[0]
+
+
+def _sums(pairs, pieces, tile):
+    n, D = pairs[0][0].shape
+    starts = [sum(pieces[:i]) // tile for i in range(len(pieces) + 1)]
+
+    def body(*refs):
+        ins, outs = refs[:2 * len(pairs)], refs[2 * len(pairs):]
+        j = pl.program_id(0)
+        for i in range(len(pairs)):
+            r = ins[2 * i][...] + ins[2 * i + 1][...]
+            for h in range(len(pieces)):
+                @pl.when((j >= starts[h]) & (j < starts[h + 1]))
+                def _():
+                    outs[len(pieces) * i + h][...] = r
+
+    spec = pl.BlockSpec((tile, D), lambda j: (j, 0))
+    outs = [pl.BlockSpec((tile, D), lambda j, lo=lo, hi=hi: (jnp.clip(j - lo, 0, hi - lo - 1), 0))
+            for lo, hi in zip(starts, starts[1:])]
+    return pl.pallas_call(
+        body, grid=(n // tile,), in_specs=[spec] * (2 * len(pairs)), out_specs=outs * len(pairs),
+        out_shape=[jax.ShapeDtypeStruct((r, D), jnp.float32) for r in pieces] * len(pairs), compiler_params=_params(),
+        cost_estimate=pl.CostEstimate(flops=2 * n * D, bytes_accessed=24 * n * D, transcendentals=0),
+    )(*[v for p in pairs for v in p])
+
+
+def _base(X, terms, tile=64):
+    n, D = X.shape
+    half = D // 2
+
+    def body(x_ref, *refs):
+        for h in range(2):
+            x = x_ref[:, h * half:(h + 1) * half].astype(jnp.float32)
+            refs[4 + h][...] = x + (refs[2 * h][...] + refs[2 * h + 1][...])
+
+    spec = pl.BlockSpec((tile, half), lambda j: (j, 0))
+    return pl.pallas_call(
+        body, grid=(n // tile,), in_specs=[pl.BlockSpec((tile, D), lambda j: (j, 0))] + [spec] * 4, out_specs=[spec] * 2,
+        out_shape=[jax.ShapeDtypeStruct((n, half), jnp.float32)] * 2, compiler_params=_params(),
+        cost_estimate=pl.CostEstimate(flops=2 * n * D, bytes_accessed=14 * n * D, transcendentals=0), name="base",
+    )(X, *[v for t in terms for v in t])
+
+
+def _dx(terms, X, dY, gamma, tile=64):
+    n, D = X.shape
+    nt = len(terms[0])
+
+    def body(x_ref, dy_ref, g_ref, *refs):
+        ts, (out, dg) = refs[:2 * nt], refs[2 * nt:]
+        halves = []
+        for h in range(2):
+            v = ts[h * nt][...]
+            for t in ts[h * nt + 1:(h + 1) * nt]:
+                v = v + t[...]
+            halves.append(v)
+        dXn = jnp.concatenate(halves, axis=1)
+        xhatv, rstd = _ln(x_ref[...].astype(jnp.float32))
+        part = jnp.sum(dXn * xhatv, axis=0, keepdims=True)
+
+        @pl.when(pl.program_id(0) == 0)
+        def _():
+            dg[...] = part
+
+        @pl.when(pl.program_id(0) > 0)
+        def _():
+            dg[...] += part
+
+        dxhat = dXn * g_ref[...]
+        dx = rstd * (dxhat - jnp.mean(dxhat, axis=-1, keepdims=True) - xhatv * jnp.mean(dxhat * xhatv, axis=-1, keepdims=True))
+        out[...] = (dy_ref[...].astype(jnp.float32) + dx).astype(out.dtype)
+
+    row = pl.BlockSpec((tile, D), lambda j: (j, 0))
+    one = pl.BlockSpec((1, D), lambda j: (0, 0))
+    return pl.pallas_call(
+        body, grid=(n // tile,),
+        in_specs=[row, row, one] + [pl.BlockSpec((tile, D // 2), lambda j: (j, 0))] * (2 * nt),
+        out_specs=[row, one],
+        out_shape=[jax.ShapeDtypeStruct((n, D), jnp.bfloat16), jax.ShapeDtypeStruct((1, D), jnp.float32)],
+        compiler_params=_params(),
+        cost_estimate=pl.CostEstimate(flops=20 * n * D, bytes_accessed=(6 + 4 * nt) * n * D, transcendentals=0),
+        name="dx",
+    )(X, dY, gamma[None], *terms[0], *terms[1])
+
+
+def _halves(v):
+    n, D = v.shape
+
+    def body(ref, lo, hi):
+        for h, out in enumerate((lo, hi)):
+            @pl.when(pl.program_id(0) == h)
+            def _():
+                out[...] = ref[...]
+
+    return pl.pallas_call(
+        body, grid=(2,), in_specs=[pl.BlockSpec((n // 2, D), lambda j: (j, 0))],
+        out_specs=[pl.BlockSpec((n // 2, D), lambda j: (0, 0))] * 2,
+        out_shape=[jax.ShapeDtypeStruct((n // 2, D), v.dtype)] * 2, compiler_params=_params(),
+        cost_estimate=pl.CostEstimate(flops=n * D, bytes_accessed=4 * n * D, transcendentals=0), name="halves",
+    )(v)
 
 
 def _tie(vals, after):
@@ -223,8 +329,10 @@
     def block(X, gamma, W1, W2, dY):
         n, D = X.shape
         xx, xy = _near(X)
-        gx, gy = _near(dY)
         W1p = _swap(W1, CORE)
+        halves = _halves(dY)
+        gx1, gy1 = _near(halves[0])
+        gx2, gy2 = _near(halves[1])
         W2p = _swap(W2, CORE)
         Ws1, Ws2 = [W1, W1p], [W2, W2p]
 
@@ -232,57 +340,57 @@
         (A0,) = _up([dY], [W2], NT, slopes=(s0,))
         H0p, s0p, _ = _up([X], [W1p], NN, gamma=gamma, after=(A0,))
         xx, xy = _tie((xx, xy), (H0p,))
-        xd = _swap(xy, XN)
+        xd = _swap(xx, YN)
         Hn, sn, Hnp, snp, Xn = _up([xx, xy], Ws1, NN, gamma=gamma, after=(H0p,))
-        (A0p,) = _up([dY], [W2p], NT, slopes=(s0p,), after=(Hn,))
-        gx, gy = _tie((gx, gy), (A0p,))
-        gd = _swap(gx, YN)
-        Yx, Yy = _down([[Hn], [Hnp]], Ws2, NN, split=2, after=(A0p,))
+        gx1, gy1 = _tie((gx1, gy1), (Hn,))
+        gd1 = _swap(gy1, XN)
+        (Yxa,), (Yya,) = _down([[Hn], [Hnp]], Ws2, NN, split=2, halves=(0,))
+        gx2, gy2 = _tie((gx2, gy2), (Yxa,))
+        gd2 = _swap(gy2, XN)
+        (Yxb,), (Yyb,) = _down([[Hn], [Hnp]], Ws2, NN, split=2, halves=(1,), after=(Yxa,))
+        Yx, Yy = (Yxa, Yxb), (Yya, Yyb)
         sa = _swap(Yx[0], XN)
         sb = _swap(Yy[1], YN)
-        An, Anp = _up([gx, gy], Ws2, NT, slopes=(sn, snp), after=(Yx[0],))
+        An, Anp = _up([gx1, gx2, gy1, gy2], Ws2, NT, slopes=(sn, snp), after=(Yxb,))
         Zx, Zy = _down([[An], [Anp]], Ws1, NT, split=2)
         ra = _swap(Zx[0], XN)
         rb = _swap(Zy[1], YN)
         Hd, sd, Hdp, sdp, Xd = _up([xd], Ws1, NN, gamma=gamma, after=(Zx[0],))
-        Ad, Adp = _up([gd], Ws2, NT, slopes=(sd, sdp))
+        Ad, Adp = _up([gd1, gd2], Ws2, NT, slopes=(sd, sdp))
         (Zd,) = _down([[Ad], [Adp]], Ws1, NT)
         fa = _swap(Zd[0], XN)
         fb = _swap(Zd[1], YN)
-        Y0, Yd = _down([[H0, Hd], [H0p, Hdp]], Ws2, NN, after=(Zd[0],))
+        (A0p,) = _up([dY], [W2p], NT, slopes=(s0p,), after=(Zd[0],))
+        Y0, Yd = _down([[H0, Hd], [H0p, Hdp]], Ws2, NN, after=(A0p,))
         ya = _swap(Yd[0], XN)
         yb = _swap(Yd[1], YN)
         pair = lambda own, sent: own + [_swap(v, CORE) for v in _tie(sent, (Ad,))]
         dW1 = _grad(pair([X0, Xn, Xd], [X0, Xn, Xd]),
                       pair([A0, An, Ad], [A0p, Anp, Adp]), 512, after=(Yd[0],))
         Zx1, Zy0 = _tie((Zx[1], Zy[0]), (dW1,))
-        far_a, far_b = Zy0 + fa, Zx1 + fb
+        far_a, far_b = _sums(((Zy0, fa), (Zx1, fb)), (n,), 64)
         za = _swap(far_a, YN)
         zb = _swap(far_b, XN)
+        Gs = [dY, gx1, gx2, gy1, gy2, gd1, gd2]
         dW2 = _grad(pair([H0, Hn, Hd], [H0p, Hnp, Hdp]),
-                      pair([dY, gx, gy, gd], [dY, gx, gy, gd]), 256, after=(far_a, far_b))
+                      pair(Gs, Gs), 256, after=(far_a, far_b))
         Yx1, Yy0, Y00, Y01, X = _tie((Yx[1], Yy[0], Y0[0], Y0[1], X), (dW2,))
-        far_a, far_b = Yy0 + ya, Yx1 + yb
-        q = n - n // 8
-        va = _swap(far_a[:q], YN)
-        vb = _swap(far_b[:q], XN)
-        x = X.astype(jnp.float32)
-        base = x[:, :D // 2] + (Y00 + sa), x[:, D // 2:] + (Y01 + sb)
-        xhatv, rstd = _ln(x)
+        cuts = n * 5 // 8, n // 4, n // 8
+        sums = _sums(((Yy0, ya), (Yx1, yb)), cuts, n // 8)
+        va, vb = _swap(sums[0], YN), _swap(sums[3], XN)
+        ua, ub = _swap(sums[1], YN), _swap(sums[4], XN)
+        base = _base(X, ((Y00, sa), (Y01, sb)))
         (Z0,) = _down([[A0], [A0p]], Ws1, NT, after=base)
-        dXn = jnp.concatenate([Z0[0] + ra + za, Z0[1] + rb + zb], axis=1)
-        dg = jnp.sum(dXn * xhatv, axis=0)
+        dX, dg = _dx(((Z0[0], ra, za), (Z0[1], rb, zb)), X, dY, gamma)
         dg = dg + _swap(dg, CORE)
-        dgamma = (dg + _swap(dg, XN)) + (_swap(dg, YN) + _swap(dg, DIAG))
-        wa = _swap(far_a[q:], YN)
-        wb = _swap(far_b[q:], XN)
-        dxhat = dXn * gamma
-        dx = rstd * (dxhat - jnp.mean(dxhat, axis=-1, keepdims=True) - xhatv * jnp.mean(dxhat * xhatv, axis=-1, keepdims=True))
-        dX = (dY.astype(jnp.float32) + dx).astype(jnp.bfloat16)
-        va, vb = _tie((va, vb), (dX,))
-        Y = _finish(base, (va, vb), 0, None, n, q // 2)
-        Y = _finish(base, (wa, wb), q, Y, n, n - q)
-        return Y, dX, dW1, dW2, dgamma
+        dgs = dg, _swap(dg, XN), _swap(dg, YN), _swap(dg, DIAG)
+        last_a, last_b = _tie((sums[2], sums[5]), (dX,))
+        wa = _swap(last_a, YN)
+        wb = _swap(last_b, XN)
+        Y = _finish(base, (va, vb), 0, None, n, cuts[0] // 2)
+        Y = _finish(base, (ua, ub), cuts[0], Y, n, cuts[2])
+        Y, dgamma = _finish(base, (wa, wb), cuts[0] + cuts[1], Y, n, cuts[2], dgs)
+        return Y, dX, dW1, dW2, dgamma.reshape(D)
 
     return jax.shard_map(block, mesh=mesh,
                          in_specs=(rows, P(None), P(None, "tp"), P("tp", None), rows),

time: 575 us -> 542 us (0.943)
  waiting for transfers between devices: 173 us -> 138 us
  Pallas kernels: 334 us -> 368 us
  other arithmetic: 30.1 us -> 0.74 us
  local copies, waits for them, and re-layouts: 7.63 us -> 0.56 us
    ppermute x39 -> x47, waiting for transfers between devices: 173 us -> 138 us  [_swap(): return lax.ppermute(v, 'tp', [(i, i ^ k) for i in range(8)])]
    pallas_call x0 -> x5, Pallas kernels: none -> 32.9 us  [the longest x2 13.7 us: _sums(): pl.pallas_call(body, grid=(n // tile,), in_specs=[spec] * (2 * len(pairs)...]
    add x8 -> x0, other arithmetic: 23.6 us -> none  [the longest x2 7.24 us: block(): far_a, far_b = (Zy0 + fa, Zx1 + fb)]
    ppermute x39 -> x47, starting transfers between devices: 29.1 us -> 33.6 us  [_swap(): return lax.ppermute(v, 'tp', [(i, i ^ k) for i in range(8)])]
    pallas_call x5 -> x6, Pallas kernels: 102 us -> 106 us  [_down(): pl.pallas_call(body, grid=(steps,), in_specs=[pl.BlockSpec(p.shape, lambd...]
  transfers between devices with their start and end apart: 39 -> 47, of which waited for: 13 -> 13; matrix products, arithmetic and copies ran while one was open for 6% -> 0% of each run, Pallas kernels for 55% -> 68%
where the time goes in v3:
time: 542 us; the launch traced here: 541 us
  Pallas kernels  368 us (68%)
  waiting for transfers between devices  138 us (25%)
  starting transfers between devices  33.6 us (6%)
    pallas_call x8, Pallas kernels, _up(): pl.pallas_call(body, grid=(F // tile,), in_specs=[pl.BlockSpec(p.shape, l...  139 us
    ppermute x47, waiting for transfers between devices, _swap(): return lax.ppermute(v, 'tp', [(i, i ^ k) for i in range(8)])  138 us
    pallas_call x6, Pallas kernels, _down(): pl.pallas_call(body, grid=(steps,), in_specs=[pl.BlockSpec(p.shape, lambd...  106 us
    pallas_call x2, Pallas kernels, _grad(): pl.pallas_call(body, grid=(M // tile,), in_specs=[pl.BlockSpec((p.shape[0...  81.9 us
    ppermute x47, starting transfers between devices, _swap(): return lax.ppermute(v, 'tp', [(i, i ^ k) for i in range(8)])  33.6 us
    pallas_call x2, Pallas kernels, _sums(): pl.pallas_call(body, grid=(n // tile,), in_specs=[spec] * (2 * len(pairs)...  13.7 us
  transfers between devices with their start and end apart: 47, of which 13 were waited for; matrix products, arithmetic and copies ran while one was open for 0% of the time, Pallas kernels for 68%

profile of v3, /device:TPU:0, one launch (start us, length us, event | category | flops | bytes accessed | tf_op | source)
XLA Modules:
  0.0 540.9 jit_solution(16681874639500979941)
XLA Ops:
  0.6 0.9 collective-permute-start.2
  1.5 2.9 collective-permute-start
  4.5 1.5 collective-permute-start.1
  6.0 2.9 halves.1
  8.9 0.5 collective-permute-start.5
  9.5 13.5 %up_A.4 = (bf16[256,1792]{1,0:T(8,128)(2,1)}, f32[256,1792]{1,0:T(8,128)}, bf16[256,4096]{1,0:T(8,128)(2,1)}) custom-call(bf16[256,4096]{1,0:T(8,128)(2,1)} %x_ref.1, bf16[4096,1792]{1,0:T(8,128)(2,1)} %refs_2_.13, f32[1,4096]{1,0:T(1,128)} %bitcast.2), custom_call_target="tpu_custom_call" | custom-call | flops 3758096384 | bytes 16777216 | tf_op jit(solution)/shard_map/up_A/pallas_call | solution.py:112
  23.0 11.7 %up_dA.4.refs_3_.refs_6_.refs_0_ = bf16[256,1792]{1,0:T(8,128)(2,1)} custom-call(bf16[256,4096]{1,0:T(8,128)(2,1)} %dy_ref.1, bf16[1792,4096]{1,0:T(8,128)(2,1)} %refs_4_.3, f32[256,1792]{1,0:T(8,128)} %get-tuple-element.87.refs_2_), custom_call_target="tpu_custom_call" | custom-call | flops 3758096384 | bytes 16777216 | tf_op jit(solution)/shard_map/up_dA/pallas_call | solution.py:112
  34.7 13.6 %up_A.5 = (bf16[256,1792]{1,0:T(8,128)(2,1)}, f32[256,1792]{1,0:T(8,128)}, bf16[256,4096]{1,0:T(8,128)(2,1)}) custom-call(bf16[256,4096]{1,0:T(8,128)(2,1)} %x_ref.1, bf16[4096,1792]{1,0:T(8,128)(2,1)} %collective-permute-done.2.refs_1_.refs_3_.refs_2_, f32[1,4096]{1,0:T(1,128)} %bitcast.3, bf16[256,1792]{1,0:T(8,128)(2,1)} %up_dA.4.refs_3_.refs_6_.refs_0_), custom_call_target="tpu_custom_call" | custom-call | flops 3758096384 | bytes 16777216 | tf_op jit(solution)/shard_map/up_A/pallas_call | solution.py:112
  48.3 2.9 collective-permute-done.refs_0_
  51.3 2.0 collective-permute-start.7
  53.3 1.5 collective-permute-start.8
  54.8 27.8 %up_A.6 = (bf16[512,1792]{1,0:T(8,128)(2,1)}, f32[512,1792]{1,0:T(8,128)}, bf16[512,1792]{1,0:T(8,128)(2,1)}, f32[512,1792]{1,0:T(8,128)}, bf16[512,4096]{1,0:T(8,128)(2,1)}) custom-call(bf16[256,4096]{1,0:T(8,128)(2,1)} %collective-permute-done.refs_0_, bf16[256,4096]{1,0:T(8,128)(2,1)} %collective-permute-done.1.refs_1_, bf16[4096,1792]{1,0:T(8,128)(2,1)} %refs_2_.13, ...), custom_call_target="tpu_custom_call" | custom-call | flops 15032385536 | bytes 33554432 | tf_op jit(solution)/shard_map/up_A/pallas_call | solution.py:112
  82.7 0.5 collective-permute-start.4
  83.2 13.1 %down.6 = (f32[256,2048]{1,0:T(8,128)}, f32[256,2048]{1,0:T(8,128)}) custom-call(bf16[512,1792]{1,0:T(8,128)(2,1)} %get-tuple-element.91.refs_0_.refs_1_, bf16[512,1792]{1,0:T(8,128)(2,1)} %get-tuple-element.119.refs_1_, bf16[1792,4096]{1,0:T(8,128)(2,1)} %refs_4_.3, bf16[1792,4096]{1,0:T(8,128)(2,1)} %collective-permute-done.3.refs_3_.refs_5_.refs_1_), custom_call_target="tpu_custom_call" | custom-call | flops 7516192768 | bytes 22544384 | tf_op jit(solution)/shard_map/down/pallas_call | solution.py:155
  96.4 1.9 collective-permute-done.8.refs_3_.refs_10_
  98.3 1.9 collective-permute-start.10
  100.3 13.2 %down.7 = (f32[256,2048]{1,0:T(8,128)}, f32[256,2048]{1,0:T(8,128)}) custom-call(bf16[512,1792]{1,0:T(8,128)(2,1)} %get-tuple-element.91.refs_0_.refs_1_, bf16[512,1792]{1,0:T(8,128)(2,1)} %get-tuple-element.119.refs_1_, bf16[1792,4096]{1,0:T(8,128)(2,1)} %refs_4_.3, bf16[1792,4096]{1,0:T(8,128)(2,1)} %collective-permute-done.3.refs_3_.refs_5_.refs_1_, ...), custom_call_target="tpu_custom_call" | custom-call | flops 7516192768 | bytes 22544384 | tf_op jit(solution)/shard_map/down/pallas_call | solution.py:155
  113.4 23.1 %up_dA.5 = (bf16[512,1792]{1,0:T(8,128)(2,1)}, bf16[512,1792]{1,0:T(8,128)(2,1)}) custom-call(bf16[128,4096]{1,0:T(8,128)(2,1)} %collective-permute-done.5.refs_0_.refs_7_, bf16[128,4096]{1,0:T(8,128)(2,1)} %collective-permute-done.7.refs_1_.refs_8_, bf16[128,4096]{1,0:T(8,128)(2,1)} %collective-permute-done.6.refs_2_.refs_9_, ...), custom_call_target="tpu_custom_call" | custom-call | flops 15032385536 | bytes 33554432 | tf_op jit(solution)/shard_map/up_dA/pallas_call | solution.py:112
  136.6 22.8 %down.8 = (f32[256,2048]{1,0:T(8,128)}, f32[256,2048]{1,0:T(8,128)}, f32[256,2048]{1,0:T(8,128)}, f32[256,2048]{1,0:T(8,128)}) custom-call(bf16[512,1792]{1,0:T(8,128)(2,1)} %get-tuple-element.105.refs_0_.refs_7_, bf16[512,1792]{1,0:T(8,128)(2,1)} %get-tuple-element.137.refs_1_, bf16[4096,1792]{1,0:T(8,128)(2,1)} %refs_2_.13, ...), custom_call_target="tpu_custom_call" | custom-call | flops 15032385536 | bytes 41418752 | tf_op jit(solution)/shard_map/down/pallas_call | solution.py:155
  159.3 20.1 %up_A.7 = (bf16[256,1792]{1,0:T(8,128)(2,1)}, f32[256,1792]{1,0:T(8,128)}, bf16[256,1792]{1,0:T(8,128)(2,1)}, f32[256,1792]{1,0:T(8,128)}, bf16[256,4096]{1,0:T(8,128)(2,1)}) custom-call(bf16[256,4096]{1,0:T(8,128)(2,1)} %collective-permute-done.4.refs_0_, bf16[4096,1792]{1,0:T(8,128)(2,1)} %refs_2_.13, ...), custom_call_target="tpu_custom_call" | custom-call | flops 7516192768 | bytes 31457280 | tf_op jit(solution)/shard_map/up_A/pallas_call | solution.py:112
  179.4 7.1 %collective-permute-done.10.refs_1_.refs_12_ = bf16[128,4096]{1,0:T(8,128)(2,1)} collective-permute-done((bf16[128,4096]{1,0:T(8,128)(2,1)}, bf16[128,4096]{1,0:T(8,128)(2,1)}, u32[]{:S(2)}, u32[]{:S(2)}) %collective-permute-start.10) | collective-permute-done | bytes 1048608 | tf_op jit(solution)/shard_map/ppermute | solution.py:45
  186.5 17.5 %up_dA.6 = (bf16[256,1792]{1,0:T(8,128)(2,1)}, bf16[256,1792]{1,0:T(8,128)(2,1)}) custom-call(bf16[128,4096]{1,0:T(8,128)(2,1)} %collective-permute-done.9.refs_0_.refs_11_, bf16[128,4096]{1,0:T(8,128)(2,1)} %collective-permute-done.10.refs_1_.refs_12_, bf16[1792,4096]{1,0:T(8,128)(2,1)} %refs_4_.3, ...), custom_call_target="tpu_custom_call" | custom-call | flops 7516192768 | bytes 31457280 | tf_op jit(solution)/shard_map/up_dA/pallas_call | solution.py:112
  204.6 16.8 %down.9 = (f32[256,2048]{1,0:T(8,128)}, f32[256,2048]{1,0:T(8,128)}) custom-call(bf16[256,1792]{1,0:T(8,128)(2,1)} %get-tuple-element.113.refs_0_.refs_8_, bf16[256,1792]{1,0:T(8,128)(2,1)} %get-tuple-element.138.refs_1_, bf16[4096,1792]{1,0:T(8,128)(2,1)} %refs_2_.13, bf16[4096,1792]{1,0:T(8,128)(2,1)} %collective-permute-done.2.refs_1_.refs_3_.refs_2_), custom_call_target="tpu_custom_call" | custom-call | flops 7516192768 | bytes 35389440 | tf_op jit(solution)/shard_map/down/pallas_call | solution.py:155
  221.3 11.7 %up_dA.7.refs_6_.refs_1_ = bf16[256,1792]{1,0:T(8,128)(2,1)} custom-call(bf16[256,4096]{1,0:T(8,128)(2,1)} %dy_ref.1, bf16[1792,4096]{1,0:T(8,128)(2,1)} %collective-permute-done.3.refs_3_.refs_5_.refs_1_, f32[256,1792]{1,0:T(8,128)} %get-tuple-element.110.refs_2_, f32[256,2048]{1,0:T(8,128)} %get-tuple-element.115.refs_3_), custom_call_target="tpu_custom_call" | custom-call | flops 3758096384 | bytes 16777216 | tf_op jit(solution)/shard_map/up_dA/pallas_call | solution.py:112
  234.1 1.8 collective-permute-done.24.refs_9_
  236.0 10.2 %collective-permute-done.26.refs_11_ = bf16[256,1792]{1,0:T(8,128)(2,1)} collective-permute-done((bf16[256,1792]{1,0:T(8,128)(2,1)}, bf16[256,1792]{1,0:T(8,128)(2,1)}, u32[]{:S(2)}, u32[]{:S(2)}) %collective-permute-start.26) | collective-permute-done | bytes 917536 | tf_op jit(solution)/shard_map/ppermute | solution.py:45
  246.9 3.5 collective-permute-done.17.refs_16_
  250.5 1.4 collective-permute-done.18.refs_17_
  252.0 1.4 collective-permute-done.19.refs_18_
  253.3 0.7 collective-permute-start.27
  254.0 1.5 collective-permute-start.28
  255.5 23.5 %down.10 = (f32[256,2048]{1,0:T(8,128)}, f32[256,2048]{1,0:T(8,128)}, f32[256,2048]{1,0:T(8,128)}, f32[256,2048]{1,0:T(8,128)}) custom-call(bf16[256,1792]{1,0:T(8,128)(2,1)} %get-tuple-element.96.refs_0_, bf16[256,1792]{1,0:T(8,128)(2,1)} %get-tuple-element.108.refs_1_.refs_2_, bf16[256,1792]{1,0:T(8,128)(2,1)} %get-tuple-element.118.refs_5_.refs_2_, ...), custom_call_target="tpu_custom_call" | custom-call | flops 15032385536 | bytes 41418752 | tf_op jit(solution)/shard_map/down/pallas_call | solution.py:155
  279.5 21.8 %collective-permute-done.27.refs_1_ = f32[256,2048]{1,0:T(8,128)} collective-permute-done((f32[256,2048]{1,0:T(8,128)}, f32[256,2048]{1,0:T(8,128)}, u32[]{:S(2)}, u32[]{:S(2)}) %collective-permute-start.27) | collective-permute-done | bytes 2097184 | tf_op jit(solution)/shard_map/ppermute | solution.py:45
  301.7 1.3 collective-permute-start.31
  303.1 1.5 collective-permute-start.32
  304.6 39.7 %shard_map.92 = f32[4096,1792]{1,0:T(8,128)} custom-call(bf16[256,4096]{1,0:T(8,128)(2,1)} %get-tuple-element.133.refs_0_, bf16[512,4096]{1,0:T(8,128)(2,1)} %get-tuple-element.134.refs_1_, bf16[256,4096]{1,0:T(8,128)(2,1)} %get-tuple-element.135.refs_2_, bf16[256,4096]{1,0:T(8,128)(2,1)} %collective-permute-done.21.refs_3_, ...), custom_call_target="tpu_custom_call" | custom-call | flops 30064771072 | bytes 53477376 | tf_op jit(solution)/shard_map/pallas_call | solution.py:181
  344.3 5.8 %shard_map.93 = (f32[256,2048]{1,0:T(8,128)}, f32[256,2048]{1,0:T(8,128)}) custom-call(f32[256,2048]{1,0:T(8,128)} %get-tuple-element.140.refs_0_, f32[256,2048]{1,0:T(8,128)} %collective-permute-done.27.refs_1_, f32[256,2048]{1,0:T(8,128)} %get-tuple-element.141.refs_2_, f32[256,2048]{1,0:T(8,128)} %collective-permute-done.28.refs_3_), custom_call_target="tpu_custom_call" | custom-call | flops 1048576 | bytes 12582912 | tf_op jit(solution)/shard_map/pallas_call | solution.py:236
  350.1 0.7 collective-permute-start.33
  350.8 0.5 collective-permute-start.30
  351.4 1.5 collective-permute-start.35
  352.9 0.5 collective-permute-start.34
  353.4 1.3 collective-permute-start.36
  354.7 42.2 %shard_map.94 = f32[1792,4096]{1,0:T(8,128)} custom-call(bf16[256,1792]{1,0:T(8,128)(2,1)} %get-tuple-element.96.refs_0_, bf16[512,1792]{1,0:T(8,128)(2,1)} %get-tuple-element.91.refs_0_.refs_1_, bf16[256,1792]{1,0:T(8,128)(2,1)} %get-tuple-element.108.refs_1_.refs_2_, bf16[256,1792]{1,0:T(8,128)(2,1)} %collective-permute-done.11.refs_3_, ...), custom_call_target="tpu_custom_call" | custom-call | flops 30064771072 | bytes 53477376 | tf_op jit(solution)/shard_map/pallas_call | solution.py:181
  396.9 7.9 %shard_map.95 = (f32[160,2048]{1,0:T(8,128)}, f32[64,2048]{1,0:T(8,128)}, f32[32,2048]{1,0:T(8,128)}, f32[160,2048]{1,0:T(8,128)}, f32[64,2048]{1,0:T(8,128)}, /*index=5*/f32[32,2048]{1,0:T(8,128)}) custom-call(f32[256,2048]{1,0:T(8,128)} %get-tuple-element.151.refs_0_, f32[256,2048]{1,0:T(8,128)} %collective-permute-done.31.refs_1_, ...), custom_call_target="tpu_custom_call" | custom-call | flops 1048576 | bytes 12582912 | tf_op jit(solution)/shard_map/pallas_call | solution.py:236
  404.8 1.5 collective-permute-start.45
  406.4 0.7 collective-permute-start.46
  407.1 6.2 %base.1 = (f32[256,2048]{1,0:T(8,128)}, f32[256,2048]{1,0:T(8,128)}) custom-call(bf16[256,4096]{1,0:T(8,128)(2,1)} %x_ref.1, f32[256,2048]{1,0:T(8,128)} %get-tuple-element.146.refs_0_, f32[256,2048]{1,0:T(8,128)} %collective-permute-done.29.refs_1_, f32[256,2048]{1,0:T(8,128)} %get-tuple-element.147.refs_2_, f32[256,2048]{1,0:T(8,128)} %collective-permute-done.30.refs_3_), custom_call_target="tpu_custom_call" | custom-call | flops 2097152 | bytes 14680064 | tf_op jit(solution)/shard_map/base/pallas_call | solution.py:253
  413.3 31.3 %collective-permute-done.35.refs_4_ = f32[256,2048]{1,0:T(8,128)} collective-permute-done((f32[256,2048]{1,0:T(8,128)}, f32[256,2048]{1,0:T(8,128)}, u32[]{:S(2)}, u32[]{:S(2)}) %collective-permute-start.35) | collective-permute-done | bytes 2097184 | tf_op jit(solution)/shard_map/ppermute | solution.py:45
  444.6 0.5 collective-permute-start.43
  445.1 44.4 %collective-permute-done.34.refs_2_ = f32[256,2048]{1,0:T(8,128)} collective-permute-done((f32[256,2048]{1,0:T(8,128)}, f32[256,2048]{1,0:T(8,128)}, u32[]{:S(2)}, u32[]{:S(2)}) %collective-permute-start.34) | collective-permute-done | bytes 2097184 | tf_op jit(solution)/shard_map/ppermute | solution.py:45
  489.5 1.3 collective-permute-start.44
  490.9 16.8 %down.11 = (f32[256,2048]{1,0:T(8,128)}, f32[256,2048]{1,0:T(8,128)}) custom-call(bf16[256,1792]{1,0:T(8,128)(2,1)} %up_dA.4.refs_3_.refs_6_.refs_0_, bf16[256,1792]{1,0:T(8,128)(2,1)} %up_dA.7.refs_6_.refs_1_, bf16[4096,1792]{1,0:T(8,128)(2,1)} %refs_2_.13, bf16[4096,1792]{1,0:T(8,128)(2,1)} %collective-permute-done.2.refs_1_.refs_3_.refs_2_, ...), custom_call_target="tpu_custom_call" | custom-call | flops 7516192768 | bytes 35389440 | tf_op jit(solution)/shard_map/down/pallas_call | solution.py:155
  507.6 10.0 %dx.1 = (bf16[256,4096]{1,0:T(8,128)(2,1)}, f32[1,4096]{1,0:T(1,128)}) custom-call(bf16[256,4096]{1,0:T(8,128)(2,1)} %x_ref.1, bf16[256,4096]{1,0:T(8,128)(2,1)} %dy_ref.1, f32[1,4096]{1,0:T(1,128)} %bitcast.6, f32[256,2048]{1,0:T(8,128)} %get-tuple-element.156.refs_0_, f32[256,2048]{1,0:T(8,128)} %collective-permute-done.33.refs_1_, ...), custom_call_target="tpu_custom_call" | custom-call | flops 20971520 | bytes 18874368 | tf_op jit(solution)/shard_map/dx/pallas_call | solution.py:290
  517.7 9.5 %collective-permute-done.43.refs_2_ = f32[64,2048]{1,0:T(8,128)} collective-permute-done((f32[64,2048]{1,0:T(8,128)}, f32[64,2048]{1,0:T(8,128)}, u32[]{:S(2)}, u32[]{:S(2)}) %collective-permute-start.43) | collective-permute-done | bytes 524320 | tf_op jit(solution)/shard_map/ppermute | solution.py:45
  527.2 0.5 collective-permute-start.37
  527.7 0.7 collective-permute-start.38
  528.4 0.7 add.3.refs_4_
  529.1 1.4 collective-permute-start.40
  530.5 1.5 collective-permute-start.41
  532.0 0.6 collective-permute-start.42
  532.6 3.4 finish.3.refs_4_
  536.1 2.3 finish.4.refs_8_
  538.4 0.6 copy-done.1
  538.9 2.0 finish.5
  (59 shorter events, 3.9 us)
Async XLA Ops:
  0.6 34.1 %collective-permute-start.2 = (bf16[4096,1792]{1,0:T(8,128)(2,1)}, bf16[4096,1792]{1,0:T(8,128)(2,1)}, u32[]{:S(2)}, u32[]{:S(2)}) collective-permute-start(bf16[4096,1792]{1,0:T(8,128)(2,1)} %refs_2_.13), channel_id=1, source_target_pairs={{0,1},{1,0},{2,3},{3,2},{4,5},{5,4},{6,7},{7,6}} | collective-permute-start | bytes 44040200 | tf_op jit(solution)/shard_map/ppermute | solution.py:45
  1.5 81.7 %collective-permute-start.3 = (bf16[1792,4096]{1,0:T(8,128)(2,1)}, bf16[1792,4096]{1,0:T(8,128)(2,1)}, u32[]{:S(2)}, u32[]{:S(2)}) collective-permute-start(bf16[1792,4096]{1,0:T(8,128)(2,1)} %refs_4_.3), channel_id=1, source_target_pairs={{0,1},{1,0},{2,3},{3,2},{4,5},{5,4},{6,7},{7,6}} | collective-permute-start | bytes 44040200 | tf_op jit(solution)/shard_map/ppermute | solution.py:45
  1.5 49.7 %collective-permute-start = (bf16[256,4096]{1,0:T(8,128)(2,1)}, bf16[256,4096]{1,0:T(8,128)(2,1)}, u32[]{:S(2)}, u32[]{:S(2)}) collective-permute-start(bf16[256,4096]{1,0:T(8,128)(2,1)} %x_ref.1), channel_id=1, source_target_pairs={{0,2},{1,3},{2,0},{3,1},{4,6},{5,7},{6,4},{7,5}} | collective-permute-start | bytes 6291464 | tf_op jit(solution)/shard_map/ppermute | solution.py:45
  4.5 48.8 %collective-permute-start.1 = (bf16[256,4096]{1,0:T(8,128)(2,1)}, bf16[256,4096]{1,0:T(8,128)(2,1)}, u32[]{:S(2)}, u32[]{:S(2)}) collective-permute-start(bf16[256,4096]{1,0:T(8,128)(2,1)} %x_ref.1), channel_id=1, source_target_pairs={{0,4},{1,5},{2,6},{3,7},{4,0},{5,1},{6,2},{7,3}} | collective-permute-start | bytes 6291464 | tf_op jit(solution)/shard_map/ppermute | solution.py:45
  8.9 73.7 %collective-permute-start.5 = (bf16[128,4096]{1,0:T(8,128)(2,1)}, bf16[128,4096]{1,0:T(8,128)(2,1)}, u32[]{:S(2)}, u32[]{:S(2)}) collective-permute-start(bf16[128,4096]{1,0:T(8,128)(2,1)} %get-tuple-element.97), channel_id=1, source_target_pairs={{0,2},{1,3},{2,0},{3,1},{4,6},{5,7},{6,4},{7,5}} | collective-permute-start | bytes 3145736 | tf_op jit(solution)/shard_map/ppermute | solution.py:45
  34.7 48.5 %collective-permute-start.6 = (bf16[128,4096]{1,0:T(8,128)(2,1)}, bf16[128,4096]{1,0:T(8,128)(2,1)}, u32[]{:S(2)}, u32[]{:S(2)}) collective-permute-start(bf16[128,4096]{1,0:T(8,128)(2,1)} %get-tuple-element.97), channel_id=1, source_target_pairs={{0,4},{1,5},{2,6},{3,7},{4,0},{5,1},{6,2},{7,3}} | collective-permute-start | bytes 3145736 | tf_op jit(solution)/shard_map/ppermute | solution.py:45
  51.3 45.1 %collective-permute-start.7 = (bf16[128,4096]{1,0:T(8,128)(2,1)}, bf16[128,4096]{1,0:T(8,128)(2,1)}, u32[]{:S(2)}, u32[]{:S(2)}) collective-permute-start(bf16[128,4096]{1,0:T(8,128)(2,1)} %get-tuple-element.99), channel_id=1, source_target_pairs={{0,2},{1,3},{2,0},{3,1},{4,6},{5,7},{6,4},{7,5}} | collective-permute-start | bytes 3145736 | tf_op jit(solution)/shard_map/ppermute | solution.py:45
  53.3 44.9 %collective-permute-start.8 = (bf16[128,4096]{1,0:T(8,128)(2,1)}, bf16[128,4096]{1,0:T(8,128)(2,1)}, u32[]{:S(2)}, u32[]{:S(2)}) collective-permute-start(bf16[128,4096]{1,0:T(8,128)(2,1)} %get-tuple-element.99), channel_id=1, source_target_pairs={{0,4},{1,5},{2,6},{3,7},{4,0},{5,1},{6,2},{7,3}} | collective-permute-start | bytes 3145736 | tf_op jit(solution)/shard_map/ppermute | solution.py:45
  82.7 76.7 %collective-permute-start.4 = (bf16[256,4096]{1,0:T(8,128)(2,1)}, bf16[256,4096]{1,0:T(8,128)(2,1)}, u32[]{:S(2)}, u32[]{:S(2)}) collective-permute-start(bf16[256,4096]{1,0:T(8,128)(2,1)} %collective-permute-done.refs_0_), channel_id=1, source_target_pairs={{0,4},{1,5},{2,6},{3,7},{4,0},{5,1},{6,2},{7,3}} | collective-permute-start | bytes 6291464 | tf_op jit(solution)/shard_map/ppermute | solution.py:45
  96.3 137.3 %collective-permute-start.29 = (f32[256,2048]{1,0:T(8,128)}, f32[256,2048]{1,0:T(8,128)}, u32[]{:S(2)}, u32[]{:S(2)}) collective-permute-start(f32[256,2048]{1,0:T(8,128)} %get-tuple-element.93.refs_4_), channel_id=1, source_target_pairs={{0,2},{1,3},{2,0},{3,1},{4,6},{5,7},{6,4},{7,5}} | collective-permute-start | bytes 6291464 | tf_op jit(solution)/shard_map/ppermute | solution.py:45
  98.2 81.2 %collective-permute-start.9 = (bf16[128,4096]{1,0:T(8,128)(2,1)}, bf16[128,4096]{1,0:T(8,128)(2,1)}, u32[]{:S(2)}, u32[]{:S(2)}) collective-permute-start(bf16[128,4096]{1,0:T(8,128)(2,1)} %collective-permute-done.6.refs_2_.refs_9_), channel_id=1, source_target_pairs={{0,2},{1,3},{2,0},{3,1},{4,6},{5,7},{6,4},{7,5}} | collective-permute-start | bytes 3145736 | tf_op jit(solution)/shard_map/ppermute | solution.py:45
  98.3 88.2 %collective-permute-start.10 = (bf16[128,4096]{1,0:T(8,128)(2,1)}, bf16[128,4096]{1,0:T(8,128)(2,1)}, u32[]{:S(2)}, u32[]{:S(2)}) collective-permute-start(bf16[128,4096]{1,0:T(8,128)(2,1)} %collective-permute-done.8.refs_3_.refs_10_), channel_id=1, source_target_pairs={{0,2},{1,3},{2,0},{3,1},{4,6},{5,7},{6,4},{7,5}} | collective-permute-start | bytes 3145736 | tf_op jit(solution)/shard_map/ppermute | solution.py:45
  204.0 29.6 %collective-permute-start.11 = (bf16[256,1792]{1,0:T(8,128)(2,1)}, bf16[256,1792]{1,0:T(8,128)(2,1)}, u32[]{:S(2)}, u32[]{:S(2)}) collective-permute-start(bf16[256,1792]{1,0:T(8,128)(2,1)} %get-tuple-element.118.refs_5_.refs_2_), channel_id=1, source_target_pairs={{0,1},{1,0},{2,3},{3,2},{4,5},{5,4},{6,7},{7,6}} | collective-permute-start | bytes 2752520 | tf_op jit(solution)/shard_map/ppermute | solution.py:45
  204.1 30.1 %collective-permute-start.13 = (bf16[256,1792]{1,0:T(8,128)(2,1)}, bf16[256,1792]{1,0:T(8,128)(2,1)}, u32[]{:S(2)}, u32[]{:S(2)}) collective-permute-start(bf16[256,1792]{1,0:T(8,128)(2,1)} %get-tuple-element.120.refs_3_), channel_id=1, source_target_pairs={{0,1},{1,0},{2,3},{3,2},{4,5},{5,4},{6,7},{7,6}} | collective-permute-start | bytes 2752520 | tf_op jit(solution)/shard_map/ppermute | solution.py:45
  233.1 2.8 collective-permute-start.24
  233.1 13.2 %collective-permute-start.15 = (bf16[128,4096]{1,0:T(8,128)(2,1)}, bf16[128,4096]{1,0:T(8,128)(2,1)}, u32[]{:S(2)}, u32[]{:S(2)}) collective-permute-start(bf16[128,4096]{1,0:T(8,128)(2,1)} %collective-permute-done.5.refs_0_.refs_7_), channel_id=1, source_target_pairs={{0,1},{1,0},{2,3},{3,2},{4,5},{5,4},{6,7},{7,6}} | collective-permute-start | bytes 3145736 | tf_op jit(solution)/shard_map/ppermute | solution.py:45
  233.6 13.1 %collective-permute-start.16 = (bf16[128,4096]{1,0:T(8,128)(2,1)}, bf16[128,4096]{1,0:T(8,128)(2,1)}, u32[]{:S(2)}, u32[]{:S(2)}) collective-permute-start(bf16[128,4096]{1,0:T(8,128)(2,1)} %collective-permute-done.7.refs_1_.refs_8_), channel_id=1, source_target_pairs={{0,1},{1,0},{2,3},{3,2},{4,5},{5,4},{6,7},{7,6}} | collective-permute-start | bytes 3145736 | tf_op jit(solution)/shard_map/ppermute | solution.py:45
  233.6 69.5 %collective-permute-start.22 = (bf16[512,4096]{1,0:T(8,128)(2,1)}, bf16[512,4096]{1,0:T(8,128)(2,1)}, u32[]{:S(2)}, u32[]{:S(2)}) collective-permute-start(bf16[512,4096]{1,0:T(8,128)(2,1)} %get-tuple-element.134.refs_1_), channel_id=1, source_target_pairs={{0,1},{1,0},{2,3},{3,2},{4,5},{5,4},{6,7},{7,6}} | collective-permute-start | bytes 12582920 | tf_op jit(solution)/shard_map/ppermute | solution.py:45
  234.1 12.1 %collective-permute-start.26 = (bf16[256,1792]{1,0:T(8,128)(2,1)}, bf16[256,1792]{1,0:T(8,128)(2,1)}, u32[]{:S(2)}, u32[]{:S(2)}) collective-permute-start(bf16[256,1792]{1,0:T(8,128)(2,1)} %get-tuple-element.138.refs_1_), channel_id=1, source_target_pairs={{0,1},{1,0},{2,3},{3,2},{4,5},{5,4},{6,7},{7,6}} | collective-permute-start | bytes 2752520 | tf_op jit(solution)/shard_map/ppermute | solution.py:45
  235.9 18.1 %collective-permute-start.25 = (bf16[512,1792]{1,0:T(8,128)(2,1)}, bf16[512,1792]{1,0:T(8,128)(2,1)}, u32[]{:S(2)}, u32[]{:S(2)}) collective-permute-start(bf16[512,1792]{1,0:T(8,128)(2,1)} %get-tuple-element.137.refs_1_), channel_id=1, source_target_pairs={{0,1},{1,0},{2,3},{3,2},{4,5},{5,4},{6,7},{7,6}} | collective-permute-start | bytes 5505032 | tf_op jit(solution)/shard_map/ppermute | solution.py:45
  246.2 4.1 collective-permute-start.17
  246.4 5.5 %collective-permute-start.18 = (bf16[128,4096]{1,0:T(8,128)(2,1)}, bf16[128,4096]{1,0:T(8,128)(2,1)}, u32[]{:S(2)}, u32[]{:S(2)}) collective-permute-start(bf16[128,4096]{1,0:T(8,128)(2,1)} %collective-permute-done.8.refs_3_.refs_10_), channel_id=1, source_target_pairs={{0,1},{1,0},{2,3},{3,2},{4,5},{5,4},{6,7},{7,6}} | collective-permute-start | bytes 3145736 | tf_op jit(solution)/shard_map/ppermute | solution.py:45
  246.7 6.6 %collective-permute-start.19 = (bf16[128,4096]{1,0:T(8,128)(2,1)}, bf16[128,4096]{1,0:T(8,128)(2,1)}, u32[]{:S(2)}, u32[]{:S(2)}) collective-permute-start(bf16[128,4096]{1,0:T(8,128)(2,1)} %collective-permute-done.9.refs_0_.refs_11_), channel_id=1, source_target_pairs={{0,1},{1,0},{2,3},{3,2},{4,5},{5,4},{6,7},{7,6}} | collective-permute-start | bytes 3145736 | tf_op jit(solution)/shard_map/ppermute | solution.py:45
  250.3 28.7 %collective-permute-start.21 = (bf16[256,4096]{1,0:T(8,128)(2,1)}, bf16[256,4096]{1,0:T(8,128)(2,1)}, u32[]{:S(2)}, u32[]{:S(2)}) collective-permute-start(bf16[256,4096]{1,0:T(8,128)(2,1)} %get-tuple-element.133.refs_0_), channel_id=1, source_target_pairs={{0,1},{1,0},{2,3},{3,2},{4,5},{5,4},{6,7},{7,6}} | collective-permute-start | bytes 6291464 | tf_op jit(solution)/shard_map/ppermute | solution.py:45
  251.8 27.2 %collective-permute-start.23 = (bf16[256,4096]{1,0:T(8,128)(2,1)}, bf16[256,4096]{1,0:T(8,128)(2,1)}, u32[]{:S(2)}, u32[]{:S(2)}) collective-permute-start(bf16[256,4096]{1,0:T(8,128)(2,1)} %get-tuple-element.135.refs_2_), channel_id=1, source_target_pairs={{0,1},{1,0},{2,3},{3,2},{4,5},{5,4},{6,7},{7,6}} | collective-permute-start | bytes 6291464 | tf_op jit(solution)/shard_map/ppermute | solution.py:45
  253.3 48.0 %collective-permute-start.27 = (f32[256,2048]{1,0:T(8,128)}, f32[256,2048]{1,0:T(8,128)}, u32[]{:S(2)}, u32[]{:S(2)}) collective-permute-start(f32[256,2048]{1,0:T(8,128)} %get-tuple-element.115.refs_3_), channel_id=1, source_target_pairs={{0,2},{1,3},{2,0},{3,1},{4,6},{5,7},{6,4},{7,5}} | collective-permute-start | bytes 6291464 | tf_op jit(solution)/shard_map/ppermute | solution.py:45
  254.0 47.7 %collective-permute-start.28 = (f32[256,2048]{1,0:T(8,128)}, f32[256,2048]{1,0:T(8,128)}, u32[]{:S(2)}, u32[]{:S(2)}) collective-permute-start(f32[256,2048]{1,0:T(8,128)} %get-tuple-element.142), channel_id=1, source_target_pairs={{0,4},{1,5},{2,6},{3,7},{4,0},{5,1},{6,2},{7,3}} | collective-permute-start | bytes 6291464 | tf_op jit(solution)/shard_map/ppermute | solution.py:45
  279.0 71.8 %collective-permute-start.12 = (bf16[512,1792]{1,0:T(8,128)(2,1)}, bf16[512,1792]{1,0:T(8,128)(2,1)}, u32[]{:S(2)}, u32[]{:S(2)}) collective-permute-start(bf16[512,1792]{1,0:T(8,128)(2,1)} %get-tuple-element.119.refs_1_), channel_id=1, source_target_pairs={{0,1},{1,0},{2,3},{3,2},{4,5},{5,4},{6,7},{7,6}} | collective-permute-start | bytes 5505032 | tf_op jit(solution)/shard_map/ppermute | solution.py:45
  279.1 72.3 %collective-permute-start.14 = (bf16[256,4096]{1,0:T(8,128)(2,1)}, bf16[256,4096]{1,0:T(8,128)(2,1)}, u32[]{:S(2)}, u32[]{:S(2)}) collective-permute-start(bf16[256,4096]{1,0:T(8,128)(2,1)} %dy_ref.1), channel_id=1, source_target_pairs={{0,1},{1,0},{2,3},{3,2},{4,5},{5,4},{6,7},{7,6}} | collective-permute-start | bytes 6291464 | tf_op jit(solution)/shard_map/ppermute | solution.py:45
  301.3 48.8 %collective-permute-start.20 = (bf16[128,4096]{1,0:T(8,128)(2,1)}, bf16[128,4096]{1,0:T(8,128)(2,1)}, u32[]{:S(2)}, u32[]{:S(2)}) collective-permute-start(bf16[128,4096]{1,0:T(8,128)(2,1)} %collective-permute-done.10.refs_1_.refs_12_), channel_id=1, source_target_pairs={{0,1},{1,0},{2,3},{3,2},{4,5},{5,4},{6,7},{7,6}} | collective-permute-start | bytes 3145736 | tf_op jit(solution)/shard_map/ppermute | solution.py:45
  301.7 51.1 %collective-permute-start.31 = (f32[256,2048]{1,0:T(8,128)}, f32[256,2048]{1,0:T(8,128)}, u32[]{:S(2)}, u32[]{:S(2)}) collective-permute-start(f32[256,2048]{1,0:T(8,128)} %get-tuple-element.139.refs_12_), channel_id=1, source_target_pairs={{0,2},{1,3},{2,0},{3,1},{4,6},{5,7},{6,4},{7,5}} | collective-permute-start | bytes 6291464 | tf_op jit(solution)/shard_map/ppermute | solution.py:45
  303.1 50.3 %collective-permute-start.32 = (f32[256,2048]{1,0:T(8,128)}, f32[256,2048]{1,0:T(8,128)}, u32[]{:S(2)}, u32[]{:S(2)}) collective-permute-start(f32[256,2048]{1,0:T(8,128)} %get-tuple-element.153), channel_id=1, source_target_pairs={{0,4},{1,5},{2,6},{3,7},{4,0},{5,1},{6,2},{7,3}} | collective-permute-start | bytes 6291464 | tf_op jit(solution)/shard_map/ppermute | solution.py:45
  350.1 56.2 %collective-permute-start.33 = (f32[256,2048]{1,0:T(8,128)}, f32[256,2048]{1,0:T(8,128)}, u32[]{:S(2)}, u32[]{:S(2)}) collective-permute-start(f32[256,2048]{1,0:T(8,128)} %get-tuple-element.107.refs_4_), channel_id=1, source_target_pairs={{0,2},{1,3},{2,0},{3,1},{4,6},{5,7},{6,4},{7,5}} | collective-permute-start | bytes 6291464 | tf_op jit(solution)/shard_map/ppermute | solution.py:45
  350.8 54.0 %collective-permute-start.30 = (f32[256,2048]{1,0:T(8,128)}, f32[256,2048]{1,0:T(8,128)}, u32[]{:S(2)}, u32[]{:S(2)}) collective-permute-start(f32[256,2048]{1,0:T(8,128)} %get-tuple-element.148), channel_id=1, source_target_pairs={{0,4},{1,5},{2,6},{3,7},{4,0},{5,1},{6,2},{7,3}} | collective-permute-start | bytes 6291464 | tf_op jit(solution)/shard_map/ppermute | solution.py:45
  351.4 93.2 %collective-permute-start.35 = (f32[256,2048]{1,0:T(8,128)}, f32[256,2048]{1,0:T(8,128)}, u32[]{:S(2)}, u32[]{:S(2)}) collective-permute-start(f32[256,2048]{1,0:T(8,128)} %get-tuple-element.158), channel_id=1, source_target_pairs={{0,4},{1,5},{2,6},{3,7},{4,0},{5,1},{6,2},{7,3}} | collective-permute-start | bytes 6291464 | tf_op jit(solution)/shard_map/ppermute | solution.py:45
  352.9 136.7 %collective-permute-start.34 = (f32[256,2048]{1,0:T(8,128)}, f32[256,2048]{1,0:T(8,128)}, u32[]{:S(2)}, u32[]{:S(2)}) collective-permute-start(f32[256,2048]{1,0:T(8,128)} %get-tuple-element.143.refs_20_), channel_id=1, source_target_pairs={{0,4},{1,5},{2,6},{3,7},{4,0},{5,1},{6,2},{7,3}} | collective-permute-start | bytes 6291464 | tf_op jit(solution)/shard_map/ppermute | solution.py:45
  353.4 154.2 %collective-permute-start.36 = (f32[256,2048]{1,0:T(8,128)}, f32[256,2048]{1,0:T(8,128)}, u32[]{:S(2)}, u32[]{:S(2)}) collective-permute-start(f32[256,2048]{1,0:T(8,128)} %get-tuple-element.144.refs_21_), channel_id=1, source_target_pairs={{0,2},{1,3},{2,0},{3,1},{4,6},{5,7},{6,4},{7,5}} | collective-permute-start | bytes 6291464 | tf_op jit(solution)/shard_map/ppermute | solution.py:45
  404.8 125.7 %collective-permute-start.45 = (f32[160,2048]{1,0:T(8,128)}, f32[160,2048]{1,0:T(8,128)}, u32[]{:S(2)}, u32[]{:S(2)}) collective-permute-start(f32[160,2048]{1,0:T(8,128)} %get-tuple-element.165), channel_id=1, source_target_pairs={{0,4},{1,5},{2,6},{3,7},{4,0},{5,1},{6,2},{7,3}} | collective-permute-start | bytes 3932168 | tf_op jit(solution)/shard_map/ppermute | solution.py:45
  406.4 125.6 %collective-permute-start.46 = (f32[160,2048]{1,0:T(8,128)}, f32[160,2048]{1,0:T(8,128)}, u32[]{:S(2)}, u32[]{:S(2)}) collective-permute-start(f32[160,2048]{1,0:T(8,128)} %get-tuple-element.166), channel_id=1, source_target_pairs={{0,2},{1,3},{2,0},{3,1},{4,6},{5,7},{6,4},{7,5}} | collective-permute-start | bytes 3932168 | tf_op jit(solution)/shard_map/ppermute | solution.py:45
  444.6 82.6 %collective-permute-start.43 = (f32[64,2048]{1,0:T(8,128)}, f32[64,2048]{1,0:T(8,128)}, u32[]{:S(2)}, u32[]{:S(2)}) collective-permute-start(f32[64,2048]{1,0:T(8,128)} %get-tuple-element.163), channel_id=1, source_target_pairs={{0,4},{1,5},{2,6},{3,7},{4,0},{5,1},{6,2},{7,3}} | collective-permute-start | bytes 1572872 | tf_op jit(solution)/shard_map/ppermute | solution.py:45
  489.5 39.6 %collective-permute-start.44 = (f32[64,2048]{1,0:T(8,128)}, f32[64,2048]{1,0:T(8,128)}, u32[]{:S(2)}, u32[]{:S(2)}) collective-permute-start(f32[64,2048]{1,0:T(8,128)} %get-tuple-element.164), channel_id=1, source_target_pairs={{0,2},{1,3},{2,0},{3,1},{4,6},{5,7},{6,4},{7,5}} | collective-permute-start | bytes 1572872 | tf_op jit(solution)/shard_map/ppermute | solution.py:45
  517.7 10.0 %collective-permute-start.39 = (f32[1,4096]{1,0:T(1,128)}, f32[1,4096]{1,0:T(1,128)S(1)}, u32[]{:S(2)}, u32[]{:S(2)}) collective-permute-start(f32[1,4096]{1,0:T(1,128)} %get-tuple-element.162), channel_id=1, source_target_pairs={{0,1},{1,0},{2,3},{3,2},{4,5},{5,4},{6,7},{7,6}} | collective-permute-start | bytes 49160 | tf_op jit(solution)/shard_map/ppermute | solution.py:45
  527.2 11.2 %collective-permute-start.37 = (f32[32,2048]{1,0:T(8,128)}, f32[32,2048]{1,0:T(8,128)}, u32[]{:S(2)}, u32[]{:S(2)}) collective-permute-start(f32[32,2048]{1,0:T(8,128)} %get-tuple-element.160), channel_id=1, source_target_pairs={{0,4},{1,5},{2,6},{3,7},{4,0},{5,1},{6,2},{7,3}} | collective-permute-start | bytes 786440 | tf_op jit(solution)/shard_map/ppermute | solution.py:45
  527.7 10.7 %collective-permute-start.38 = (f32[32,2048]{1,0:T(8,128)}, f32[32,2048]{1,0:T(8,128)}, u32[]{:S(2)}, u32[]{:S(2)}) collective-permute-start(f32[32,2048]{1,0:T(8,128)} %get-tuple-element.161), channel_id=1, source_target_pairs={{0,2},{1,3},{2,0},{3,1},{4,6},{5,7},{6,4},{7,5}} | collective-permute-start | bytes 786440 | tf_op jit(solution)/shard_map/ppermute | solution.py:45
  529.1 7.0 %copy-start = (f32[1,4096]{1,0:T(1,128)}, f32[1,4096]{1,0:T(1,128)S(1)}, u32[]{:S(2)}) copy-start(f32[1,4096]{1,0:T(1,128)S(1)} %add.3.refs_4_) | copy-start | bytes 49156
  529.1 9.2 %collective-permute-start.40 = (f32[1,4096]{1,0:T(1,128)S(1)}, f32[1,4096]{1,0:T(1,128)S(1)}, u32[]{:S(2)}, u32[]{:S(2)}) collective-permute-start(f32[1,4096]{1,0:T(1,128)S(1)} %add.3.refs_4_), channel_id=1, source_target_pairs={{0,2},{1,3},{2,0},{3,1},{4,6},{5,7},{6,4},{7,5}} | collective-permute-start | bytes 49160 | tf_op jit(solution)/shard_map/ppermute | solution.py:45
  530.5 7.9 %collective-permute-start.41 = (f32[1,4096]{1,0:T(1,128)S(1)}, f32[1,4096]{1,0:T(1,128)}, u32[]{:S(2)}, u32[]{:S(2)}) collective-permute-start(f32[1,4096]{1,0:T(1,128)S(1)} %add.3.refs_4_), channel_id=1, source_target_pairs={{0,4},{1,5},{2,6},{3,7},{4,0},{5,1},{6,2},{7,3}} | collective-permute-start | bytes 49160 | tf_op jit(solution)/shard_map/ppermute | solution.py:45
  532.0 6.4 %collective-permute-start.42 = (f32[1,4096]{1,0:T(1,128)S(1)}, f32[1,4096]{1,0:T(1,128)}, u32[]{:S(2)}, u32[]{:S(2)}) collective-permute-start(f32[1,4096]{1,0:T(1,128)S(1)} %add.3.refs_4_), channel_id=1, source_target_pairs={{0,6},{1,7},{2,4},{3,5},{4,2},{5,3},{6,0},{7,1}} | collective-permute-start | bytes 49160 | tf_op jit(solution)/shard_map/ppermute | solution.py:45
  538.3 0.6 copy-start.1

commit v4 on v3

--- a/solution.py
+++ b/solution.py
@@ -43,6 +43,10 @@
 
 def _swap(v, k):
     return lax.ppermute(v, "tp", [(i, i ^ k) for i in range(8)])
+
+
+def _cross(v, k):
+    return lax.ppermute(v, "tp", [(i, i ^ (k if i % 2 else k ^ DIAG)) for i in range(8)])
 
 
 def _cost(m, k, n, extra=0):
@@ -320,7 +324,7 @@
 
 
 def _near(v):
-    return _swap(v, XN), _swap(v, YN)
+    return _cross(v, XN), _cross(v, YN)
 
 
 def solution(mesh):
@@ -340,53 +344,53 @@
         (A0,) = _up([dY], [W2], NT, slopes=(s0,))
         H0p, s0p, _ = _up([X], [W1p], NN, gamma=gamma, after=(A0,))
         xx, xy = _tie((xx, xy), (H0p,))
-        xd = _swap(xx, YN)
+        xd = _cross(xx, YN)
         Hn, sn, Hnp, snp, Xn = _up([xx, xy], Ws1, NN, gamma=gamma, after=(H0p,))
         gx1, gy1 = _tie((gx1, gy1), (Hn,))
-        gd1 = _swap(gy1, XN)
+        gd1 = _cross(gy1, XN)
         (Yxa,), (Yya,) = _down([[Hn], [Hnp]], Ws2, NN, split=2, halves=(0,))
         gx2, gy2 = _tie((gx2, gy2), (Yxa,))
-        gd2 = _swap(gy2, XN)
+        gd2 = _cross(gy2, XN)
         (Yxb,), (Yyb,) = _down([[Hn], [Hnp]], Ws2, NN, split=2, halves=(1,), after=(Yxa,))
         Yx, Yy = (Yxa, Yxb), (Yya, Yyb)
-        sa = _swap(Yx[0], XN)
-        sb = _swap(Yy[1], YN)
+        sa = _cross(Yx[0], XN)
+        sb = _cross(Yy[1], YN)
         An, Anp = _up([gx1, gx2, gy1, gy2], Ws2, NT, slopes=(sn, snp), after=(Yxb,))
         Zx, Zy = _down([[An], [Anp]], Ws1, NT, split=2)
-        ra = _swap(Zx[0], XN)
-        rb = _swap(Zy[1], YN)
+        ra = _cross(Zx[0], XN)
+        rb = _cross(Zy[1], YN)
         Hd, sd, Hdp, sdp, Xd = _up([xd], Ws1, NN, gamma=gamma, after=(Zx[0],))
         Ad, Adp = _up([gd1, gd2], Ws2, NT, slopes=(sd, sdp))
         (Zd,) = _down([[Ad], [Adp]], Ws1, NT)
-        fa = _swap(Zd[0], XN)
-        fb = _swap(Zd[1], YN)
+        fa = _cross(Zd[0], XN)
+        fb = _cross(Zd[1], YN)
         (A0p,) = _up([dY], [W2p], NT, slopes=(s0p,), after=(Zd[0],))
         Y0, Yd = _down([[H0, Hd], [H0p, Hdp]], Ws2, NN, after=(A0p,))
-        ya = _swap(Yd[0], XN)
-        yb = _swap(Yd[1], YN)
+        ya = _cross(Yd[0], XN)
+        yb = _cross(Yd[1], YN)
         pair = lambda own, sent: own + [_swap(v, CORE) for v in _tie(sent, (Ad,))]
         dW1 = _grad(pair([X0, Xn, Xd], [X0, Xn, Xd]),
                       pair([A0, An, Ad], [A0p, Anp, Adp]), 512, after=(Yd[0],))
         Zx1, Zy0 = _tie((Zx[1], Zy[0]), (dW1,))
         far_a, far_b = _sums(((Zy0, fa), (Zx1, fb)), (n,), 64)
-        za = _swap(far_a, YN)
-        zb = _swap(far_b, XN)
+        za = _cross(far_a, YN)
+        zb = _cross(far_b, XN)
         Gs = [dY, gx1, gx2, gy1, gy2, gd1, gd2]
         dW2 = _grad(pair([H0, Hn, Hd], [H0p, Hnp, Hdp]),
                       pair(Gs, Gs), 256, after=(far_a, far_b))
         Yx1, Yy0, Y00, Y01, X = _tie((Yx[1], Yy[0], Y0[0], Y0[1], X), (dW2,))
         cuts = n * 5 // 8, n // 4, n // 8
         sums = _sums(((Yy0, ya), (Yx1, yb)), cuts, n // 8)
-        va, vb = _swap(sums[0], YN), _swap(sums[3], XN)
-        ua, ub = _swap(sums[1], YN), _swap(sums[4], XN)
+        va, vb = _cross(sums[0], YN), _cross(sums[3], XN)
+        ua, ub = _cross(sums[1], YN), _cross(sums[4], XN)
         base = _base(X, ((Y00, sa), (Y01, sb)))
         (Z0,) = _down([[A0], [A0p]], Ws1, NT, after=base)
         dX, dg = _dx(((Z0[0], ra, za), (Z0[1], rb, zb)), X, dY, gamma)
         dg = dg + _swap(dg, CORE)
         dgs = dg, _swap(dg, XN), _swap(dg, YN), _swap(dg, DIAG)
         last_a, last_b = _tie((sums[2], sums[5]), (dX,))
-        wa = _swap(last_a, YN)
-        wb = _swap(last_b, XN)
+        wa = _cross(last_a, YN)
+        wb = _cross(last_b, XN)
         Y = _finish(base, (va, vb), 0, None, n, cuts[0] // 2)
         Y = _finish(base, (ua, ub), cuts[0], Y, n, cuts[2])
         Y, dgamma = _finish(base, (wa, wb), cuts[0] + cuts[1], Y, n, cuts[2], dgs)

time: 542 us -> 515 us (0.950)
  waiting for transfers between devices: 138 us -> 108 us
    ppermute x47 -> x22, waiting for transfers between devices: 138 us -> 18.5 us  [_swap(): return lax.ppermute(v, 'tp', [(i, i ^ k) for i in range(8)])]
    ppermute x0 -> x25, waiting for transfers between devices: none -> 89.4 us  [_cross(): lax.ppermute(v, 'tp', [(i, i ^ (k if i % 2 else k ^ DIAG)) for i in range...]
    ppermute x0 -> x25, starting transfers between devices: none -> 27.3 us  [_cross(): lax.ppermute(v, 'tp', [(i, i ^ (k if i % 2 else k ^ DIAG)) for i in range...]
    ppermute x47 -> x22, starting transfers between devices: 33.6 us -> 8.82 us  [_swap(): return lax.ppermute(v, 'tp', [(i, i ^ k) for i in range(8)])]
  transfers between devices with their start and end apart: 47 -> 47, of which waited for: 13 -> 12; matrix products, arithmetic and copies ran while one was open for 0% -> 0% of each run, Pallas kernels for 68% -> 71%
where the time goes in v4:
time: 515 us; the launch traced here: 514 us
  Pallas kernels  368 us (71%)
  waiting for transfers between devices  108 us (21%)
  starting transfers between devices  36.1 us (7%)
    pallas_call x8, Pallas kernels, _up(): pl.pallas_call(body, grid=(F // tile,), in_specs=[pl.BlockSpec(p.shape, l...  139 us
    pallas_call x6, Pallas kernels, _down(): pl.pallas_call(body, grid=(steps,), in_specs=[pl.BlockSpec(p.shape, lambd...  106 us
    ppermute x25, waiting for transfers between devices, _cross(): lax.ppermute(v, 'tp', [(i, i ^ (k if i % 2 else k ^ DIAG)) for i in range...  89.4 us
    pallas_call x2, Pallas kernels, _grad(): pl.pallas_call(body, grid=(M // tile,), in_specs=[pl.BlockSpec((p.shape[0...  81.9 us
    ppermute x25, starting transfers between devices, _cross(): lax.ppermute(v, 'tp', [(i, i ^ (k if i % 2 else k ^ DIAG)) for i in range...  27.3 us
    ppermute x22, waiting for transfers between devices, _swap(): return lax.ppermute(v, 'tp', [(i, i ^ k) for i in range(8)])  18.5 us
    pallas_call x2, Pallas kernels, _sums(): pl.pallas_call(body, grid=(n // tile,), in_specs=[spec] * (2 * len(pairs)...  13.7 us
  transfers between devices with their start and end apart: 47, of which 12 were waited for; matrix products, arithmetic and copies ran while one was open for 0% of the time, Pallas kernels for 71%

profile of v4, /device:TPU:0, one launch (start us, length us, event | category | flops | bytes accessed | tf_op | source)
XLA Modules:
  0.0 513.7 jit_solution(9241994599229200852)
XLA Ops:
  0.6 0.9 collective-permute-start.2
  1.5 3.0 collective-permute-start
  4.5 1.5 collective-permute-start.1
  6.0 2.9 halves.1
  8.9 0.5 collective-permute-start.5
  9.4 13.5 %up_A.4 = (bf16[256,1792]{1,0:T(8,128)(2,1)}, f32[256,1792]{1,0:T(8,128)}, bf16[256,4096]{1,0:T(8,128)(2,1)}) custom-call(bf16[256,4096]{1,0:T(8,128)(2,1)} %x_ref.1, bf16[4096,1792]{1,0:T(8,128)(2,1)} %refs_2_.13, f32[1,4096]{1,0:T(1,128)} %bitcast.2), custom_call_target="tpu_custom_call" | custom-call | flops 3758096384 | bytes 16777216 | tf_op jit(solution)/shard_map/up_A/pallas_call | solution.py:116
  23.0 11.7 %up_dA.4.refs_3_.refs_6_.refs_0_ = bf16[256,1792]{1,0:T(8,128)(2,1)} custom-call(bf16[256,4096]{1,0:T(8,128)(2,1)} %dy_ref.1, bf16[1792,4096]{1,0:T(8,128)(2,1)} %refs_4_.3, f32[256,1792]{1,0:T(8,128)} %get-tuple-element.87.refs_2_), custom_call_target="tpu_custom_call" | custom-call | flops 3758096384 | bytes 16777216 | tf_op jit(solution)/shard_map/up_dA/pallas_call | solution.py:116
  34.7 13.6 %up_A.5 = (bf16[256,1792]{1,0:T(8,128)(2,1)}, f32[256,1792]{1,0:T(8,128)}, bf16[256,4096]{1,0:T(8,128)(2,1)}) custom-call(bf16[256,4096]{1,0:T(8,128)(2,1)} %x_ref.1, bf16[4096,1792]{1,0:T(8,128)(2,1)} %collective-permute-done.2.refs_1_.refs_3_.refs_2_, f32[1,4096]{1,0:T(1,128)} %bitcast.3, bf16[256,1792]{1,0:T(8,128)(2,1)} %up_dA.4.refs_3_.refs_6_.refs_0_), custom_call_target="tpu_custom_call" | custom-call | flops 3758096384 | bytes 16777216 | tf_op jit(solution)/shard_map/up_A/pallas_call | solution.py:116
  48.3 2.3 collective-permute-done.refs_0_
  50.6 2.5 collective-permute-start.7
  53.3 1.5 collective-permute-start.8
  54.8 27.8 %up_A.6 = (bf16[512,1792]{1,0:T(8,128)(2,1)}, f32[512,1792]{1,0:T(8,128)}, bf16[512,1792]{1,0:T(8,128)(2,1)}, f32[512,1792]{1,0:T(8,128)}, bf16[512,4096]{1,0:T(8,128)(2,1)}) custom-call(bf16[256,4096]{1,0:T(8,128)(2,1)} %collective-permute-done.refs_0_, bf16[256,4096]{1,0:T(8,128)(2,1)} %collective-permute-done.1.refs_1_, bf16[4096,1792]{1,0:T(8,128)(2,1)} %refs_2_.13, ...), custom_call_target="tpu_custom_call" | custom-call | flops 15032385536 | bytes 33554432 | tf_op jit(solution)/shard_map/up_A/pallas_call | solution.py:116
  82.7 0.6 collective-permute-start.4
  83.2 13.1 %down.6 = (f32[256,2048]{1,0:T(8,128)}, f32[256,2048]{1,0:T(8,128)}) custom-call(bf16[512,1792]{1,0:T(8,128)(2,1)} %get-tuple-element.91.refs_0_.refs_1_, bf16[512,1792]{1,0:T(8,128)(2,1)} %get-tuple-element.119.refs_1_, bf16[1792,4096]{1,0:T(8,128)(2,1)} %refs_4_.3, bf16[1792,4096]{1,0:T(8,128)(2,1)} %collective-permute-done.3.refs_3_.refs_5_.refs_1_), custom_call_target="tpu_custom_call" | custom-call | flops 7516192768 | bytes 22544384 | tf_op jit(solution)/shard_map/down/pallas_call | solution.py:159
  96.3 2.0 collective-permute-start.9
  98.4 13.2 %down.7 = (f32[256,2048]{1,0:T(8,128)}, f32[256,2048]{1,0:T(8,128)}) custom-call(bf16[512,1792]{1,0:T(8,128)(2,1)} %get-tuple-element.91.refs_0_.refs_1_, bf16[512,1792]{1,0:T(8,128)(2,1)} %get-tuple-element.119.refs_1_, bf16[1792,4096]{1,0:T(8,128)(2,1)} %refs_4_.3, bf16[1792,4096]{1,0:T(8,128)(2,1)} %collective-permute-done.3.refs_3_.refs_5_.refs_1_, ...), custom_call_target="tpu_custom_call" | custom-call | flops 7516192768 | bytes 22544384 | tf_op jit(solution)/shard_map/down/pallas_call | solution.py:159
  111.6 23.1 %up_dA.5 = (bf16[512,1792]{1,0:T(8,128)(2,1)}, bf16[512,1792]{1,0:T(8,128)(2,1)}) custom-call(bf16[128,4096]{1,0:T(8,128)(2,1)} %collective-permute-done.5.refs_0_.refs_7_, bf16[128,4096]{1,0:T(8,128)(2,1)} %collective-permute-done.7.refs_1_.refs_8_, bf16[128,4096]{1,0:T(8,128)(2,1)} %collective-permute-done.6.refs_2_.refs_9_, ...), custom_call_target="tpu_custom_call" | custom-call | flops 15032385536 | bytes 33554432 | tf_op jit(solution)/shard_map/up_dA/pallas_call | solution.py:116
  134.7 22.8 %down.8 = (f32[256,2048]{1,0:T(8,128)}, f32[256,2048]{1,0:T(8,128)}, f32[256,2048]{1,0:T(8,128)}, f32[256,2048]{1,0:T(8,128)}) custom-call(bf16[512,1792]{1,0:T(8,128)(2,1)} %get-tuple-element.105.refs_0_.refs_7_, bf16[512,1792]{1,0:T(8,128)(2,1)} %get-tuple-element.137.refs_1_, bf16[4096,1792]{1,0:T(8,128)(2,1)} %refs_2_.13, ...), custom_call_target="tpu_custom_call" | custom-call | flops 15032385536 | bytes 41418752 | tf_op jit(solution)/shard_map/down/pallas_call | solution.py:159
  157.5 20.1 %up_A.7 = (bf16[256,1792]{1,0:T(8,128)(2,1)}, f32[256,1792]{1,0:T(8,128)}, bf16[256,1792]{1,0:T(8,128)(2,1)}, f32[256,1792]{1,0:T(8,128)}, bf16[256,4096]{1,0:T(8,128)(2,1)}) custom-call(bf16[256,4096]{1,0:T(8,128)(2,1)} %collective-permute-done.4.refs_0_, bf16[4096,1792]{1,0:T(8,128)(2,1)} %refs_2_.13, ...), custom_call_target="tpu_custom_call" | custom-call | flops 7516192768 | bytes 31457280 | tf_op jit(solution)/shard_map/up_A/pallas_call | solution.py:116
  177.6 17.6 %up_dA.6 = (bf16[256,1792]{1,0:T(8,128)(2,1)}, bf16[256,1792]{1,0:T(8,128)(2,1)}) custom-call(bf16[128,4096]{1,0:T(8,128)(2,1)} %collective-permute-done.9.refs_0_.refs_11_, bf16[128,4096]{1,0:T(8,128)(2,1)} %collective-permute-done.10.refs_1_.refs_12_, bf16[1792,4096]{1,0:T(8,128)(2,1)} %refs_4_.3, ...), custom_call_target="tpu_custom_call" | custom-call | flops 7516192768 | bytes 31457280 | tf_op jit(solution)/shard_map/up_dA/pallas_call | solution.py:116
  195.1 0.5 collective-permute-start.13
  195.6 16.8 %down.9 = (f32[256,2048]{1,0:T(8,128)}, f32[256,2048]{1,0:T(8,128)}) custom-call(bf16[256,1792]{1,0:T(8,128)(2,1)} %get-tuple-element.113.refs_0_.refs_8_, bf16[256,1792]{1,0:T(8,128)(2,1)} %get-tuple-element.138.refs_1_, bf16[4096,1792]{1,0:T(8,128)(2,1)} %refs_2_.13, bf16[4096,1792]{1,0:T(8,128)(2,1)} %collective-permute-done.2.refs_1_.refs_3_.refs_2_), custom_call_target="tpu_custom_call" | custom-call | flops 7516192768 | bytes 35389440 | tf_op jit(solution)/shard_map/down/pallas_call | solution.py:159
  212.4 11.7 %up_dA.7.refs_6_.refs_1_ = bf16[256,1792]{1,0:T(8,128)(2,1)} custom-call(bf16[256,4096]{1,0:T(8,128)(2,1)} %dy_ref.1, bf16[1792,4096]{1,0:T(8,128)(2,1)} %collective-permute-done.3.refs_3_.refs_5_.refs_1_, f32[256,1792]{1,0:T(8,128)} %get-tuple-element.110.refs_2_, f32[256,2048]{1,0:T(8,128)} %get-tuple-element.115.refs_3_), custom_call_target="tpu_custom_call" | custom-call | flops 3758096384 | bytes 16777216 | tf_op jit(solution)/shard_map/up_dA/pallas_call | solution.py:116
  224.2 0.5 collective-permute-start.15
  224.7 0.5 collective-permute-start.22
  225.2 1.8 collective-permute-done.24.refs_9_
  227.1 10.2 %collective-permute-done.26.refs_11_ = bf16[256,1792]{1,0:T(8,128)(2,1)} collective-permute-done((bf16[256,1792]{1,0:T(8,128)(2,1)}, bf16[256,1792]{1,0:T(8,128)(2,1)}, u32[]{:S(2)}, u32[]{:S(2)}) %collective-permute-start.26) | collective-permute-done | bytes 917536 | tf_op jit(solution)/shard_map/ppermute | solution.py:45
  237.4 0.4 collective-permute-start.18
  237.9 3.5 collective-permute-done.17.refs_16_
  241.6 1.4 collective-permute-done.18.refs_17_
  243.1 1.4 collective-permute-done.19.refs_18_
  244.4 2.0 collective-permute-start.27
  246.4 1.5 collective-permute-start.28
  247.9 23.5 %down.10 = (f32[256,2048]{1,0:T(8,128)}, f32[256,2048]{1,0:T(8,128)}, f32[256,2048]{1,0:T(8,128)}, f32[256,2048]{1,0:T(8,128)}) custom-call(bf16[256,1792]{1,0:T(8,128)(2,1)} %get-tuple-element.96.refs_0_, bf16[256,1792]{1,0:T(8,128)(2,1)} %get-tuple-element.108.refs_1_.refs_2_, bf16[256,1792]{1,0:T(8,128)(2,1)} %get-tuple-element.118.refs_5_.refs_2_, ...), custom_call_target="tpu_custom_call" | custom-call | flops 15032385536 | bytes 41418752 | tf_op jit(solution)/shard_map/down/pallas_call | solution.py:159
  271.4 0.5 collective-permute-start.14
  271.9 20.5 %collective-permute-done.27.refs_1_ = f32[256,2048]{1,0:T(8,128)} collective-permute-done((f32[256,2048]{1,0:T(8,128)}, f32[256,2048]{1,0:T(8,128)}, u32[]{:S(2)}, u32[]{:S(2)}) %collective-permute-start.27) | collective-permute-done | bytes 2097184 | tf_op jit(solution)/shard_map/ppermute | solution.py:49
  292.6 2.2 collective-permute-start.31
  294.9 1.3 collective-permute-start.32
  296.2 39.7 %shard_map.92 = f32[4096,1792]{1,0:T(8,128)} custom-call(bf16[256,4096]{1,0:T(8,128)(2,1)} %get-tuple-element.133.refs_0_, bf16[512,4096]{1,0:T(8,128)(2,1)} %get-tuple-element.134.refs_1_, bf16[256,4096]{1,0:T(8,128)(2,1)} %get-tuple-element.135.refs_2_, bf16[256,4096]{1,0:T(8,128)(2,1)} %collective-permute-done.21.refs_3_, ...), custom_call_target="tpu_custom_call" | custom-call | flops 30064771072 | bytes 53477376 | tf_op jit(solution)/shard_map/pallas_call | solution.py:185
  335.9 5.8 %shard_map.93 = (f32[256,2048]{1,0:T(8,128)}, f32[256,2048]{1,0:T(8,128)}) custom-call(f32[256,2048]{1,0:T(8,128)} %get-tuple-element.140.refs_0_, f32[256,2048]{1,0:T(8,128)} %collective-permute-done.27.refs_1_, f32[256,2048]{1,0:T(8,128)} %get-tuple-element.141.refs_2_, f32[256,2048]{1,0:T(8,128)} %collective-permute-done.28.refs_3_), custom_call_target="tpu_custom_call" | custom-call | flops 1048576 | bytes 12582912 | tf_op jit(solution)/shard_map/pallas_call | solution.py:240
  342.0 0.5 collective-permute-start.30
  342.5 1.5 collective-permute-start.35
  344.0 0.5 collective-permute-start.34
  344.5 2.0 collective-permute-start.36
  346.5 42.2 %shard_map.94 = f32[1792,4096]{1,0:T(8,128)} custom-call(bf16[256,1792]{1,0:T(8,128)(2,1)} %get-tuple-element.96.refs_0_, bf16[512,1792]{1,0:T(8,128)(2,1)} %get-tuple-element.91.refs_0_.refs_1_, bf16[256,1792]{1,0:T(8,128)(2,1)} %get-tuple-element.108.refs_1_.refs_2_, bf16[256,1792]{1,0:T(8,128)(2,1)} %collective-permute-done.11.refs_3_, ...), custom_call_target="tpu_custom_call" | custom-call | flops 30064771072 | bytes 53477376 | tf_op jit(solution)/shard_map/pallas_call | solution.py:185
  388.7 7.9 %shard_map.95 = (f32[160,2048]{1,0:T(8,128)}, f32[64,2048]{1,0:T(8,128)}, f32[32,2048]{1,0:T(8,128)}, f32[160,2048]{1,0:T(8,128)}, f32[64,2048]{1,0:T(8,128)}, /*index=5*/f32[32,2048]{1,0:T(8,128)}) custom-call(f32[256,2048]{1,0:T(8,128)} %get-tuple-element.151.refs_0_, f32[256,2048]{1,0:T(8,128)} %collective-permute-done.31.refs_1_, ...), custom_call_target="tpu_custom_call" | custom-call | flops 1048576 | bytes 12582912 | tf_op jit(solution)/shard_map/pallas_call | solution.py:240
  396.6 1.3 collective-permute-start.45
  398.2 6.2 %base.1 = (f32[256,2048]{1,0:T(8,128)}, f32[256,2048]{1,0:T(8,128)}) custom-call(bf16[256,4096]{1,0:T(8,128)(2,1)} %x_ref.1, f32[256,2048]{1,0:T(8,128)} %get-tuple-element.146.refs_0_, f32[256,2048]{1,0:T(8,128)} %collective-permute-done.29.refs_1_, f32[256,2048]{1,0:T(8,128)} %get-tuple-element.147.refs_2_, f32[256,2048]{1,0:T(8,128)} %collective-permute-done.30.refs_3_), custom_call_target="tpu_custom_call" | custom-call | flops 2097152 | bytes 14680064 | tf_op jit(solution)/shard_map/base/pallas_call | solution.py:257
  404.4 31.3 %collective-permute-done.35.refs_4_ = f32[256,2048]{1,0:T(8,128)} collective-permute-done((f32[256,2048]{1,0:T(8,128)}, f32[256,2048]{1,0:T(8,128)}, u32[]{:S(2)}, u32[]{:S(2)}) %collective-permute-start.35) | collective-permute-done | bytes 2097184 | tf_op jit(solution)/shard_map/ppermute | solution.py:49
  435.8 0.5 collective-permute-start.43
  436.2 34.7 %collective-permute-done.34.refs_2_ = f32[256,2048]{1,0:T(8,128)} collective-permute-done((f32[256,2048]{1,0:T(8,128)}, f32[256,2048]{1,0:T(8,128)}, u32[]{:S(2)}, u32[]{:S(2)}) %collective-permute-start.34) | collective-permute-done | bytes 2097184 | tf_op jit(solution)/shard_map/ppermute | solution.py:49
  471.3 16.8 %down.11 = (f32[256,2048]{1,0:T(8,128)}, f32[256,2048]{1,0:T(8,128)}) custom-call(bf16[256,1792]{1,0:T(8,128)(2,1)} %up_dA.4.refs_3_.refs_6_.refs_0_, bf16[256,1792]{1,0:T(8,128)(2,1)} %up_dA.7.refs_6_.refs_1_, bf16[4096,1792]{1,0:T(8,128)(2,1)} %refs_2_.13, bf16[4096,1792]{1,0:T(8,128)(2,1)} %collective-permute-done.2.refs_1_.refs_3_.refs_2_, ...), custom_call_target="tpu_custom_call" | custom-call | flops 7516192768 | bytes 35389440 | tf_op jit(solution)/shard_map/down/pallas_call | solution.py:159
  488.0 10.0 %dx.1 = (bf16[256,4096]{1,0:T(8,128)(2,1)}, f32[1,4096]{1,0:T(1,128)}) custom-call(bf16[256,4096]{1,0:T(8,128)(2,1)} %x_ref.1, bf16[256,4096]{1,0:T(8,128)(2,1)} %dy_ref.1, f32[1,4096]{1,0:T(1,128)} %bitcast.6, f32[256,2048]{1,0:T(8,128)} %get-tuple-element.156.refs_0_, f32[256,2048]{1,0:T(8,128)} %collective-permute-done.33.refs_1_, ...), custom_call_target="tpu_custom_call" | custom-call | flops 20971520 | bytes 18874368 | tf_op jit(solution)/shard_map/dx/pallas_call | solution.py:294
  498.1 1.3 collective-permute-start.39
  499.4 0.7 collective-permute-start.37
  500.4 0.8 collective-permute-start.38
  501.2 0.7 add.3.refs_4_
  502.0 0.8 collective-permute-start.40
  502.7 1.5 collective-permute-start.41
  504.2 1.3 collective-permute-start.42
  505.5 3.4 finish.3.refs_4_
  508.9 2.3 finish.4.refs_8_
  511.2 0.6 copy-done.1
  511.8 2.0 finish.5
  (59 shorter events, 2.7 us)
Async XLA Ops:
  0.6 34.0 %collective-permute-start.2 = (bf16[4096,1792]{1,0:T(8,128)(2,1)}, bf16[4096,1792]{1,0:T(8,128)(2,1)}, u32[]{:S(2)}, u32[]{:S(2)}) collective-permute-start(bf16[4096,1792]{1,0:T(8,128)(2,1)} %refs_2_.13), channel_id=1, source_target_pairs={{0,1},{1,0},{2,3},{3,2},{4,5},{5,4},{6,7},{7,6}} | collective-permute-start | bytes 44040200 | tf_op jit(solution)/shard_map/ppermute | solution.py:45
  1.5 81.7 %collective-permute-start.3 = (bf16[1792,4096]{1,0:T(8,128)(2,1)}, bf16[1792,4096]{1,0:T(8,128)(2,1)}, u32[]{:S(2)}, u32[]{:S(2)}) collective-permute-start(bf16[1792,4096]{1,0:T(8,128)(2,1)} %refs_4_.3), channel_id=1, source_target_pairs={{0,1},{1,0},{2,3},{3,2},{4,5},{5,4},{6,7},{7,6}} | collective-permute-start | bytes 44040200 | tf_op jit(solution)/shard_map/ppermute | solution.py:45
  1.5 49.0 %collective-permute-start = (bf16[256,4096]{1,0:T(8,128)(2,1)}, bf16[256,4096]{1,0:T(8,128)(2,1)}, u32[]{:S(2)}, u32[]{:S(2)}) collective-permute-start(bf16[256,4096]{1,0:T(8,128)(2,1)} %x_ref.1), channel_id=1, source_target_pairs={{0,4},{1,3},{2,6},{3,1},{4,0},{5,7},{6,2},{7,5}} | collective-permute-start | bytes 6291464 | tf_op jit(solution)/shard_map/ppermute | solution.py:49
  4.5 48.8 %collective-permute-start.1 = (bf16[256,4096]{1,0:T(8,128)(2,1)}, bf16[256,4096]{1,0:T(8,128)(2,1)}, u32[]{:S(2)}, u32[]{:S(2)}) collective-permute-start(bf16[256,4096]{1,0:T(8,128)(2,1)} %x_ref.1), channel_id=1, source_target_pairs={{0,2},{1,5},{2,0},{3,7},{4,6},{5,1},{6,4},{7,3}} | collective-permute-start | bytes 6291464 | tf_op jit(solution)/shard_map/ppermute | solution.py:49
  8.9 73.7 %collective-permute-start.5 = (bf16[128,4096]{1,0:T(8,128)(2,1)}, bf16[128,4096]{1,0:T(8,128)(2,1)}, u32[]{:S(2)}, u32[]{:S(2)}) collective-permute-start(bf16[128,4096]{1,0:T(8,128)(2,1)} %get-tuple-element.97), channel_id=1, source_target_pairs={{0,4},{1,3},{2,6},{3,1},{4,0},{5,7},{6,2},{7,5}} | collective-permute-start | bytes 3145736 | tf_op jit(solution)/shard_map/ppermute | solution.py:49
  34.7 48.5 %collective-permute-start.6 = (bf16[128,4096]{1,0:T(8,128)(2,1)}, bf16[128,4096]{1,0:T(8,128)(2,1)}, u32[]{:S(2)}, u32[]{:S(2)}) collective-permute-start(bf16[128,4096]{1,0:T(8,128)(2,1)} %get-tuple-element.97), channel_id=1, source_target_pairs={{0,2},{1,5},{2,0},{3,7},{4,6},{5,1},{6,4},{7,3}} | collective-permute-start | bytes 3145736 | tf_op jit(solution)/shard_map/ppermute | solution.py:49
  50.6 45.8 %collective-permute-start.7 = (bf16[128,4096]{1,0:T(8,128)(2,1)}, bf16[128,4096]{1,0:T(8,128)(2,1)}, u32[]{:S(2)}, u32[]{:S(2)}) collective-permute-start(bf16[128,4096]{1,0:T(8,128)(2,1)} %get-tuple-element.99), channel_id=1, source_target_pairs={{0,4},{1,3},{2,6},{3,1},{4,0},{5,7},{6,2},{7,5}} | collective-permute-start | bytes 3145736 | tf_op jit(solution)/shard_map/ppermute | solution.py:49
  53.3 43.0 %collective-permute-start.8 = (bf16[128,4096]{1,0:T(8,128)(2,1)}, bf16[128,4096]{1,0:T(8,128)(2,1)}, u32[]{:S(2)}, u32[]{:S(2)}) collective-permute-start(bf16[128,4096]{1,0:T(8,128)(2,1)} %get-tuple-element.99), channel_id=1, source_target_pairs={{0,2},{1,5},{2,0},{3,7},{4,6},{5,1},{6,4},{7,3}} | collective-permute-start | bytes 3145736 | tf_op jit(solution)/shard_map/ppermute | solution.py:49
  82.7 74.8 %collective-permute-start.4 = (bf16[256,4096]{1,0:T(8,128)(2,1)}, bf16[256,4096]{1,0:T(8,128)(2,1)}, u32[]{:S(2)}, u32[]{:S(2)}) collective-permute-start(bf16[256,4096]{1,0:T(8,128)(2,1)} %collective-permute-done.refs_0_), channel_id=1, source_target_pairs={{0,2},{1,5},{2,0},{3,7},{4,6},{5,1},{6,4},{7,3}} | collective-permute-start | bytes 6291464 | tf_op jit(solution)/shard_map/ppermute | solution.py:49
  96.3 128.4 %collective-permute-start.29 = (f32[256,2048]{1,0:T(8,128)}, f32[256,2048]{1,0:T(8,128)}, u32[]{:S(2)}, u32[]{:S(2)}) collective-permute-start(f32[256,2048]{1,0:T(8,128)} %get-tuple-element.93.refs_4_), channel_id=1, source_target_pairs={{0,4},{1,3},{2,6},{3,1},{4,0},{5,7},{6,2},{7,5}} | collective-permute-start | bytes 6291464 | tf_op jit(solution)/shard_map/ppermute | solution.py:49
  96.3 81.2 %collective-permute-start.9 = (bf16[128,4096]{1,0:T(8,128)(2,1)}, bf16[128,4096]{1,0:T(8,128)(2,1)}, u32[]{:S(2)}, u32[]{:S(2)}) collective-permute-start(bf16[128,4096]{1,0:T(8,128)(2,1)} %collective-permute-done.6.refs_2_.refs_9_), channel_id=1, source_target_pairs={{0,4},{1,3},{2,6},{3,1},{4,0},{5,7},{6,2},{7,5}} | collective-permute-start | bytes 3145736 | tf_op jit(solution)/shard_map/ppermute | solution.py:49
  98.4 79.2 %collective-permute-start.10 = (bf16[128,4096]{1,0:T(8,128)(2,1)}, bf16[128,4096]{1,0:T(8,128)(2,1)}, u32[]{:S(2)}, u32[]{:S(2)}) collective-permute-start(bf16[128,4096]{1,0:T(8,128)(2,1)} %collective-permute-done.8.refs_3_.refs_10_), channel_id=1, source_target_pairs={{0,4},{1,3},{2,6},{3,1},{4,0},{5,7},{6,2},{7,5}} | collective-permute-start | bytes 3145736 | tf_op jit(solution)/shard_map/ppermute | solution.py:49
  195.1 29.6 %collective-permute-start.11 = (bf16[256,1792]{1,0:T(8,128)(2,1)}, bf16[256,1792]{1,0:T(8,128)(2,1)}, u32[]{:S(2)}, u32[]{:S(2)}) collective-permute-start(bf16[256,1792]{1,0:T(8,128)(2,1)} %get-tuple-element.118.refs_5_.refs_2_), channel_id=1, source_target_pairs={{0,1},{1,0},{2,3},{3,2},{4,5},{5,4},{6,7},{7,6}} | collective-permute-start | bytes 2752520 | tf_op jit(solution)/shard_map/ppermute | solution.py:45
  195.1 30.1 %collective-permute-start.13 = (bf16[256,1792]{1,0:T(8,128)(2,1)}, bf16[256,1792]{1,0:T(8,128)(2,1)}, u32[]{:S(2)}, u32[]{:S(2)}) collective-permute-start(bf16[256,1792]{1,0:T(8,128)(2,1)} %get-tuple-element.120.refs_3_), channel_id=1, source_target_pairs={{0,1},{1,0},{2,3},{3,2},{4,5},{5,4},{6,7},{7,6}} | collective-permute-start | bytes 2752520 | tf_op jit(solution)/shard_map/ppermute | solution.py:45
  224.2 2.8 collective-permute-start.24
  224.2 13.2 %collective-permute-start.15 = (bf16[128,4096]{1,0:T(8,128)(2,1)}, bf16[128,4096]{1,0:T(8,128)(2,1)}, u32[]{:S(2)}, u32[]{:S(2)}) collective-permute-start(bf16[128,4096]{1,0:T(8,128)(2,1)} %collective-permute-done.5.refs_0_.refs_7_), channel_id=1, source_target_pairs={{0,1},{1,0},{2,3},{3,2},{4,5},{5,4},{6,7},{7,6}} | collective-permute-start | bytes 3145736 | tf_op jit(solution)/shard_map/ppermute | solution.py:45
  224.7 13.1 %collective-permute-start.16 = (bf16[128,4096]{1,0:T(8,128)(2,1)}, bf16[128,4096]{1,0:T(8,128)(2,1)}, u32[]{:S(2)}, u32[]{:S(2)}) collective-permute-start(bf16[128,4096]{1,0:T(8,128)(2,1)} %collective-permute-done.7.refs_1_.refs_8_), channel_id=1, source_target_pairs={{0,1},{1,0},{2,3},{3,2},{4,5},{5,4},{6,7},{7,6}} | collective-permute-start | bytes 3145736 | tf_op jit(solution)/shard_map/ppermute | solution.py:45
  224.7 70.1 %collective-permute-start.22 = (bf16[512,4096]{1,0:T(8,128)(2,1)}, bf16[512,4096]{1,0:T(8,128)(2,1)}, u32[]{:S(2)}, u32[]{:S(2)}) collective-permute-start(bf16[512,4096]{1,0:T(8,128)(2,1)} %get-tuple-element.134.refs_1_), channel_id=1, source_target_pairs={{0,1},{1,0},{2,3},{3,2},{4,5},{5,4},{6,7},{7,6}} | collective-permute-start | bytes 12582920 | tf_op jit(solution)/shard_map/ppermute | solution.py:45
  225.2 12.1 %collective-permute-start.26 = (bf16[256,1792]{1,0:T(8,128)(2,1)}, bf16[256,1792]{1,0:T(8,128)(2,1)}, u32[]{:S(2)}, u32[]{:S(2)}) collective-permute-start(bf16[256,1792]{1,0:T(8,128)(2,1)} %get-tuple-element.138.refs_1_), channel_id=1, source_target_pairs={{0,1},{1,0},{2,3},{3,2},{4,5},{5,4},{6,7},{7,6}} | collective-permute-start | bytes 2752520 | tf_op jit(solution)/shard_map/ppermute | solution.py:45
  227.0 19.4 %collective-permute-start.25 = (bf16[512,1792]{1,0:T(8,128)(2,1)}, bf16[512,1792]{1,0:T(8,128)(2,1)}, u32[]{:S(2)}, u32[]{:S(2)}) collective-permute-start(bf16[512,1792]{1,0:T(8,128)(2,1)} %get-tuple-element.137.refs_1_), channel_id=1, source_target_pairs={{0,1},{1,0},{2,3},{3,2},{4,5},{5,4},{6,7},{7,6}} | collective-permute-start | bytes 5505032 | tf_op jit(solution)/shard_map/ppermute | solution.py:45
  237.3 4.1 collective-permute-start.17
  237.4 5.5 %collective-permute-start.18 = (bf16[128,4096]{1,0:T(8,128)(2,1)}, bf16[128,4096]{1,0:T(8,128)(2,1)}, u32[]{:S(2)}, u32[]{:S(2)}) collective-permute-start(bf16[128,4096]{1,0:T(8,128)(2,1)} %collective-permute-done.8.refs_3_.refs_10_), channel_id=1, source_target_pairs={{0,1},{1,0},{2,3},{3,2},{4,5},{5,4},{6,7},{7,6}} | collective-permute-start | bytes 3145736 | tf_op jit(solution)/shard_map/ppermute | solution.py:45
  237.8 6.6 %collective-permute-start.19 = (bf16[128,4096]{1,0:T(8,128)(2,1)}, bf16[128,4096]{1,0:T(8,128)(2,1)}, u32[]{:S(2)}, u32[]{:S(2)}) collective-permute-start(bf16[128,4096]{1,0:T(8,128)(2,1)} %collective-permute-done.9.refs_0_.refs_11_), channel_id=1, source_target_pairs={{0,1},{1,0},{2,3},{3,2},{4,5},{5,4},{6,7},{7,6}} | collective-permute-start | bytes 3145736 | tf_op jit(solution)/shard_map/ppermute | solution.py:45
  241.4 29.9 %collective-permute-start.21 = (bf16[256,4096]{1,0:T(8,128)(2,1)}, bf16[256,4096]{1,0:T(8,128)(2,1)}, u32[]{:S(2)}, u32[]{:S(2)}) collective-permute-start(bf16[256,4096]{1,0:T(8,128)(2,1)} %get-tuple-element.133.refs_0_), channel_id=1, source_target_pairs={{0,1},{1,0},{2,3},{3,2},{4,5},{5,4},{6,7},{7,6}} | collective-permute-start | bytes 6291464 | tf_op jit(solution)/shard_map/ppermute | solution.py:45
  242.9 28.5 %collective-permute-start.23 = (bf16[256,4096]{1,0:T(8,128)(2,1)}, bf16[256,4096]{1,0:T(8,128)(2,1)}, u32[]{:S(2)}, u32[]{:S(2)}) collective-permute-start(bf16[256,4096]{1,0:T(8,128)(2,1)} %get-tuple-element.135.refs_2_), channel_id=1, source_target_pairs={{0,1},{1,0},{2,3},{3,2},{4,5},{5,4},{6,7},{7,6}} | collective-permute-start | bytes 6291464 | tf_op jit(solution)/shard_map/ppermute | solution.py:45
  244.4 48.0 %collective-permute-start.27 = (f32[256,2048]{1,0:T(8,128)}, f32[256,2048]{1,0:T(8,128)}, u32[]{:S(2)}, u32[]{:S(2)}) collective-permute-start(f32[256,2048]{1,0:T(8,128)} %get-tuple-element.115.refs_3_), channel_id=1, source_target_pairs={{0,4},{1,3},{2,6},{3,1},{4,0},{5,7},{6,2},{7,5}} | collective-permute-start | bytes 6291464 | tf_op jit(solution)/shard_map/ppermute | solution.py:49
  246.4 46.2 %collective-permute-start.28 = (f32[256,2048]{1,0:T(8,128)}, f32[256,2048]{1,0:T(8,128)}, u32[]{:S(2)}, u32[]{:S(2)}) collective-permute-start(f32[256,2048]{1,0:T(8,128)} %get-tuple-element.142), channel_id=1, source_target_pairs={{0,2},{1,5},{2,0},{3,7},{4,6},{5,1},{6,4},{7,3}} | collective-permute-start | bytes 6291464 | tf_op jit(solution)/shard_map/ppermute | solution.py:49
  271.4 70.6 %collective-permute-start.12 = (bf16[512,1792]{1,0:T(8,128)(2,1)}, bf16[512,1792]{1,0:T(8,128)(2,1)}, u32[]{:S(2)}, u32[]{:S(2)}) collective-permute-start(bf16[512,1792]{1,0:T(8,128)(2,1)} %get-tuple-element.119.refs_1_), channel_id=1, source_target_pairs={{0,1},{1,0},{2,3},{3,2},{4,5},{5,4},{6,7},{7,6}} | collective-permute-start | bytes 5505032 | tf_op jit(solution)/shard_map/ppermute | solution.py:45
  271.4 71.1 %collective-permute-start.14 = (bf16[256,4096]{1,0:T(8,128)(2,1)}, bf16[256,4096]{1,0:T(8,128)(2,1)}, u32[]{:S(2)}, u32[]{:S(2)}) collective-permute-start(bf16[256,4096]{1,0:T(8,128)(2,1)} %dy_ref.1), channel_id=1, source_target_pairs={{0,1},{1,0},{2,3},{3,2},{4,5},{5,4},{6,7},{7,6}} | collective-permute-start | bytes 6291464 | tf_op jit(solution)/shard_map/ppermute | solution.py:45
  292.4 49.3 %collective-permute-start.20 = (bf16[128,4096]{1,0:T(8,128)(2,1)}, bf16[128,4096]{1,0:T(8,128)(2,1)}, u32[]{:S(2)}, u32[]{:S(2)}) collective-permute-start(bf16[128,4096]{1,0:T(8,128)(2,1)} %collective-permute-done.10.refs_1_.refs_12_), channel_id=1, source_target_pairs={{0,1},{1,0},{2,3},{3,2},{4,5},{5,4},{6,7},{7,6}} | collective-permute-start | bytes 3145736 | tf_op jit(solution)/shard_map/ppermute | solution.py:45
  292.6 51.4 %collective-permute-start.31 = (f32[256,2048]{1,0:T(8,128)}, f32[256,2048]{1,0:T(8,128)}, u32[]{:S(2)}, u32[]{:S(2)}) collective-permute-start(f32[256,2048]{1,0:T(8,128)} %get-tuple-element.139.refs_12_), channel_id=1, source_target_pairs={{0,4},{1,3},{2,6},{3,1},{4,0},{5,7},{6,2},{7,5}} | collective-permute-start | bytes 6291464 | tf_op jit(solution)/shard_map/ppermute | solution.py:49
  294.9 49.7 %collective-permute-start.32 = (f32[256,2048]{1,0:T(8,128)}, f32[256,2048]{1,0:T(8,128)}, u32[]{:S(2)}, u32[]{:S(2)}) collective-permute-start(f32[256,2048]{1,0:T(8,128)} %get-tuple-element.153), channel_id=1, source_target_pairs={{0,2},{1,5},{2,0},{3,7},{4,6},{5,1},{6,4},{7,3}} | collective-permute-start | bytes 6291464 | tf_op jit(solution)/shard_map/ppermute | solution.py:49
  341.7 56.2 %collective-permute-start.33 = (f32[256,2048]{1,0:T(8,128)}, f32[256,2048]{1,0:T(8,128)}, u32[]{:S(2)}, u32[]{:S(2)}) collective-permute-start(f32[256,2048]{1,0:T(8,128)} %get-tuple-element.107.refs_4_), channel_id=1, source_target_pairs={{0,4},{1,3},{2,6},{3,1},{4,0},{5,7},{6,2},{7,5}} | collective-permute-start | bytes 6291464 | tf_op jit(solution)/shard_map/ppermute | solution.py:49
  342.0 54.6 %collective-permute-start.30 = (f32[256,2048]{1,0:T(8,128)}, f32[256,2048]{1,0:T(8,128)}, u32[]{:S(2)}, u32[]{:S(2)}) collective-permute-start(f32[256,2048]{1,0:T(8,128)} %get-tuple-element.148), channel_id=1, source_target_pairs={{0,2},{1,5},{2,0},{3,7},{4,6},{5,1},{6,4},{7,3}} | collective-permute-start | bytes 6291464 | tf_op jit(solution)/shard_map/ppermute | solution.py:49
  342.5 93.3 %collective-permute-start.35 = (f32[256,2048]{1,0:T(8,128)}, f32[256,2048]{1,0:T(8,128)}, u32[]{:S(2)}, u32[]{:S(2)}) collective-permute-start(f32[256,2048]{1,0:T(8,128)} %get-tuple-element.158), channel_id=1, source_target_pairs={{0,2},{1,5},{2,0},{3,7},{4,6},{5,1},{6,4},{7,3}} | collective-permute-start | bytes 6291464 | tf_op jit(solution)/shard_map/ppermute | solution.py:49
  344.0 126.9 %collective-permute-start.34 = (f32[256,2048]{1,0:T(8,128)}, f32[256,2048]{1,0:T(8,128)}, u32[]{:S(2)}, u32[]{:S(2)}) collective-permute-start(f32[256,2048]{1,0:T(8,128)} %get-tuple-element.143.refs_20_), channel_id=1, source_target_pairs={{0,2},{1,5},{2,0},{3,7},{4,6},{5,1},{6,4},{7,3}} | collective-permute-start | bytes 6291464 | tf_op jit(solution)/shard_map/ppermute | solution.py:49
  344.5 143.5 %collective-permute-start.36 = (f32[256,2048]{1,0:T(8,128)}, f32[256,2048]{1,0:T(8,128)}, u32[]{:S(2)}, u32[]{:S(2)}) collective-permute-start(f32[256,2048]{1,0:T(8,128)} %get-tuple-element.144.refs_21_), channel_id=1, source_target_pairs={{0,4},{1,3},{2,6},{3,1},{4,0},{5,7},{6,2},{7,5}} | collective-permute-start | bytes 6291464 | tf_op jit(solution)/shard_map/ppermute | solution.py:49
  396.6 106.1 %collective-permute-start.45 = (f32[160,2048]{1,0:T(8,128)}, f32[160,2048]{1,0:T(8,128)}, u32[]{:S(2)}, u32[]{:S(2)}) collective-permute-start(f32[160,2048]{1,0:T(8,128)} %get-tuple-element.165), channel_id=1, source_target_pairs={{0,2},{1,5},{2,0},{3,7},{4,6},{5,1},{6,4},{7,3}} | collective-permute-start | bytes 3932168 | tf_op jit(solution)/shard_map/ppermute | solution.py:49
  397.9 106.3 %collective-permute-start.46 = (f32[160,2048]{1,0:T(8,128)}, f32[160,2048]{1,0:T(8,128)}, u32[]{:S(2)}, u32[]{:S(2)}) collective-permute-start(f32[160,2048]{1,0:T(8,128)} %get-tuple-element.166), channel_id=1, source_target_pairs={{0,4},{1,3},{2,6},{3,1},{4,0},{5,7},{6,2},{7,5}} | collective-permute-start | bytes 3932168 | tf_op jit(solution)/shard_map/ppermute | solution.py:49
  435.8 63.6 %collective-permute-start.43 = (f32[64,2048]{1,0:T(8,128)}, f32[64,2048]{1,0:T(8,128)}, u32[]{:S(2)}, u32[]{:S(2)}) collective-permute-start(f32[64,2048]{1,0:T(8,128)} %get-tuple-element.163), channel_id=1, source_target_pairs={{0,2},{1,5},{2,0},{3,7},{4,6},{5,1},{6,4},{7,3}} | collective-permute-start | bytes 1572872 | tf_op jit(solution)/shard_map/ppermute | solution.py:49
  471.0 31.0 %collective-permute-start.44 = (f32[64,2048]{1,0:T(8,128)}, f32[64,2048]{1,0:T(8,128)}, u32[]{:S(2)}, u32[]{:S(2)}) collective-permute-start(f32[64,2048]{1,0:T(8,128)} %get-tuple-element.164), channel_id=1, source_target_pairs={{0,4},{1,3},{2,6},{3,1},{4,0},{5,7},{6,2},{7,5}} | collective-permute-start | bytes 1572872 | tf_op jit(solution)/shard_map/ppermute | solution.py:49
  498.1 2.3 collective-permute-start.39
  499.4 11.8 %collective-permute-start.37 = (f32[32,2048]{1,0:T(8,128)}, f32[32,2048]{1,0:T(8,128)}, u32[]{:S(2)}, u32[]{:S(2)}) collective-permute-start(f32[32,2048]{1,0:T(8,128)} %get-tuple-element.160), channel_id=1, source_target_pairs={{0,2},{1,5},{2,0},{3,7},{4,6},{5,1},{6,4},{7,3}} | collective-permute-start | bytes 786440 | tf_op jit(solution)/shard_map/ppermute | solution.py:49
  500.4 10.8 %collective-permute-start.38 = (f32[32,2048]{1,0:T(8,128)}, f32[32,2048]{1,0:T(8,128)}, u32[]{:S(2)}, u32[]{:S(2)}) collective-permute-start(f32[32,2048]{1,0:T(8,128)} %get-tuple-element.161), channel_id=1, source_target_pairs={{0,4},{1,3},{2,6},{3,1},{4,0},{5,7},{6,2},{7,5}} | collective-permute-start | bytes 786440 | tf_op jit(solution)/shard_map/ppermute | solution.py:49
  501.9 7.0 %copy-start = (f32[1,4096]{1,0:T(1,128)}, f32[1,4096]{1,0:T(1,128)S(1)}, u32[]{:S(2)}) copy-start(f32[1,4096]{1,0:T(1,128)S(1)} %add.3.refs_4_) | copy-start | bytes 49156
  502.0 9.2 %collective-permute-start.40 = (f32[1,4096]{1,0:T(1,128)S(1)}, f32[1,4096]{1,0:T(1,128)S(1)}, u32[]{:S(2)}, u32[]{:S(2)}) collective-permute-start(f32[1,4096]{1,0:T(1,128)S(1)} %add.3.refs_4_), channel_id=1, source_target_pairs={{0,2},{1,3},{2,0},{3,1},{4,6},{5,7},{6,4},{7,5}} | collective-permute-start | bytes 49160 | tf_op jit(solution)/shard_map/ppermute | solution.py:45
  502.7 8.5 %collective-permute-start.41 = (f32[1,4096]{1,0:T(1,128)S(1)}, f32[1,4096]{1,0:T(1,128)}, u32[]{:S(2)}, u32[]{:S(2)}) collective-permute-start(f32[1,4096]{1,0:T(1,128)S(1)} %add.3.refs_4_), channel_id=1, source_target_pairs={{0,4},{1,5},{2,6},{3,7},{4,0},{5,1},{6,2},{7,3}} | collective-permute-start | bytes 49160 | tf_op jit(solution)/shard_map/ppermute | solution.py:45
  504.2 7.0 %collective-permute-start.42 = (f32[1,4096]{1,0:T(1,128)S(1)}, f32[1,4096]{1,0:T(1,128)}, u32[]{:S(2)}, u32[]{:S(2)}) collective-permute-start(f32[1,4096]{1,0:T(1,128)S(1)} %add.3.refs_4_), channel_id=1, source_target_pairs={{0,6},{1,7},{2,4},{3,5},{4,2},{5,3},{6,0},{7,1}} | collective-permute-start | bytes 49160 | tf_op jit(solution)/shard_map/ppermute | solution.py:45
  511.2 0.6 copy-start.1

commit v5 on v4

--- a/solution.py
+++ b/solution.py
@@ -46,7 +46,7 @@
 
 
 def _cross(v, k):
-    return lax.ppermute(v, "tp", [(i, i ^ (k if i % 2 else k ^ DIAG)) for i in range(8)])
+    return lax.ppermute(v, "tp", [(i, i ^ (k ^ DIAG if i % 2 else k)) for i in range(8)])
 
 
 def _cost(m, k, n, extra=0):
@@ -197,26 +197,27 @@
     nw, ng = int(whole is not None), len(dgs)
 
     def body(*refs):
-        gs, outs = refs[4:4 + ng], refs[4 + ng + nw:]
+        gs, outs = refs[3:3 + ng], refs[3 + ng + nw:]
         half = outs[0].shape[1] // 2
         for h in range(2):
-            outs[0][:, h * half:(h + 1) * half] = (refs[h][...] + refs[2 + h][...]).astype(outs[0].dtype)
+            cols = slice(h * half, (h + 1) * half)
+            outs[0][:, cols] = (refs[0][:, cols] + refs[1 + h][...]).astype(outs[0].dtype)
         if ng:
             outs[1][...] = (gs[0][...] + gs[1][...]) + (gs[2][...] + gs[3][...])
 
     rows, half = last[0].shape
     at = lambda j: (j + row // tile, 0)
-    spec = pl.BlockSpec((tile, half), at)
+    spec = pl.BlockSpec((tile, 2 * half), at)
     one = pl.BlockSpec((1, 2 * half), lambda j: (0, 0))
     out = pl.pallas_call(
         body, grid=(rows // tile,),
-        in_specs=[spec] * 2 + [pl.BlockSpec((tile, half), lambda j: (j, 0))] * 2 + [one] * ng + [ANY] * nw,
-        out_specs=[pl.BlockSpec((tile, 2 * half), at)] + [one] * bool(ng),
+        in_specs=[spec] + [pl.BlockSpec((tile, half), lambda j: (j, 0))] * 2 + [one] * ng + [ANY] * nw,
+        out_specs=[spec] + [one] * bool(ng),
         out_shape=[jax.ShapeDtypeStruct((n, 2 * half), jnp.bfloat16)] + [jax.ShapeDtypeStruct((1, 2 * half), jnp.float32)] * bool(ng),
-        input_output_aliases={4 + ng: 0} if nw else {}, compiler_params=_params(),
+        input_output_aliases={3 + ng: 0} if nw else {}, compiler_params=_params(),
         cost_estimate=pl.CostEstimate(flops=2 * rows * half, bytes_accessed=20 * rows * half, transcendentals=0),
         name="finish",
-    )(*base, *last, *dgs, *([whole] if nw else []))
+    )(base, *last, *dgs, *([whole] if nw else []))
     return out if ng else out[0]
 
 
@@ -251,12 +252,13 @@
     def body(x_ref, *refs):
         for h in range(2):
             x = x_ref[:, h * half:(h + 1) * half].astype(jnp.float32)
-            refs[4 + h][...] = x + (refs[2 * h][...] + refs[2 * h + 1][...])
+            refs[4][:, h * half:(h + 1) * half] = x + (refs[2 * h][...] + refs[2 * h + 1][...])
 
     spec = pl.BlockSpec((tile, half), lambda j: (j, 0))
     return pl.pallas_call(
-        body, grid=(n // tile,), in_specs=[pl.BlockSpec((tile, D), lambda j: (j, 0))] + [spec] * 4, out_specs=[spec] * 2,
-        out_shape=[jax.ShapeDtypeStruct((n, half), jnp.float32)] * 2, compiler_params=_params(),
+        body, grid=(n // tile,), in_specs=[pl.BlockSpec((tile, D), lambda j: (j, 0))] + [spec] * 4,
+        out_specs=pl.BlockSpec((tile, D), lambda j: (j, 0)),
+        out_shape=jax.ShapeDtypeStruct((n, D), jnp.float32), compiler_params=_params(),
         cost_estimate=pl.CostEstimate(flops=2 * n * D, bytes_accessed=14 * n * D, transcendentals=0), name="base",
     )(X, *[v for t in terms for v in t])
 
@@ -384,7 +386,7 @@
         va, vb = _cross(sums[0], YN), _cross(sums[3], XN)
         ua, ub = _cross(sums[1], YN), _cross(sums[4], XN)
         base = _base(X, ((Y00, sa), (Y01, sb)))
-        (Z0,) = _down([[A0], [A0p]], Ws1, NT, after=base)
+        (Z0,) = _down([[A0], [A0p]], Ws1, NT, after=(base,))
         dX, dg = _dx(((Z0[0], ra, za), (Z0[1], rb, zb)), X, dY, gamma)
         dg = dg + _swap(dg, CORE)
         dgs = dg, _swap(dg, XN), _swap(dg, YN), _swap(dg, DIAG)
@@ -393,7 +395,7 @@
         wb = _cross(last_b, XN)
         Y = _finish(base, (va, vb), 0, None, n, cuts[0] // 2)
         Y = _finish(base, (ua, ub), cuts[0], Y, n, cuts[2])
-        Y, dgamma = _finish(base, (wa, wb), cuts[0] + cuts[1], Y, n, cuts[2], dgs)
+        Y, dgamma = _finish(base, (wa, wb), cuts[0] + cuts[1], Y, n, cuts[2] // 2, dgs)
         return Y, dX, dW1, dW2, dgamma.reshape(D)
 
     return jax.shard_map(block, mesh=mesh,

time: 515 us -> 514 us (level)
  no operation moved by 1% of the time
where the time goes in v5:
time: 514 us
  Pallas kernels  368 us (72%)
  waiting for transfers between devices  108 us (21%)
  starting transfers between devices  36.1 us (7%)
    pallas_call x8, Pallas kernels, _up(): pl.pallas_call(body, grid=(F // tile,), in_specs=[pl.BlockSpec(p.shape, l...  139 us
    pallas_call x6, Pallas kernels, _down(): pl.pallas_call(body, grid=(steps,), in_specs=[pl.BlockSpec(p.shape, lambd...  106 us
    ppermute x25, waiting for transfers between devices, _cross(): lax.ppermute(v, 'tp', [(i, i ^ (k ^ DIAG if i % 2 else k)) for i in range...  89.3 us
    pallas_call x2, Pallas kernels, _grad(): pl.pallas_call(body, grid=(M // tile,), in_specs=[pl.BlockSpec((p.shape[0...  81.9 us
    ppermute x25, starting transfers between devices, _cross(): lax.ppermute(v, 'tp', [(i, i ^ (k ^ DIAG if i % 2 else k)) for i in range...  27.3 us
    ppermute x22, waiting for transfers between devices, _swap(): return lax.ppermute(v, 'tp', [(i, i ^ k) for i in range(8)])  18.5 us
    pallas_call x2, Pallas kernels, _sums(): pl.pallas_call(body, grid=(n // tile,), in_specs=[spec] * (2 * len(pairs)...  13.7 us
  transfers between devices with their start and end apart: 47, of which 12 were waited for; matrix products, arithmetic and copies ran while one was open for 0% of the time, Pallas kernels for 71%

profile of v5, /device:TPU:0, one launch (start us, length us, event | category | flops | bytes accessed | tf_op | source)
XLA Modules:
  0.0 513.6 jit_solution(8531158061243747154)
XLA Ops:
  0.6 0.9 collective-permute-start.2
  1.5 2.9 collective-permute-start
  4.5 1.5 collective-permute-start.1
  6.0 2.9 halves.1
  8.9 0.5 collective-permute-start.5
  9.5 13.5 %up_A.4 = (bf16[256,1792]{1,0:T(8,128)(2,1)}, f32[256,1792]{1,0:T(8,128)}, bf16[256,4096]{1,0:T(8,128)(2,1)}) custom-call(bf16[256,4096]{1,0:T(8,128)(2,1)} %x_ref.1, bf16[4096,1792]{1,0:T(8,128)(2,1)} %refs_2_.13, f32[1,4096]{1,0:T(1,128)} %bitcast.2), custom_call_target="tpu_custom_call" | custom-call | flops 3758096384 | bytes 16777216 | tf_op jit(solution)/shard_map/up_A/pallas_call | solution.py:116
  23.0 11.7 %up_dA.4.refs_3_.refs_6_.refs_0_ = bf16[256,1792]{1,0:T(8,128)(2,1)} custom-call(bf16[256,4096]{1,0:T(8,128)(2,1)} %dy_ref.1, bf16[1792,4096]{1,0:T(8,128)(2,1)} %refs_4_.3, f32[256,1792]{1,0:T(8,128)} %get-tuple-element.85.refs_2_), custom_call_target="tpu_custom_call" | custom-call | flops 3758096384 | bytes 16777216 | tf_op jit(solution)/shard_map/up_dA/pallas_call | solution.py:116
  34.7 13.6 %up_A.5 = (bf16[256,1792]{1,0:T(8,128)(2,1)}, f32[256,1792]{1,0:T(8,128)}, bf16[256,4096]{1,0:T(8,128)(2,1)}) custom-call(bf16[256,4096]{1,0:T(8,128)(2,1)} %x_ref.1, bf16[4096,1792]{1,0:T(8,128)(2,1)} %collective-permute-done.2.refs_1_.refs_3_.refs_2_, f32[1,4096]{1,0:T(1,128)} %bitcast.3, bf16[256,1792]{1,0:T(8,128)(2,1)} %up_dA.4.refs_3_.refs_6_.refs_0_), custom_call_target="tpu_custom_call" | custom-call | flops 3758096384 | bytes 16777216 | tf_op jit(solution)/shard_map/up_A/pallas_call | solution.py:116
  48.3 2.2 collective-permute-done.refs_0_
  50.5 2.5 collective-permute-start.7
  53.3 1.5 collective-permute-start.8
  54.8 27.8 %up_A.6 = (bf16[512,1792]{1,0:T(8,128)(2,1)}, f32[512,1792]{1,0:T(8,128)}, bf16[512,1792]{1,0:T(8,128)(2,1)}, f32[512,1792]{1,0:T(8,128)}, bf16[512,4096]{1,0:T(8,128)(2,1)}) custom-call(bf16[256,4096]{1,0:T(8,128)(2,1)} %collective-permute-done.refs_0_, bf16[256,4096]{1,0:T(8,128)(2,1)} %collective-permute-done.1.refs_1_, bf16[4096,1792]{1,0:T(8,128)(2,1)} %refs_2_.13, ...), custom_call_target="tpu_custom_call" | custom-call | flops 15032385536 | bytes 33554432 | tf_op jit(solution)/shard_map/up_A/pallas_call | solution.py:116
  82.7 0.5 collective-permute-start.4
  83.2 13.1 %down.6 = (f32[256,2048]{1,0:T(8,128)}, f32[256,2048]{1,0:T(8,128)}) custom-call(bf16[512,1792]{1,0:T(8,128)(2,1)} %get-tuple-element.89.refs_0_.refs_1_, bf16[512,1792]{1,0:T(8,128)(2,1)} %get-tuple-element.117.refs_1_, bf16[1792,4096]{1,0:T(8,128)(2,1)} %refs_4_.3, bf16[1792,4096]{1,0:T(8,128)(2,1)} %collective-permute-done.3.refs_3_.refs_5_.refs_1_), custom_call_target="tpu_custom_call" | custom-call | flops 7516192768 | bytes 22544384 | tf_op jit(solution)/shard_map/down/pallas_call | solution.py:159
  96.4 2.0 collective-permute-start.9
  98.4 13.1 %down.7 = (f32[256,2048]{1,0:T(8,128)}, f32[256,2048]{1,0:T(8,128)}) custom-call(bf16[512,1792]{1,0:T(8,128)(2,1)} %get-tuple-element.89.refs_0_.refs_1_, bf16[512,1792]{1,0:T(8,128)(2,1)} %get-tuple-element.117.refs_1_, bf16[1792,4096]{1,0:T(8,128)(2,1)} %refs_4_.3, bf16[1792,4096]{1,0:T(8,128)(2,1)} %collective-permute-done.3.refs_3_.refs_5_.refs_1_, ...), custom_call_target="tpu_custom_call" | custom-call | flops 7516192768 | bytes 22544384 | tf_op jit(solution)/shard_map/down/pallas_call | solution.py:159
  111.5 23.0 %up_dA.5 = (bf16[512,1792]{1,0:T(8,128)(2,1)}, bf16[512,1792]{1,0:T(8,128)(2,1)}) custom-call(bf16[128,4096]{1,0:T(8,128)(2,1)} %collective-permute-done.5.refs_0_.refs_7_, bf16[128,4096]{1,0:T(8,128)(2,1)} %collective-permute-done.7.refs_1_.refs_8_, bf16[128,4096]{1,0:T(8,128)(2,1)} %collective-permute-done.6.refs_2_.refs_9_, ...), custom_call_target="tpu_custom_call" | custom-call | flops 15032385536 | bytes 33554432 | tf_op jit(solution)/shard_map/up_dA/pallas_call | solution.py:116
  134.6 22.8 %down.8 = (f32[256,2048]{1,0:T(8,128)}, f32[256,2048]{1,0:T(8,128)}, f32[256,2048]{1,0:T(8,128)}, f32[256,2048]{1,0:T(8,128)}) custom-call(bf16[512,1792]{1,0:T(8,128)(2,1)} %get-tuple-element.103.refs_0_.refs_7_, bf16[512,1792]{1,0:T(8,128)(2,1)} %get-tuple-element.135.refs_1_, bf16[4096,1792]{1,0:T(8,128)(2,1)} %refs_2_.13, ...), custom_call_target="tpu_custom_call" | custom-call | flops 15032385536 | bytes 41418752 | tf_op jit(solution)/shard_map/down/pallas_call | solution.py:159
  157.3 20.1 %up_A.7 = (bf16[256,1792]{1,0:T(8,128)(2,1)}, f32[256,1792]{1,0:T(8,128)}, bf16[256,1792]{1,0:T(8,128)(2,1)}, f32[256,1792]{1,0:T(8,128)}, bf16[256,4096]{1,0:T(8,128)(2,1)}) custom-call(bf16[256,4096]{1,0:T(8,128)(2,1)} %collective-permute-done.4.refs_0_, bf16[4096,1792]{1,0:T(8,128)(2,1)} %refs_2_.13, ...), custom_call_target="tpu_custom_call" | custom-call | flops 7516192768 | bytes 31457280 | tf_op jit(solution)/shard_map/up_A/pallas_call | solution.py:116
  177.5 17.6 %up_dA.6 = (bf16[256,1792]{1,0:T(8,128)(2,1)}, bf16[256,1792]{1,0:T(8,128)(2,1)}) custom-call(bf16[128,4096]{1,0:T(8,128)(2,1)} %collective-permute-done.9.refs_0_.refs_11_, bf16[128,4096]{1,0:T(8,128)(2,1)} %collective-permute-done.10.refs_1_.refs_12_, bf16[1792,4096]{1,0:T(8,128)(2,1)} %refs_4_.3, ...), custom_call_target="tpu_custom_call" | custom-call | flops 7516192768 | bytes 31457280 | tf_op jit(solution)/shard_map/up_dA/pallas_call | solution.py:116
  195.1 0.5 collective-permute-start.13
  195.6 16.8 %down.9 = (f32[256,2048]{1,0:T(8,128)}, f32[256,2048]{1,0:T(8,128)}) custom-call(bf16[256,1792]{1,0:T(8,128)(2,1)} %get-tuple-element.111.refs_0_.refs_8_, bf16[256,1792]{1,0:T(8,128)(2,1)} %get-tuple-element.136.refs_1_, bf16[4096,1792]{1,0:T(8,128)(2,1)} %refs_2_.13, bf16[4096,1792]{1,0:T(8,128)(2,1)} %collective-permute-done.2.refs_1_.refs_3_.refs_2_), custom_call_target="tpu_custom_call" | custom-call | flops 7516192768 | bytes 35389440 | tf_op jit(solution)/shard_map/down/pallas_call | solution.py:159
  212.4 11.7 %up_dA.7.refs_6_.refs_1_ = bf16[256,1792]{1,0:T(8,128)(2,1)} custom-call(bf16[256,4096]{1,0:T(8,128)(2,1)} %dy_ref.1, bf16[1792,4096]{1,0:T(8,128)(2,1)} %collective-permute-done.3.refs_3_.refs_5_.refs_1_, f32[256,1792]{1,0:T(8,128)} %get-tuple-element.108.refs_2_, f32[256,2048]{1,0:T(8,128)} %get-tuple-element.113.refs_3_), custom_call_target="tpu_custom_call" | custom-call | flops 3758096384 | bytes 16777216 | tf_op jit(solution)/shard_map/up_dA/pallas_call | solution.py:116
  224.1 0.5 collective-permute-start.15
  224.6 0.5 collective-permute-start.22
  225.1 1.8 collective-permute-done.24.refs_9_
  227.0 10.2 %collective-permute-done.26.refs_11_ = bf16[256,1792]{1,0:T(8,128)(2,1)} collective-permute-done((bf16[256,1792]{1,0:T(8,128)(2,1)}, bf16[256,1792]{1,0:T(8,128)(2,1)}, u32[]{:S(2)}, u32[]{:S(2)}) %collective-permute-start.26) | collective-permute-done | bytes 917536 | tf_op jit(solution)/shard_map/ppermute | solution.py:45
  237.3 0.4 collective-permute-start.18
  237.9 3.5 collective-permute-done.17.refs_16_
  241.5 1.4 collective-permute-done.18.refs_17_
  243.0 1.4 collective-permute-done.19.refs_18_
  244.3 2.0 collective-permute-start.27
  246.3 1.5 collective-permute-start.28
  247.8 23.5 %down.10 = (f32[256,2048]{1,0:T(8,128)}, f32[256,2048]{1,0:T(8,128)}, f32[256,2048]{1,0:T(8,128)}, f32[256,2048]{1,0:T(8,128)}) custom-call(bf16[256,1792]{1,0:T(8,128)(2,1)} %get-tuple-element.94.refs_0_, bf16[256,1792]{1,0:T(8,128)(2,1)} %get-tuple-element.106.refs_1_.refs_2_, bf16[256,1792]{1,0:T(8,128)(2,1)} %get-tuple-element.116.refs_5_.refs_2_, ...), custom_call_target="tpu_custom_call" | custom-call | flops 15032385536 | bytes 41418752 | tf_op jit(solution)/shard_map/down/pallas_call | solution.py:159
  271.3 0.5 collective-permute-start.14
  271.8 20.4 %collective-permute-done.27.refs_1_ = f32[256,2048]{1,0:T(8,128)} collective-permute-done((f32[256,2048]{1,0:T(8,128)}, f32[256,2048]{1,0:T(8,128)}, u32[]{:S(2)}, u32[]{:S(2)}) %collective-permute-start.27) | collective-permute-done | bytes 2097184 | tf_op jit(solution)/shard_map/ppermute | solution.py:49
  292.6 2.1 collective-permute-start.31
  294.7 1.3 collective-permute-start.32
  296.0 39.7 %shard_map.92 = f32[4096,1792]{1,0:T(8,128)} custom-call(bf16[256,4096]{1,0:T(8,128)(2,1)} %get-tuple-element.131.refs_0_, bf16[512,4096]{1,0:T(8,128)(2,1)} %get-tuple-element.132.refs_1_, bf16[256,4096]{1,0:T(8,128)(2,1)} %get-tuple-element.133.refs_2_, bf16[256,4096]{1,0:T(8,128)(2,1)} %collective-permute-done.21.refs_3_, ...), custom_call_target="tpu_custom_call" | custom-call | flops 30064771072 | bytes 53477376 | tf_op jit(solution)/shard_map/pallas_call | solution.py:185
  335.8 5.8 %shard_map.93 = (f32[256,2048]{1,0:T(8,128)}, f32[256,2048]{1,0:T(8,128)}) custom-call(f32[256,2048]{1,0:T(8,128)} %get-tuple-element.138.refs_0_, f32[256,2048]{1,0:T(8,128)} %collective-permute-done.27.refs_1_, f32[256,2048]{1,0:T(8,128)} %get-tuple-element.139.refs_2_, f32[256,2048]{1,0:T(8,128)} %collective-permute-done.28.refs_3_), custom_call_target="tpu_custom_call" | custom-call | flops 1048576 | bytes 12582912 | tf_op jit(solution)/shard_map/pallas_call | solution.py:241
  341.9 0.4 collective-permute-start.30
  342.3 1.6 collective-permute-start.35
  343.9 0.4 collective-permute-start.34
  344.3 2.0 collective-permute-start.36
  346.3 42.2 %shard_map.94 = f32[1792,4096]{1,0:T(8,128)} custom-call(bf16[256,1792]{1,0:T(8,128)(2,1)} %get-tuple-element.94.refs_0_, bf16[512,1792]{1,0:T(8,128)(2,1)} %get-tuple-element.89.refs_0_.refs_1_, bf16[256,1792]{1,0:T(8,128)(2,1)} %get-tuple-element.106.refs_1_.refs_2_, bf16[256,1792]{1,0:T(8,128)(2,1)} %collective-permute-done.11.refs_3_, ...), custom_call_target="tpu_custom_call" | custom-call | flops 30064771072 | bytes 53477376 | tf_op jit(solution)/shard_map/pallas_call | solution.py:185
  388.5 8.0 %shard_map.95 = (f32[160,2048]{1,0:T(8,128)}, f32[64,2048]{1,0:T(8,128)}, f32[32,2048]{1,0:T(8,128)}, f32[160,2048]{1,0:T(8,128)}, f32[64,2048]{1,0:T(8,128)}, /*index=5*/f32[32,2048]{1,0:T(8,128)}) custom-call(f32[256,2048]{1,0:T(8,128)} %get-tuple-element.147.refs_0_, f32[256,2048]{1,0:T(8,128)} %collective-permute-done.31.refs_1_, ...), custom_call_target="tpu_custom_call" | custom-call | flops 1048576 | bytes 12582912 | tf_op jit(solution)/shard_map/pallas_call | solution.py:241
  396.4 1.4 collective-permute-start.45
  398.1 6.2 %base.1.refs_4_.refs_0_ = f32[256,4096]{1,0:T(8,128)} custom-call(bf16[256,4096]{1,0:T(8,128)(2,1)} %x_ref.1, f32[256,2048]{1,0:T(8,128)} %get-tuple-element.144.refs_0_, f32[256,2048]{1,0:T(8,128)} %collective-permute-done.29.refs_1_, f32[256,2048]{1,0:T(8,128)} %get-tuple-element.145.refs_2_, f32[256,2048]{1,0:T(8,128)} %collective-permute-done.30.refs_3_), custom_call_target="tpu_custom_call" | custom-call | flops 2097152 | bytes 14680064 | tf_op jit(solution)/shard_map/base/pallas_call | solution.py:258
  404.4 31.3 %collective-permute-done.35.refs_4_ = f32[256,2048]{1,0:T(8,128)} collective-permute-done((f32[256,2048]{1,0:T(8,128)}, f32[256,2048]{1,0:T(8,128)}, u32[]{:S(2)}, u32[]{:S(2)}) %collective-permute-start.35) | collective-permute-done | bytes 2097184 | tf_op jit(solution)/shard_map/ppermute | solution.py:49
  435.7 0.4 collective-permute-start.43
  436.1 34.8 %collective-permute-done.34.refs_2_ = f32[256,2048]{1,0:T(8,128)} collective-permute-done((f32[256,2048]{1,0:T(8,128)}, f32[256,2048]{1,0:T(8,128)}, u32[]{:S(2)}, u32[]{:S(2)}) %collective-permute-start.34) | collective-permute-done | bytes 2097184 | tf_op jit(solution)/shard_map/ppermute | solution.py:49
  471.1 16.8 %down.11 = (f32[256,2048]{1,0:T(8,128)}, f32[256,2048]{1,0:T(8,128)}) custom-call(bf16[256,1792]{1,0:T(8,128)(2,1)} %up_dA.4.refs_3_.refs_6_.refs_0_, bf16[256,1792]{1,0:T(8,128)(2,1)} %up_dA.7.refs_6_.refs_1_, bf16[4096,1792]{1,0:T(8,128)(2,1)} %refs_2_.13, bf16[4096,1792]{1,0:T(8,128)(2,1)} %collective-permute-done.2.refs_1_.refs_3_.refs_2_, ...), custom_call_target="tpu_custom_call" | custom-call | flops 7516192768 | bytes 35389440 | tf_op jit(solution)/shard_map/down/pallas_call | solution.py:159
  487.9 10.0 %dx.1 = (bf16[256,4096]{1,0:T(8,128)(2,1)}, f32[1,4096]{1,0:T(1,128)}) custom-call(bf16[256,4096]{1,0:T(8,128)(2,1)} %x_ref.1, bf16[256,4096]{1,0:T(8,128)(2,1)} %dy_ref.1, f32[1,4096]{1,0:T(1,128)} %bitcast.6, f32[256,2048]{1,0:T(8,128)} %get-tuple-element.152.refs_0_, f32[256,2048]{1,0:T(8,128)} %collective-permute-done.33.refs_1_, ...), custom_call_target="tpu_custom_call" | custom-call | flops 20971520 | bytes 18874368 | tf_op jit(solution)/shard_map/dx/pallas_call | solution.py:296
  497.9 1.2 collective-permute-start.39
  499.1 0.7 collective-permute-start.37
  500.2 0.8 collective-permute-start.38
  501.0 0.7 add.3.refs_3_
  501.7 1.2 collective-permute-start.40
  503.0 1.0 collective-permute-start.41
  504.0 1.3 collective-permute-start.42
  505.3 3.4 finish.3.refs_3_
  508.7 2.3 finish.4.refs_7_
  511.0 0.6 copy-done.1
  511.6 2.0 finish.5
  (59 shorter events, 3.0 us)
Async XLA Ops:
  0.6 34.1 %collective-permute-start.2 = (bf16[4096,1792]{1,0:T(8,128)(2,1)}, bf16[4096,1792]{1,0:T(8,128)(2,1)}, u32[]{:S(2)}, u32[]{:S(2)}) collective-permute-start(bf16[4096,1792]{1,0:T(8,128)(2,1)} %refs_2_.13), channel_id=1, source_target_pairs={{0,1},{1,0},{2,3},{3,2},{4,5},{5,4},{6,7},{7,6}} | collective-permute-start | bytes 44040200 | tf_op jit(solution)/shard_map/ppermute | solution.py:45
  1.5 81.7 %collective-permute-start.3 = (bf16[1792,4096]{1,0:T(8,128)(2,1)}, bf16[1792,4096]{1,0:T(8,128)(2,1)}, u32[]{:S(2)}, u32[]{:S(2)}) collective-permute-start(bf16[1792,4096]{1,0:T(8,128)(2,1)} %refs_4_.3), channel_id=1, source_target_pairs={{0,1},{1,0},{2,3},{3,2},{4,5},{5,4},{6,7},{7,6}} | collective-permute-start | bytes 44040200 | tf_op jit(solution)/shard_map/ppermute | solution.py:45
  1.5 49.0 %collective-permute-start = (bf16[256,4096]{1,0:T(8,128)(2,1)}, bf16[256,4096]{1,0:T(8,128)(2,1)}, u32[]{:S(2)}, u32[]{:S(2)}) collective-permute-start(bf16[256,4096]{1,0:T(8,128)(2,1)} %x_ref.1), channel_id=1, source_target_pairs={{0,2},{1,5},{2,0},{3,7},{4,6},{5,1},{6,4},{7,3}} | collective-permute-start | bytes 6291464 | tf_op jit(solution)/shard_map/ppermute | solution.py:49
  4.5 48.8 %collective-permute-start.1 = (bf16[256,4096]{1,0:T(8,128)(2,1)}, bf16[256,4096]{1,0:T(8,128)(2,1)}, u32[]{:S(2)}, u32[]{:S(2)}) collective-permute-start(bf16[256,4096]{1,0:T(8,128)(2,1)} %x_ref.1), channel_id=1, source_target_pairs={{0,4},{1,3},{2,6},{3,1},{4,0},{5,7},{6,2},{7,5}} | collective-permute-start | bytes 6291464 | tf_op jit(solution)/shard_map/ppermute | solution.py:49
  8.9 73.7 %collective-permute-start.5 = (bf16[128,4096]{1,0:T(8,128)(2,1)}, bf16[128,4096]{1,0:T(8,128)(2,1)}, u32[]{:S(2)}, u32[]{:S(2)}) collective-permute-start(bf16[128,4096]{1,0:T(8,128)(2,1)} %get-tuple-element.95), channel_id=1, source_target_pairs={{0,2},{1,5},{2,0},{3,7},{4,6},{5,1},{6,4},{7,3}} | collective-permute-start | bytes 3145736 | tf_op jit(solution)/shard_map/ppermute | solution.py:49
  34.7 48.5 %collective-permute-start.6 = (bf16[128,4096]{1,0:T(8,128)(2,1)}, bf16[128,4096]{1,0:T(8,128)(2,1)}, u32[]{:S(2)}, u32[]{:S(2)}) collective-permute-start(bf16[128,4096]{1,0:T(8,128)(2,1)} %get-tuple-element.95), channel_id=1, source_target_pairs={{0,4},{1,3},{2,6},{3,1},{4,0},{5,7},{6,2},{7,5}} | collective-permute-start | bytes 3145736 | tf_op jit(solution)/shard_map/ppermute | solution.py:49
  50.5 45.9 %collective-permute-start.7 = (bf16[128,4096]{1,0:T(8,128)(2,1)}, bf16[128,4096]{1,0:T(8,128)(2,1)}, u32[]{:S(2)}, u32[]{:S(2)}) collective-permute-start(bf16[128,4096]{1,0:T(8,128)(2,1)} %get-tuple-element.97), channel_id=1, source_target_pairs={{0,2},{1,5},{2,0},{3,7},{4,6},{5,1},{6,4},{7,3}} | collective-permute-start | bytes 3145736 | tf_op jit(solution)/shard_map/ppermute | solution.py:49
  53.3 43.1 %collective-permute-start.8 = (bf16[128,4096]{1,0:T(8,128)(2,1)}, bf16[128,4096]{1,0:T(8,128)(2,1)}, u32[]{:S(2)}, u32[]{:S(2)}) collective-permute-start(bf16[128,4096]{1,0:T(8,128)(2,1)} %get-tuple-element.97), channel_id=1, source_target_pairs={{0,4},{1,3},{2,6},{3,1},{4,0},{5,7},{6,2},{7,5}} | collective-permute-start | bytes 3145736 | tf_op jit(solution)/shard_map/ppermute | solution.py:49
  82.7 74.7 %collective-permute-start.4 = (bf16[256,4096]{1,0:T(8,128)(2,1)}, bf16[256,4096]{1,0:T(8,128)(2,1)}, u32[]{:S(2)}, u32[]{:S(2)}) collective-permute-start(bf16[256,4096]{1,0:T(8,128)(2,1)} %collective-permute-done.refs_0_), channel_id=1, source_target_pairs={{0,4},{1,3},{2,6},{3,1},{4,0},{5,7},{6,2},{7,5}} | collective-permute-start | bytes 6291464 | tf_op jit(solution)/shard_map/ppermute | solution.py:49
  96.3 128.3 %collective-permute-start.29 = (f32[256,2048]{1,0:T(8,128)}, f32[256,2048]{1,0:T(8,128)}, u32[]{:S(2)}, u32[]{:S(2)}) collective-permute-start(f32[256,2048]{1,0:T(8,128)} %get-tuple-element.91.refs_4_), channel_id=1, source_target_pairs={{0,2},{1,5},{2,0},{3,7},{4,6},{5,1},{6,4},{7,3}} | collective-permute-start | bytes 6291464 | tf_op jit(solution)/shard_map/ppermute | solution.py:49
  96.4 81.1 %collective-permute-start.9 = (bf16[128,4096]{1,0:T(8,128)(2,1)}, bf16[128,4096]{1,0:T(8,128)(2,1)}, u32[]{:S(2)}, u32[]{:S(2)}) collective-permute-start(bf16[128,4096]{1,0:T(8,128)(2,1)} %collective-permute-done.6.refs_2_.refs_9_), channel_id=1, source_target_pairs={{0,2},{1,5},{2,0},{3,7},{4,6},{5,1},{6,4},{7,3}} | collective-permute-start | bytes 3145736 | tf_op jit(solution)/shard_map/ppermute | solution.py:49
  98.4 79.1 %collective-permute-start.10 = (bf16[128,4096]{1,0:T(8,128)(2,1)}, bf16[128,4096]{1,0:T(8,128)(2,1)}, u32[]{:S(2)}, u32[]{:S(2)}) collective-permute-start(bf16[128,4096]{1,0:T(8,128)(2,1)} %collective-permute-done.8.refs_3_.refs_10_), channel_id=1, source_target_pairs={{0,2},{1,5},{2,0},{3,7},{4,6},{5,1},{6,4},{7,3}} | collective-permute-start | bytes 3145736 | tf_op jit(solution)/shard_map/ppermute | solution.py:49
  195.1 29.5 %collective-permute-start.11 = (bf16[256,1792]{1,0:T(8,128)(2,1)}, bf16[256,1792]{1,0:T(8,128)(2,1)}, u32[]{:S(2)}, u32[]{:S(2)}) collective-permute-start(bf16[256,1792]{1,0:T(8,128)(2,1)} %get-tuple-element.116.refs_5_.refs_2_), channel_id=1, source_target_pairs={{0,1},{1,0},{2,3},{3,2},{4,5},{5,4},{6,7},{7,6}} | collective-permute-start | bytes 2752520 | tf_op jit(solution)/shard_map/ppermute | solution.py:45
  195.1 30.0 %collective-permute-start.13 = (bf16[256,1792]{1,0:T(8,128)(2,1)}, bf16[256,1792]{1,0:T(8,128)(2,1)}, u32[]{:S(2)}, u32[]{:S(2)}) collective-permute-start(bf16[256,1792]{1,0:T(8,128)(2,1)} %get-tuple-element.118.refs_3_), channel_id=1, source_target_pairs={{0,1},{1,0},{2,3},{3,2},{4,5},{5,4},{6,7},{7,6}} | collective-permute-start | bytes 2752520 | tf_op jit(solution)/shard_map/ppermute | solution.py:45
  224.1 2.8 collective-permute-start.24
  224.1 13.2 %collective-permute-start.15 = (bf16[128,4096]{1,0:T(8,128)(2,1)}, bf16[128,4096]{1,0:T(8,128)(2,1)}, u32[]{:S(2)}, u32[]{:S(2)}) collective-permute-start(bf16[128,4096]{1,0:T(8,128)(2,1)} %collective-permute-done.5.refs_0_.refs_7_), channel_id=1, source_target_pairs={{0,1},{1,0},{2,3},{3,2},{4,5},{5,4},{6,7},{7,6}} | collective-permute-start | bytes 3145736 | tf_op jit(solution)/shard_map/ppermute | solution.py:45
  224.6 13.1 %collective-permute-start.16 = (bf16[128,4096]{1,0:T(8,128)(2,1)}, bf16[128,4096]{1,0:T(8,128)(2,1)}, u32[]{:S(2)}, u32[]{:S(2)}) collective-permute-start(bf16[128,4096]{1,0:T(8,128)(2,1)} %collective-permute-done.7.refs_1_.refs_8_), channel_id=1, source_target_pairs={{0,1},{1,0},{2,3},{3,2},{4,5},{5,4},{6,7},{7,6}} | collective-permute-start | bytes 3145736 | tf_op jit(solution)/shard_map/ppermute | solution.py:45
  224.6 70.1 %collective-permute-start.22 = (bf16[512,4096]{1,0:T(8,128)(2,1)}, bf16[512,4096]{1,0:T(8,128)(2,1)}, u32[]{:S(2)}, u32[]{:S(2)}) collective-permute-start(bf16[512,4096]{1,0:T(8,128)(2,1)} %get-tuple-element.132.refs_1_), channel_id=1, source_target_pairs={{0,1},{1,0},{2,3},{3,2},{4,5},{5,4},{6,7},{7,6}} | collective-permute-start | bytes 12582920 | tf_op jit(solution)/shard_map/ppermute | solution.py:45
  225.1 12.1 %collective-permute-start.26 = (bf16[256,1792]{1,0:T(8,128)(2,1)}, bf16[256,1792]{1,0:T(8,128)(2,1)}, u32[]{:S(2)}, u32[]{:S(2)}) collective-permute-start(bf16[256,1792]{1,0:T(8,128)(2,1)} %get-tuple-element.136.refs_1_), channel_id=1, source_target_pairs={{0,1},{1,0},{2,3},{3,2},{4,5},{5,4},{6,7},{7,6}} | collective-permute-start | bytes 2752520 | tf_op jit(solution)/shard_map/ppermute | solution.py:45
  226.9 19.4 %collective-permute-start.25 = (bf16[512,1792]{1,0:T(8,128)(2,1)}, bf16[512,1792]{1,0:T(8,128)(2,1)}, u32[]{:S(2)}, u32[]{:S(2)}) collective-permute-start(bf16[512,1792]{1,0:T(8,128)(2,1)} %get-tuple-element.135.refs_1_), channel_id=1, source_target_pairs={{0,1},{1,0},{2,3},{3,2},{4,5},{5,4},{6,7},{7,6}} | collective-permute-start | bytes 5505032 | tf_op jit(solution)/shard_map/ppermute | solution.py:45
  237.2 4.1 collective-permute-start.17
  237.3 5.5 %collective-permute-start.18 = (bf16[128,4096]{1,0:T(8,128)(2,1)}, bf16[128,4096]{1,0:T(8,128)(2,1)}, u32[]{:S(2)}, u32[]{:S(2)}) collective-permute-start(bf16[128,4096]{1,0:T(8,128)(2,1)} %collective-permute-done.8.refs_3_.refs_10_), channel_id=1, source_target_pairs={{0,1},{1,0},{2,3},{3,2},{4,5},{5,4},{6,7},{7,6}} | collective-permute-start | bytes 3145736 | tf_op jit(solution)/shard_map/ppermute | solution.py:45
  237.7 6.6 %collective-permute-start.19 = (bf16[128,4096]{1,0:T(8,128)(2,1)}, bf16[128,4096]{1,0:T(8,128)(2,1)}, u32[]{:S(2)}, u32[]{:S(2)}) collective-permute-start(bf16[128,4096]{1,0:T(8,128)(2,1)} %collective-permute-done.9.refs_0_.refs_11_), channel_id=1, source_target_pairs={{0,1},{1,0},{2,3},{3,2},{4,5},{5,4},{6,7},{7,6}} | collective-permute-start | bytes 3145736 | tf_op jit(solution)/shard_map/ppermute | solution.py:45
  241.3 30.0 %collective-permute-start.21 = (bf16[256,4096]{1,0:T(8,128)(2,1)}, bf16[256,4096]{1,0:T(8,128)(2,1)}, u32[]{:S(2)}, u32[]{:S(2)}) collective-permute-start(bf16[256,4096]{1,0:T(8,128)(2,1)} %get-tuple-element.131.refs_0_), channel_id=1, source_target_pairs={{0,1},{1,0},{2,3},{3,2},{4,5},{5,4},{6,7},{7,6}} | collective-permute-start | bytes 6291464 | tf_op jit(solution)/shard_map/ppermute | solution.py:45
  242.8 28.5 %collective-permute-start.23 = (bf16[256,4096]{1,0:T(8,128)(2,1)}, bf16[256,4096]{1,0:T(8,128)(2,1)}, u32[]{:S(2)}, u32[]{:S(2)}) collective-permute-start(bf16[256,4096]{1,0:T(8,128)(2,1)} %get-tuple-element.133.refs_2_), channel_id=1, source_target_pairs={{0,1},{1,0},{2,3},{3,2},{4,5},{5,4},{6,7},{7,6}} | collective-permute-start | bytes 6291464 | tf_op jit(solution)/shard_map/ppermute | solution.py:45
  244.3 47.9 %collective-permute-start.27 = (f32[256,2048]{1,0:T(8,128)}, f32[256,2048]{1,0:T(8,128)}, u32[]{:S(2)}, u32[]{:S(2)}) collective-permute-start(f32[256,2048]{1,0:T(8,128)} %get-tuple-element.113.refs_3_), channel_id=1, source_target_pairs={{0,2},{1,5},{2,0},{3,7},{4,6},{5,1},{6,4},{7,3}} | collective-permute-start | bytes 6291464 | tf_op jit(solution)/shard_map/ppermute | solution.py:49
  246.3 46.3 %collective-permute-start.28 = (f32[256,2048]{1,0:T(8,128)}, f32[256,2048]{1,0:T(8,128)}, u32[]{:S(2)}, u32[]{:S(2)}) collective-permute-start(f32[256,2048]{1,0:T(8,128)} %get-tuple-element.140), channel_id=1, source_target_pairs={{0,4},{1,3},{2,6},{3,1},{4,0},{5,7},{6,2},{7,5}} | collective-permute-start | bytes 6291464 | tf_op jit(solution)/shard_map/ppermute | solution.py:49
  271.3 70.6 %collective-permute-start.12 = (bf16[512,1792]{1,0:T(8,128)(2,1)}, bf16[512,1792]{1,0:T(8,128)(2,1)}, u32[]{:S(2)}, u32[]{:S(2)}) collective-permute-start(bf16[512,1792]{1,0:T(8,128)(2,1)} %get-tuple-element.117.refs_1_), channel_id=1, source_target_pairs={{0,1},{1,0},{2,3},{3,2},{4,5},{5,4},{6,7},{7,6}} | collective-permute-start | bytes 5505032 | tf_op jit(solution)/shard_map/ppermute | solution.py:45
  271.3 71.0 %collective-permute-start.14 = (bf16[256,4096]{1,0:T(8,128)(2,1)}, bf16[256,4096]{1,0:T(8,128)(2,1)}, u32[]{:S(2)}, u32[]{:S(2)}) collective-permute-start(bf16[256,4096]{1,0:T(8,128)(2,1)} %dy_ref.1), channel_id=1, source_target_pairs={{0,1},{1,0},{2,3},{3,2},{4,5},{5,4},{6,7},{7,6}} | collective-permute-start | bytes 6291464 | tf_op jit(solution)/shard_map/ppermute | solution.py:45
  292.3 49.3 %collective-permute-start.20 = (bf16[128,4096]{1,0:T(8,128)(2,1)}, bf16[128,4096]{1,0:T(8,128)(2,1)}, u32[]{:S(2)}, u32[]{:S(2)}) collective-permute-start(bf16[128,4096]{1,0:T(8,128)(2,1)} %collective-permute-done.10.refs_1_.refs_12_), channel_id=1, source_target_pairs={{0,1},{1,0},{2,3},{3,2},{4,5},{5,4},{6,7},{7,6}} | collective-permute-start | bytes 3145736 | tf_op jit(solution)/shard_map/ppermute | solution.py:45
  292.6 51.4 %collective-permute-start.31 = (f32[256,2048]{1,0:T(8,128)}, f32[256,2048]{1,0:T(8,128)}, u32[]{:S(2)}, u32[]{:S(2)}) collective-permute-start(f32[256,2048]{1,0:T(8,128)} %get-tuple-element.137.refs_12_), channel_id=1, source_target_pairs={{0,2},{1,5},{2,0},{3,7},{4,6},{5,1},{6,4},{7,3}} | collective-permute-start | bytes 6291464 | tf_op jit(solution)/shard_map/ppermute | solution.py:49
  294.7 49.6 %collective-permute-start.32 = (f32[256,2048]{1,0:T(8,128)}, f32[256,2048]{1,0:T(8,128)}, u32[]{:S(2)}, u32[]{:S(2)}) collective-permute-start(f32[256,2048]{1,0:T(8,128)} %get-tuple-element.149), channel_id=1, source_target_pairs={{0,4},{1,3},{2,6},{3,1},{4,0},{5,7},{6,2},{7,5}} | collective-permute-start | bytes 6291464 | tf_op jit(solution)/shard_map/ppermute | solution.py:49
  341.6 56.3 %collective-permute-start.33 = (f32[256,2048]{1,0:T(8,128)}, f32[256,2048]{1,0:T(8,128)}, u32[]{:S(2)}, u32[]{:S(2)}) collective-permute-start(f32[256,2048]{1,0:T(8,128)} %get-tuple-element.105.refs_4_), channel_id=1, source_target_pairs={{0,2},{1,5},{2,0},{3,7},{4,6},{5,1},{6,4},{7,3}} | collective-permute-start | bytes 6291464 | tf_op jit(solution)/shard_map/ppermute | solution.py:49
  341.9 54.5 %collective-permute-start.30 = (f32[256,2048]{1,0:T(8,128)}, f32[256,2048]{1,0:T(8,128)}, u32[]{:S(2)}, u32[]{:S(2)}) collective-permute-start(f32[256,2048]{1,0:T(8,128)} %get-tuple-element.146), channel_id=1, source_target_pairs={{0,4},{1,3},{2,6},{3,1},{4,0},{5,7},{6,2},{7,5}} | collective-permute-start | bytes 6291464 | tf_op jit(solution)/shard_map/ppermute | solution.py:49
  342.3 93.3 %collective-permute-start.35 = (f32[256,2048]{1,0:T(8,128)}, f32[256,2048]{1,0:T(8,128)}, u32[]{:S(2)}, u32[]{:S(2)}) collective-permute-start(f32[256,2048]{1,0:T(8,128)} %get-tuple-element.154), channel_id=1, source_target_pairs={{0,4},{1,3},{2,6},{3,1},{4,0},{5,7},{6,2},{7,5}} | collective-permute-start | bytes 6291464 | tf_op jit(solution)/shard_map/ppermute | solution.py:49
  343.9 126.9 %collective-permute-start.34 = (f32[256,2048]{1,0:T(8,128)}, f32[256,2048]{1,0:T(8,128)}, u32[]{:S(2)}, u32[]{:S(2)}) collective-permute-start(f32[256,2048]{1,0:T(8,128)} %get-tuple-element.141.refs_20_), channel_id=1, source_target_pairs={{0,4},{1,3},{2,6},{3,1},{4,0},{5,7},{6,2},{7,5}} | collective-permute-start | bytes 6291464 | tf_op jit(solution)/shard_map/ppermute | solution.py:49
  344.3 143.6 %collective-permute-start.36 = (f32[256,2048]{1,0:T(8,128)}, f32[256,2048]{1,0:T(8,128)}, u32[]{:S(2)}, u32[]{:S(2)}) collective-permute-start(f32[256,2048]{1,0:T(8,128)} %get-tuple-element.142.refs_21_), channel_id=1, source_target_pairs={{0,2},{1,5},{2,0},{3,7},{4,6},{5,1},{6,4},{7,3}} | collective-permute-start | bytes 6291464 | tf_op jit(solution)/shard_map/ppermute | solution.py:49
  396.4 106.5 %collective-permute-start.45 = (f32[160,2048]{1,0:T(8,128)}, f32[160,2048]{1,0:T(8,128)}, u32[]{:S(2)}, u32[]{:S(2)}) collective-permute-start(f32[160,2048]{1,0:T(8,128)} %get-tuple-element.161), channel_id=1, source_target_pairs={{0,4},{1,3},{2,6},{3,1},{4,0},{5,7},{6,2},{7,5}} | collective-permute-start | bytes 3932168 | tf_op jit(solution)/shard_map/ppermute | solution.py:49
  397.8 106.1 %collective-permute-start.46 = (f32[160,2048]{1,0:T(8,128)}, f32[160,2048]{1,0:T(8,128)}, u32[]{:S(2)}, u32[]{:S(2)}) collective-permute-start(f32[160,2048]{1,0:T(8,128)} %get-tuple-element.162), channel_id=1, source_target_pairs={{0,2},{1,5},{2,0},{3,7},{4,6},{5,1},{6,4},{7,3}} | collective-permute-start | bytes 3932168 | tf_op jit(solution)/shard_map/ppermute | solution.py:49
  435.7 63.5 %collective-permute-start.43 = (f32[64,2048]{1,0:T(8,128)}, f32[64,2048]{1,0:T(8,128)}, u32[]{:S(2)}, u32[]{:S(2)}) collective-permute-start(f32[64,2048]{1,0:T(8,128)} %get-tuple-element.159), channel_id=1, source_target_pairs={{0,4},{1,3},{2,6},{3,1},{4,0},{5,7},{6,2},{7,5}} | collective-permute-start | bytes 1572872 | tf_op jit(solution)/shard_map/ppermute | solution.py:49
  470.8 30.9 %collective-permute-start.44 = (f32[64,2048]{1,0:T(8,128)}, f32[64,2048]{1,0:T(8,128)}, u32[]{:S(2)}, u32[]{:S(2)}) collective-permute-start(f32[64,2048]{1,0:T(8,128)} %get-tuple-element.160), channel_id=1, source_target_pairs={{0,2},{1,5},{2,0},{3,7},{4,6},{5,1},{6,4},{7,3}} | collective-permute-start | bytes 1572872 | tf_op jit(solution)/shard_map/ppermute | solution.py:49
  497.9 2.3 collective-permute-start.39
  499.1 11.9 %collective-permute-start.37 = (f32[32,2048]{1,0:T(8,128)}, f32[32,2048]{1,0:T(8,128)}, u32[]{:S(2)}, u32[]{:S(2)}) collective-permute-start(f32[32,2048]{1,0:T(8,128)} %get-tuple-element.156), channel_id=1, source_target_pairs={{0,4},{1,3},{2,6},{3,1},{4,0},{5,7},{6,2},{7,5}} | collective-permute-start | bytes 786440 | tf_op jit(solution)/shard_map/ppermute | solution.py:49
  500.2 10.8 %collective-permute-start.38 = (f32[32,2048]{1,0:T(8,128)}, f32[32,2048]{1,0:T(8,128)}, u32[]{:S(2)}, u32[]{:S(2)}) collective-permute-start(f32[32,2048]{1,0:T(8,128)} %get-tuple-element.157), channel_id=1, source_target_pairs={{0,2},{1,5},{2,0},{3,7},{4,6},{5,1},{6,4},{7,3}} | collective-permute-start | bytes 786440 | tf_op jit(solution)/shard_map/ppermute | solution.py:49
  501.7 7.0 %copy-start = (f32[1,4096]{1,0:T(1,128)}, f32[1,4096]{1,0:T(1,128)S(1)}, u32[]{:S(2)}) copy-start(f32[1,4096]{1,0:T(1,128)S(1)} %add.3.refs_3_) | copy-start | bytes 49156
  501.7 9.2 %collective-permute-start.40 = (f32[1,4096]{1,0:T(1,128)S(1)}, f32[1,4096]{1,0:T(1,128)S(1)}, u32[]{:S(2)}, u32[]{:S(2)}) collective-permute-start(f32[1,4096]{1,0:T(1,128)S(1)} %add.3.refs_3_), channel_id=1, source_target_pairs={{0,2},{1,3},{2,0},{3,1},{4,6},{5,7},{6,4},{7,5}} | collective-permute-start | bytes 49160 | tf_op jit(solution)/shard_map/ppermute | solution.py:45
  503.0 8.0 %collective-permute-start.41 = (f32[1,4096]{1,0:T(1,128)S(1)}, f32[1,4096]{1,0:T(1,128)}, u32[]{:S(2)}, u32[]{:S(2)}) collective-permute-start(f32[1,4096]{1,0:T(1,128)S(1)} %add.3.refs_3_), channel_id=1, source_target_pairs={{0,4},{1,5},{2,6},{3,7},{4,0},{5,1},{6,2},{7,3}} | collective-permute-start | bytes 49160 | tf_op jit(solution)/shard_map/ppermute | solution.py:45
  504.0 7.0 %collective-permute-start.42 = (f32[1,4096]{1,0:T(1,128)S(1)}, f32[1,4096]{1,0:T(1,128)}, u32[]{:S(2)}, u32[]{:S(2)}) collective-permute-start(f32[1,4096]{1,0:T(1,128)S(1)} %add.3.refs_3_), channel_id=1, source_target_pairs={{0,6},{1,7},{2,4},{3,5},{4,2},{5,3},{6,0},{7,1}} | collective-permute-start | bytes 49160 | tf_op jit(solution)/shard_map/ppermute | solution.py:45
  511.0 0.6 copy-start.1
